TPU v7x, 768 devices: a whole 4x8x12 slice. The times are simulated.
768 devices in a mesh: dp: 32 (over z_hi, y, core), tensor: 24 (over z_lo, x).
Axes of the slice: x: 4, y: 8, z: 12 (z_hi: 2, z_lo: 6; z = z_hi * 6 + z_lo), core: 2. Of those that a mesh axis runs over, the one named last changes fastest.
Arguments:
- tokens: bfloat16 [1024, 6144], P('dp', 'tensor'), may hold values from -6 to 6
- router_weight: bfloat16 [6144, 8], P('tensor'), may hold values from -0.078125 to 0.078125
- expert_ids: int32 [1024, 2], P('dp'), may hold values from 0 to 7, all different within a row; in each aligned block of 32 rows (0 to 31, 32 to 63, ...) at most 12 rows name the same one
- w_gate: bfloat16 [32, 6144, 3072], P('dp', None, 'tensor'), may hold values from -0.078125 to 0.078125
- w_up: bfloat16 [32, 6144, 3072], P('dp', None, 'tensor'), may hold values from -0.078125 to 0.078125
- w_down: bfloat16 [32, 3072, 6144], P('dp', 'tensor'), may hold values from -0.0546875 to 0.0546875
Outputs:
- moe_out: bfloat16 [1024, 6144], P('dp', 'tensor')
Inputs may be any that keep to these rules, and one draw needn't show every extreme that they name: `expert_ids`: the two experts of a token differ. In each aligned block of 32 rows (the rows of one index of dp) no expert is named by more than 12 rows, a bound that some blocks reach.
All inputs are finite; a program needn't handle non-finite values.
Results may differ from a plain program's by a relative error of at most 0.022.
Values may be sent and summed in bfloat16 or wider, within the bound.
No kernel may reach another device: no remote copies, remote signals or barrier semaphores. Data moves between devices by JAX's collectives and lax.ppermute only.
A program may use at most 32 MiB of HBM per device.

v0:
```python
import jax
import jax.numpy as jnp
from jax import lax
from jax.experimental import pallas as pl
from jax.experimental.pallas import tpu as pltpu
from jax.sharding import Mesh
from jax.sharding import PartitionSpec as P


CAP = 12
LANES = 128
CHUNK = 2 * CAP
FAR = ("zh", "yq", "yp", "z")
f32, bf16 = jnp.float32, jnp.bfloat16


def call(body, out_shape, flops, nbytes, **kw):
    return pl.pallas_call(
        body,
        out_shape=out_shape,
        cost_estimate=pl.CostEstimate(flops=flops, bytes_accessed=nbytes, transcendentals=0),
        **kw,
    )


def slot_matrices(ids, experts):
    tok = ids.shape[1]
    which = lax.broadcasted_iota(jnp.int32, (experts, tok), 0)
    chosen = [(which == ids[k : k + 1, :]).astype(f32) for k in range(2)]
    earlier = (
        lax.broadcasted_iota(jnp.int32, (tok, tok), 0) < lax.broadcasted_iota(jnp.int32, (tok, tok), 1)
    ).astype(f32)
    counts = jnp.dot(chosen[0] + chosen[1], earlier, preferred_element_type=f32)
    rows = experts * CHUNK
    flat = lax.broadcasted_iota(jnp.int32, (rows, tok), 0)
    expert = jnp.zeros((rows, tok), jnp.int32)
    for e in range(1, experts):
        expert = expert + (flat >= e * CHUNK).astype(jnp.int32)
    row = flat - expert * CHUNK
    slot = jnp.where(row < 12, row, jnp.where(row < 16, row - 4, row - 16))
    place = expert * CAP + slot
    matrices = []
    for k in range(2):
        rank = jnp.sum(chosen[k] * counts, axis=0, keepdims=True)
        position = ids[k : k + 1, :] * CAP + (rank + 0.5).astype(jnp.int32)
        matrices.append((place == position).astype(f32))
    return chosen, matrices, row < 12


def pack_kernel(ids_ref, tokens_ref, router_ref, out_ref, logits_ref):
    experts, copies = out_ref.shape[0], out_ref.shape[1]
    tok = tokens_ref.shape[0]
    _, (first, second), low = slot_matrices(ids_ref[...], experts)
    placing = first + second
    zero = jnp.zeros_like(placing)
    tokens = tokens_ref[...]
    packed = jnp.dot(
        jnp.where(low, placing, zero).astype(bf16), tokens[:, :LANES], preferred_element_type=f32
    ) + jnp.dot(jnp.where(low, zero, placing).astype(bf16), tokens[:, LANES:], preferred_element_type=f32)
    packed = packed.reshape(experts, CHUNK, LANES).astype(bf16)
    for n in range(copies):
        out_ref[:, n] = packed
    logits = lax.dot_general(router_ref[...], tokens, (((1,), (1,)), ((), ())), preferred_element_type=f32)
    each = LANES // tok
    lines = [jnp.concatenate([logits[i + k : i + k + 1] for k in range(each)], axis=1) for i in range(0, experts, each)]
    lines = jnp.concatenate(lines, axis=0)
    for n in range(logits_ref.shape[0]):
        logits_ref[n] = lines


def spread_kernel(in_ref, lo_ref, hi_ref):
    sources, zs = in_ref.shape[0], in_ref.shape[1]
    top = lax.broadcasted_iota(jnp.int32, (8, LANES), 0) < 4
    for z in range(zs):
        ref, at = (lo_ref, z) if z < zs // 2 else (hi_ref, z - zs // 2)
        for p in range(sources // 2):
            a = in_ref[2 * p, z].astype(f32)
            b = in_ref[2 * p + 1, z].astype(f32)
            ac, bc = a[8:16], b[8:16]
            left = jnp.concatenate([a[0:8], jnp.where(top, ac, pltpu.roll(bc, 4, 0)), b[0:8]], axis=0)
            right = jnp.concatenate([a[16:24], jnp.where(top, pltpu.roll(ac, 4, 0), bc), b[16:24]], axis=0)
            ref[at, CHUNK * p : CHUNK * (p + 1), :LANES] = left.astype(bf16)
            ref[at, CHUNK * p : CHUNK * (p + 1), LANES:] = right.astype(bf16)


def unspread_kernel(*refs):
    ins, out_ref = refs[:-1], refs[-1]
    sources, zs = out_ref.shape[0], out_ref.shape[1]
    top = lax.broadcasted_iota(jnp.int32, (8, LANES), 0) < 4
    for z in range(zs):
        half, at = (0, z) if z < zs // 2 else (1, z - zs // 2)
        for p in range(sources // 2):
            total = None
            for n in range(len(ins) // 2):
                term = ins[2 * n + half][at, CHUNK * p : CHUNK * (p + 1), :].astype(f32)
                total = term if total is None else total + term
            y, w = total[:, :LANES], total[:, LANES:]
            yc, wc = y[8:16], w[8:16]
            a = jnp.concatenate([y[0:8], jnp.where(top, yc, pltpu.roll(wc, 4, 0)), w[0:8]], axis=0)
            b = jnp.concatenate([y[16:24], jnp.where(top, pltpu.roll(yc, 4, 0), wc), w[16:24]], axis=0)
            out_ref[2 * p, z] = a.astype(bf16)
            out_ref[2 * p + 1, z] = b.astype(bf16)


def products(lo_ref, hi_ref, weights, total):
    half = lo_ref.shape[0]
    for z in range(2 * half):
        rows = lo_ref[z] if z < half else hi_ref[z - half]
        both = jnp.concatenate([w[z, 0] for w in weights], axis=1)
        term = jnp.dot(rows, both, preferred_element_type=f32)
        total = term if total is None else total + term
    return total


def gate_up_kernel(more, xi_ref, *refs):
    lo_ref, hi_ref, *weights = refs[:6]
    total = refs[6][...] if more else None
    refs[-1][...] = products(lo_ref, hi_ref, weights, total)


def down(hidden, own_ref, other_ref, column, z, xs):
    at = pl.ds(pl.multiple_of((z * xs + column) * 256, 256), 256)
    both = jnp.concatenate([own_ref[:, at], other_ref[:, at]], axis=0)
    return jnp.dot(hidden, both, preferred_element_type=f32).astype(bf16)


def turn_kernel(xs, xi_ref, *refs):
    lo_ref, hi_ref, *weights = refs[:6]
    total_ref, own_ref, other_ref, hidden_ref, out_lo, out_hi = refs[6:]
    total = products(lo_ref, hi_ref, weights, total_ref[...])
    units = total.shape[1] // 2
    gate, up = total[:, :units], total[:, units:]
    hidden = (jax.nn.silu(gate) * up).astype(bf16)
    hidden_ref[...] = hidden
    half = lo_ref.shape[0]
    for z in range(2 * half):
        value = down(hidden, own_ref, other_ref, xi_ref[0], z, xs)
        if z < half:
            out_lo[z] = value
        else:
            out_hi[z - half] = value


def down_kernel(xs, first_ref, second_ref, third_ref, hidden_ref, own_ref, other_ref, *outs):
    hidden = hidden_ref[...]
    half = outs[0].shape[0]
    for n in range(len(outs) // 2):
        for z in range(2 * half):
            value = down(hidden, own_ref, other_ref, (first_ref, second_ref, third_ref)[n][0], z, xs)
            if z < half:
                outs[2 * n][z] = value
            else:
                outs[2 * n + 1][z - half] = value


def merge_kernel(ids_ref, logits_ref, in_ref, out_ref):
    experts, copies = in_ref.shape[0], in_ref.shape[1]
    tok = ids_ref.shape[1]
    chosen, (first, second), low = slot_matrices(ids_ref[...], experts)
    logits = logits_ref[0]
    for n in range(1, logits_ref.shape[0]):
        logits = logits + logits_ref[n]
    logits = jnp.concatenate(
        [logits[i : i + 1, k : k + tok] for i in range(logits.shape[0]) for k in range(0, LANES, tok)], axis=0
    )
    a = jnp.sum(chosen[0] * logits, axis=0, keepdims=True)
    b = jnp.sum(chosen[1] * logits, axis=0, keepdims=True)
    gate = jax.nn.sigmoid(a - b)
    weights = first * gate + second * (1.0 - gate)
    merged = in_ref[:, 0].astype(f32)
    for n in range(1, copies):
        merged = merged + in_ref[:, n].astype(f32)
    merged = merged.reshape(experts * CHUNK, LANES)
    zero = jnp.zeros_like(weights)
    for h in range(2):
        part = jnp.where(low, weights, zero) if h == 0 else jnp.where(low, zero, weights)
        value = lax.dot_general(
            part, merged, (((0,), (0,)), ((), ())), precision=lax.Precision.HIGHEST, preferred_element_type=f32
        )
        out_ref[:, h * LANES : (h + 1) * LANES] = value.astype(bf16)


def block(tokens, router_weight, expert_ids, w_gate, w_up, w_down):
    tok, share = tokens.shape
    xs, zs = lax.axis_size("x"), lax.axis_size("z")
    experts = lax.axis_size(("zh", "yq"))
    sources = experts * 2
    far = sources * zs
    rows = sources * CAP
    half = zs // 2
    assert xs == 4 and share == 256 and zs % 2 == 0
    units = w_gate.shape[2]
    ids = expert_ids.T
    me = lax.axis_index("x")
    near = [((me + k) & (xs - 1)).astype(jnp.int32).reshape(1) for k in (0, 1, 3, 2)]
    forward = [(i, (i + 1) % xs) for i in range(xs)]
    backward = [(i, (i - 1) % xs) for i in range(xs)]

    def ahead(v):
        return lax.ppermute(v, "x", forward)

    def behind(v):
        return lax.ppermute(v, "x", backward)

    messages, logits = call(
        pack_kernel,
        (
            jax.ShapeDtypeStruct((experts, 2 * zs, CHUNK, LANES), bf16),
            jax.ShapeDtypeStruct((zs * xs, experts * tok // LANES, LANES), f32),
        ),
        10**7,
        10**6,
        name="pack",
    )(ids, tokens, router_weight.T)
    partial_logits = lax.all_to_all(logits, ("z", "x"), 0, 0, tiled=True)
    arrived = lax.all_to_all(messages.reshape(far, CHUNK, LANES), FAR, 0, 0, tiled=True)

    part_shape = jax.ShapeDtypeStruct((half, rows, share), bf16)
    own_lo, own_hi = call(spread_kernel, (part_shape, part_shape), 10**6, 2 * far * CHUNK * LANES * 2, name="spread")(
        arrived.reshape(sources, zs, CHUNK, LANES)
    )

    left_hi = ahead(own_hi)
    right_lo = behind(own_lo)
    left_lo = ahead(own_lo)
    right_hi = behind(own_hi)
    swap = [(0, 1), (1, 0)]
    gate_w, up_w, down_w, _ = lax.optimization_barrier((w_gate[0], w_up[0], w_down[0], own_lo))
    gate_o = lax.ppermute(gate_w, "c", swap)
    up_o = lax.ppermute(up_w, "c", swap)
    down_o = lax.ppermute(down_w, "c", swap)
    far_hi = ahead(left_hi)
    far_lo = behind(right_lo)

    stacked = [v.reshape(zs, xs, share, units) for v in (gate_w, gate_o, up_w, up_o)]
    weight_spec = pl.BlockSpec((zs, 1, share, units), lambda g, xi: (0, xi[0], 0, 0))

    def whole(*shape):
        return pl.BlockSpec(shape, lambda g, *xi: (0,) * len(shape))

    part = whole(half, rows, share)
    sums = jax.ShapeDtypeStruct((rows, 4 * units), f32)
    sums_spec = whole(rows, 4 * units)
    flops = 2 * rows * zs * share * 4 * units
    nbytes = zs * share * units * 8 + 2 * half * rows * share * 2

    def gate_up(total, column, lo, hi):
        more = total is not None
        return call(
            lambda *refs: gate_up_kernel(more, *refs),
            sums,
            flops,
            nbytes,
            grid_spec=pltpu.PrefetchScalarGridSpec(
                num_scalar_prefetch=1,
                grid=(1,),
                in_specs=[part, part] + [weight_spec] * 4 + [sums_spec] * more,
                out_specs=sums_spec,
            ),
            name="gate_up",
        )(near[column], lo, hi, *stacked, *([total] if more else []))

    total = gate_up(None, 0, own_lo, own_hi)
    total = gate_up(total, 1, right_lo, right_hi)
    total = gate_up(total, 2, left_lo, left_hi)
    down_spec = whole(units, zs * xs * share)
    hidden_spec = whole(rows, 2 * units)
    hidden, opp_lo, opp_hi = call(
        lambda *refs: turn_kernel(xs, *refs),
        (jax.ShapeDtypeStruct((rows, 2 * units), bf16), part_shape, part_shape),
        2 * flops,
        2 * nbytes,
        grid_spec=pltpu.PrefetchScalarGridSpec(
            num_scalar_prefetch=1,
            grid=(1,),
            in_specs=[part, part] + [weight_spec] * 4 + [sums_spec, down_spec, down_spec],
            out_specs=(hidden_spec, part, part),
        ),
        name="turn",
    )(near[3], far_lo, far_hi, *stacked, total, down_w, down_o)

    from_left_lo = ahead(opp_lo)
    from_right_hi = behind(opp_hi)
    outs = call(
        lambda *refs: down_kernel(xs, *refs),
        (part_shape,) * 6,
        2 * flops,
        2 * nbytes,
        grid_spec=pltpu.PrefetchScalarGridSpec(
            num_scalar_prefetch=3,
            grid=(1,),
            in_specs=[hidden_spec, down_spec, down_spec],
            out_specs=(part,) * 6,
        ),
        name="down",
    )(near[1], near[2], near[0], hidden, down_w, down_o)
    next_lo, next_hi, prev_lo, prev_hi, mine_lo, mine_hi = outs
    c_hi = ahead(next_hi)
    e_lo = behind(prev_lo)
    c_lo = ahead((next_lo.astype(f32) + from_left_lo.astype(f32)).astype(bf16))
    e_hi = behind((prev_hi.astype(f32) + from_right_hi.astype(f32)).astype(bf16))

    leaving = call(
        unspread_kernel,
        jax.ShapeDtypeStruct((sources, zs, CHUNK, LANES), bf16),
        10**7,
        4 * far * CHUNK * LANES * 2,
        name="unspread",
    )(mine_lo, mine_hi, c_lo, c_hi, e_lo, e_hi)
    back = lax.all_to_all(leaving.reshape(far, CHUNK, LANES), FAR, 0, 0, tiled=True)
    return call(
        merge_kernel,
        jax.ShapeDtypeStruct((tok, share), bf16),
        10**7,
        10**6,
        name="merge",
    )(ids, partial_logits, back.reshape(experts, 2 * zs, CHUNK, LANES))


def solution(mesh):
    finer = Mesh(mesh.devices.reshape(2, 4, 2, 2, 6, 4), ("zh", "yq", "yp", "c", "z", "x"))
    dp, tensor = ("zh", "yq", "yp", "c"), ("z", "x")
    return jax.shard_map(
        block,
        mesh=finer,
        in_specs=(
            P(dp, tensor),
            P(tensor, None),
            P(dp, None),
            P(dp, None, tensor),
            P(dp, None, tensor),
            P(dp, tensor, None),
        ),
        out_specs=P(dp, tensor),
        check_vma=False,
    )
```

profile of v0, /device:TPU:8, one launch (start us, length us, event | category | flops | bytes accessed | tf_op | source)
XLA Modules:
  0.0 178.1 jit_solution(13306538467928365337)
XLA Ops:
  0.0 2.0 %pack.1 = (bf16[8,12,24,128]{3,2,1,0:T(8,128)(2,1)}, f32[24,2,128]{2,1,0:T(2,128)}) custom-call(s32[2,32]{1,0:T(2,128)} %bitcast.38, bf16[32,256]{1,0:T(8,128)(2,1)} %tokens_ref.1, bf16[8,256]{1,0:T(8,128)(2,1)} %bitcast.40), custom_call_target="tpu_custom_call" | custom-call | flops 10000000 | bytes 1000000 | tf_op jit(solution)/shard_map/pack/pallas_call | solution.py:205
  2.0 51.4 %all_to_all.15 = bf16[96,24,128]{2,1,0:T(8,128)(2,1)} all-to-all(bf16[96,24,128]{2,1,0:T(8,128)(2,1)} %bitcast.37), channel_id=1, replica_groups=mesh['zh'=2,'yq'=4,'yp'=2,'c'=2,'z'=6,'x'=4] {'zh','yq','yp','z'}, dimensions={0} | all-to-all | bytes 1179648 | tf_op jit(solution)/shard_map/all_to_all | solution.py:216
  53.4 2.0 %spread.1 = (bf16[3,192,256]{2,1,0:T(8,128)(2,1)}, bf16[3,192,256]{2,1,0:T(8,128)(2,1)}) custom-call(bf16[16,6,24,128]{3,2,1,0:T(8,128)(2,1)} %bitcast.34), custom_call_target="tpu_custom_call" | custom-call | flops 1000000 | bytes 1179648 | tf_op jit(solution)/shard_map/spread/pallas_call | solution.py:219
  55.5 1.9 %collective-permute-start.4 = (bf16[6144,128]{1,0:T(8,128)(2,1)S(1)}, bf16[6144,128]{1,0:T(8,128)(2,1)S(1)}, u32[]{:S(2)}, u32[]{:S(2)}) collective-permute-start(bf16[6144,128]{1,0:T(8,128)(2,1)S(1)} %bitcast.21), channel_id=1, source_target_pairs={{0,24},{24,0},{1,25},{25,1},{2,26},{26,2},{3,27},{27,3},{4,28},{28... | collective-permute-start | bytes 4718600 | tf_op jit(solution)/shard_map/ppermute | solution.py:229
  57.4 2.4 %collective-permute-start.5 = (bf16[6144,128]{1,0:T(8,128)(2,1)}, bf16[6144,128]{1,0:T(8,128)(2,1)}, u32[]{:S(2)}, u32[]{:S(2)}) collective-permute-start(bf16[6144,128]{1,0:T(8,128)(2,1)} %bitcast.22), channel_id=1, source_target_pairs={{0,24},{24,0},{1,25},{25,1},{2,26},{26,2},{3,27},{27,3},{4,28},{28... | collective-permute-start | bytes 4718600 | tf_op jit(solution)/shard_map/ppermute | solution.py:230
  59.8 1.9 %collective-permute-start.8 = (bf16[128,6144]{1,0:T(8,128)(2,1)}, bf16[128,6144]{1,0:T(8,128)(2,1)}, u32[]{:S(2)}, u32[]{:S(2)}) collective-permute-start(bf16[128,6144]{1,0:T(8,128)(2,1)} %bitcast.31), channel_id=1, source_target_pairs={{0,24},{24,0},{1,25},{25,1},{2,26},{26,2},{3,27},{27,3},{4,28},{28... | collective-permute-start | bytes 4718600 | tf_op jit(solution)/shard_map/ppermute | solution.py:231
  61.7 3.4 %collective-permute-start.2 = (bf16[3,192,256]{2,1,0:T(8,128)(2,1)}, bf16[3,192,256]{2,1,0:T(8,128)(2,1)S(1)}, u32[]{:S(2)}, u32[]{:S(2)}) collective-permute-start(bf16[3,192,256]{2,1,0:T(8,128)(2,1)} %get-tuple-element.24.refs_2_), channel_id=1, source_target_pairs={{0,1},{1,2},{2,3},{3,0},{4,5},{5,6},{6,7},{7,4},{8,9},{9,10},{10,1... | collective-permute-start | bytes 884744 | tf_op jit(solution)/shard_map/ppermute | solution.py:200
  65.1 3.7 %collective-permute-start = (bf16[3,192,256]{2,1,0:T(8,128)(2,1)}, bf16[3,192,256]{2,1,0:T(8,128)(2,1)}, u32[]{:S(2)}, u32[]{:S(2)}) collective-permute-start(bf16[3,192,256]{2,1,0:T(8,128)(2,1)} %get-tuple-element.23.refs_1_), channel_id=1, source_target_pairs={{0,3},{1,0},{2,1},{3,2},{4,7},{5,4},{6,5},{7,6},{8,11},{9,8},{10,9... | collective-permute-start | bytes 884744 | tf_op jit(solution)/shard_map/ppermute | solution.py:203
  68.8 5.7 %collective-permute-done.2.refs_2_ = bf16[3,192,256]{2,1,0:T(8,128)(2,1)S(1)} collective-permute-done((bf16[3,192,256]{2,1,0:T(8,128)(2,1)}, bf16[3,192,256]{2,1,0:T(8,128)(2,1)S(1)}, u32[]{:S(2)}, u32[]{:S(2)}) %collective-permute-start.2) | collective-permute-done | bytes 294944 | tf_op jit(solution)/shard_map/ppermute | solution.py:200
  74.5 3.4 %collective-permute-start.7 = (bf16[3,192,256]{2,1,0:T(8,128)(2,1)}, bf16[3,192,256]{2,1,0:T(8,128)(2,1)}, u32[]{:S(2)}, u32[]{:S(2)}) collective-permute-start(bf16[3,192,256]{2,1,0:T(8,128)(2,1)} %get-tuple-element.24.refs_2_), channel_id=1, source_target_pairs={{0,3},{1,0},{2,1},{3,2},{4,7},{5,4},{6,5},{7,6},{8,11},{9,8},{10,9... | collective-permute-start | bytes 884744 | tf_op jit(solution)/shard_map/ppermute | solution.py:203
  77.9 2.4 %collective-permute-start.6 = (bf16[3,192,256]{2,1,0:T(8,128)(2,1)}, bf16[3,192,256]{2,1,0:T(8,128)(2,1)}, u32[]{:S(2)}, u32[]{:S(2)}) collective-permute-start(bf16[3,192,256]{2,1,0:T(8,128)(2,1)} %get-tuple-element.23.refs_1_), channel_id=1, source_target_pairs={{0,1},{1,2},{2,3},{3,0},{4,5},{5,6},{6,7},{7,4},{8,9},{9,10},{10,1... | collective-permute-start | bytes 884744 | tf_op jit(solution)/shard_map/ppermute | solution.py:200
  80.3 2.7 %collective-permute-start.3 = (bf16[3,192,256]{2,1,0:T(8,128)(2,1)S(1)}, bf16[3,192,256]{2,1,0:T(8,128)(2,1)S(1)}, u32[]{:S(2)}, u32[]{:S(2)}) collective-permute-start(bf16[3,192,256]{2,1,0:T(8,128)(2,1)S(1)} %collective-permute-done.2.refs_2_), channel_id=1, source_target_pairs={{0,1},{1,2},{2,3},{3,0},{4,5},{5,6},{6,7},{7,4},{8,9},{9,10},{10,1... | collective-permute-start | bytes 884744 | tf_op jit(solution)/shard_map/ppermute | solution.py:200
  83.0 4.4 %collective-permute-start.1 = (bf16[3,192,256]{2,1,0:T(8,128)(2,1)}, bf16[3,192,256]{2,1,0:T(8,128)(2,1)S(1)}, u32[]{:S(2)}, u32[]{:S(2)}) collective-permute-start(bf16[3,192,256]{2,1,0:T(8,128)(2,1)} %collective-permute-done.refs_1_), channel_id=1, source_target_pairs={{0,3},{1,0},{2,1},{3,2},{4,7},{5,4},{6,5},{7,6},{8,11},{9,8},{10,9... | collective-permute-start | bytes 884744 | tf_op jit(solution)/shard_map/ppermute | solution.py:203
  87.4 2.8 %gate_up.3.refs_7_ = f32[192,512]{1,0:T(8,128)} custom-call(s32[1]{0:T(128)} %bitcast.4.refs_0_.refs_2_, bf16[3,192,256]{2,1,0:T(8,128)(2,1)} %get-tuple-element.23.refs_1_, bf16[3,192,256]{2,1,0:T(8,128)(2,1)} %get-tuple-element.24.refs_2_, bf16[6,4,256,128]{3,2,1,0:T(8,128)(2,1)} %bitcast.17, bf16[6,4,256,128]{3,2,1,0:T(8,128)(2,1)} %bitcast.27, ...), custom_call_target="tpu_custom_call" | custom-call | flops 301989888 | bytes 2162688 | tf_op jit(solution)/shard_map/gate_up/pallas_call | solution.py:249
  90.2 2.9 %gate_up.4.refs_7_ = f32[192,512]{1,0:T(8,128)} custom-call(s32[1]{0:T(128)} %bitcast.2.refs_0_, bf16[3,192,256]{2,1,0:T(8,128)(2,1)} %collective-permute-done.refs_1_, bf16[3,192,256]{2,1,0:T(8,128)(2,1)} %collective-permute-done.7.refs_2_, bf16[6,4,256,128]{3,2,1,0:T(8,128)(2,1)} %bitcast.18, bf16[6,4,256,128]{3,2,1,0:T(8,128)(2,1)} %bitcast.28, ...), custom_call_target="tpu_custom_call" | custom-call | flops 301989888 | bytes 2162688 | tf_op jit(solution)/shard_map/gate_up/pallas_call | solution.py:249
  93.1 2.9 %gate_up.5.refs_7_ = f32[192,512]{1,0:T(8,128)} custom-call(s32[1]{0:T(128)} %bitcast.3.refs_0_.refs_1_, bf16[3,192,256]{2,1,0:T(8,128)(2,1)} %collective-permute-done.6.refs_1_, bf16[3,192,256]{2,1,0:T(8,128)(2,1)} %copy-done.2, bf16[6,4,256,128]{3,2,1,0:T(8,128)(2,1)} %bitcast.19, bf16[6,4,256,128]{3,2,1,0:T(8,128)(2,1)} %bitcast.29, ...), custom_call_target="tpu_custom_call" | custom-call | flops 301989888 | bytes 2162688 | tf_op jit(solution)/shard_map/gate_up/pallas_call | solution.py:249
  96.0 0.7 copy-done.7
  96.8 4.2 %turn.1 = (bf16[192,256]{1,0:T(8,128)(2,1)}, bf16[3,192,256]{2,1,0:T(8,128)(2,1)}, bf16[3,192,256]{2,1,0:T(8,128)(2,1)}) custom-call(s32[1]{0:T(128)} %bitcast.5.refs_0_, bf16[3,192,256]{2,1,0:T(8,128)(2,1)} %copy-done.8, bf16[3,192,256]{2,1,0:T(8,128)(2,1)} %copy-done.7, bf16[6,4,256,128]{3,2,1,0:T(8,128)(2,1)} %bitcast.20, ...), custom_call_target="tpu_custom_call" | custom-call | flops 603979776 | bytes 4325376 | tf_op jit(solution)/shard_map/turn/pallas_call | solution.py:268
  101.0 1.9 %collective-permute-start.9 = (bf16[3,192,256]{2,1,0:T(8,128)(2,1)}, bf16[3,192,256]{2,1,0:T(8,128)(2,1)S(1)}, u32[]{:S(2)}, u32[]{:S(2)}) collective-permute-start(bf16[3,192,256]{2,1,0:T(8,128)(2,1)} %get-tuple-element.32), channel_id=1, source_target_pairs={{0,1},{1,2},{2,3},{3,0},{4,5},{5,6},{6,7},{7,4},{8,9},{9,10},{10,1... | collective-permute-start | bytes 884744 | tf_op jit(solution)/shard_map/ppermute | solution.py:200
  103.0 5.1 %collective-permute-start.13 = (bf16[3,192,256]{2,1,0:T(8,128)(2,1)}, bf16[3,192,256]{2,1,0:T(8,128)(2,1)S(1)}, u32[]{:S(2)}, u32[]{:S(2)}) collective-permute-start(bf16[3,192,256]{2,1,0:T(8,128)(2,1)} %get-tuple-element.36), channel_id=1, source_target_pairs={{0,3},{1,0},{2,1},{3,2},{4,7},{5,4},{6,5},{7,6},{8,11},{9,8},{10,9... | collective-permute-start | bytes 884744 | tf_op jit(solution)/shard_map/ppermute | solution.py:203
  108.1 3.5 %down.1 = (bf16[3,192,256]{2,1,0:T(8,128)(2,1)}, bf16[3,192,256]{2,1,0:T(8,128)(2,1)}, bf16[3,192,256]{2,1,0:T(8,128)(2,1)}, bf16[3,192,256]{2,1,0:T(8,128)(2,1)...) custom-call(s32[1]{0:T(128)} %bitcast.2.refs_0_, s32[1]{0:T(128)} %bitcast.3.refs_0_.refs_1_, ...), custom_call_target="tpu_custom_call" | custom-call | flops 603979776 | bytes 4325376 | tf_op jit(solution)/shard_map/down/pallas_call | solution.py:284
  111.6 1.9 %collective-permute-start.11 = (bf16[3,192,256]{2,1,0:T(8,128)(2,1)}, bf16[3,192,256]{2,1,0:T(8,128)(2,1)S(1)}, u32[]{:S(2)}, u32[]{:S(2)}) collective-permute-start(bf16[3,192,256]{2,1,0:T(8,128)(2,1)} %get-tuple-element.33), channel_id=1, source_target_pairs={{0,1},{1,2},{2,3},{3,0},{4,5},{5,6},{6,7},{7,4},{8,9},{9,10},{10,1... | collective-permute-start | bytes 884744 | tf_op jit(solution)/shard_map/ppermute | solution.py:200
  113.5 5.1 %collective-permute-start.12 = (bf16[3,192,256]{2,1,0:T(8,128)(2,1)}, bf16[3,192,256]{2,1,0:T(8,128)(2,1)S(1)}, u32[]{:S(2)}, u32[]{:S(2)}) collective-permute-start(bf16[3,192,256]{2,1,0:T(8,128)(2,1)} %get-tuple-element.34), channel_id=1, source_target_pairs={{0,3},{1,0},{2,1},{3,2},{4,7},{5,4},{6,5},{7,6},{8,11},{9,8},{10,9... | collective-permute-start | bytes 884744 | tf_op jit(solution)/shard_map/ppermute | solution.py:203
  118.6 1.0 add_convert_fusion.1
  119.7 1.9 %collective-permute-start.10 = (bf16[3,192,256]{2,1,0:T(8,128)(2,1)S(1)}, bf16[3,192,256]{2,1,0:T(8,128)(2,1)S(1)}, u32[]{:S(2)}, u32[]{:S(2)}) collective-permute-start(bf16[3,192,256]{2,1,0:T(8,128)(2,1)S(1)} %add_convert_fusion.1), channel_id=1, source_target_pairs={{0,1},{1,2},{2,3},{3,0},{4,5},{5,6},{6,7},{7,4},{8,9},{9,10},{10,1... | collective-permute-start | bytes 884744 | tf_op jit(solution)/shard_map/ppermute | solution.py:200
  121.6 1.0 add_convert_fusion
  122.6 5.1 %collective-permute-start.14 = (bf16[3,192,256]{2,1,0:T(8,128)(2,1)S(1)}, bf16[3,192,256]{2,1,0:T(8,128)(2,1)S(1)}, u32[]{:S(2)}, u32[]{:S(2)}) collective-permute-start(bf16[3,192,256]{2,1,0:T(8,128)(2,1)S(1)} %add_convert_fusion), channel_id=1, source_target_pairs={{0,3},{1,0},{2,1},{3,2},{4,7},{5,4},{6,5},{7,6},{8,11},{9,8},{10,9... | collective-permute-start | bytes 884744 | tf_op jit(solution)/shard_map/ppermute | solution.py:203
  127.8 3.8 %all-to-all-start = ((f32[24,2,128]{2,1,0:T(2,128)}), f32[24,2,128]{2,1,0:T(2,128)S(1)}, u32[]{:S(2)}, u32[]{:S(2)}) async-start(f32[24,2,128]{2,1,0:T(2,128)} %get-tuple-element.21), calls=%async_computation | async-start | bytes 49152 | tf_op jit(solution)/shard_map/all_to_all | solution.py:215
  132.8 2.5 %unspread.1 = bf16[16,6,24,128]{3,2,1,0:T(8,128)(2,1)} custom-call(bf16[3,192,256]{2,1,0:T(8,128)(2,1)} %get-tuple-element.29.refs_0_, bf16[3,192,256]{2,1,0:T(8,128)(2,1)} %get-tuple-element.30.refs_1_, bf16[3,192,256]{2,1,0:T(8,128)(2,1)} %copy-done.5, bf16[3,192,256]{2,1,0:T(8,128)(2,1)} %copy-done.3, bf16[3,192,256]{2,1,0:T(8,128)(2,1)} %copy-done.4, ...), custom_call_target="tpu_custom_call" | custom-call | flops 10000000 | bytes 2359296 | tf_op jit(solution)/shard_map/unspread/pallas_call | solution.py:303
  135.3 7.1 %all-to-all-done.logits_ref = f32[24,2,128]{2,1,0:T(2,128)S(1)} async-done(((f32[24,2,128]{2,1,0:T(2,128)}), f32[24,2,128]{2,1,0:T(2,128)S(1)}, u32[]{:S(2)}, u32[]{:S(2)}) %all-to-all-start) | async-done | bytes 24608 | tf_op jit(solution)/shard_map/all_to_all | solution.py:215
  142.4 33.4 %all_to_all.16 = bf16[96,24,128]{2,1,0:T(8,128)(2,1)} all-to-all(bf16[96,24,128]{2,1,0:T(8,128)(2,1)} %bitcast.36), channel_id=1, replica_groups=mesh['zh'=2,'yq'=4,'yp'=2,'c'=2,'z'=6,'x'=4] {'zh','yq','yp','z'}, dimensions={0} | all-to-all | bytes 1179648 | tf_op jit(solution)/shard_map/all_to_all | solution.py:310
  175.8 2.2 %merge.1 = bf16[32,256]{1,0:T(8,128)(2,1)} custom-call(s32[2,32]{1,0:T(2,128)} %bitcast.39, f32[24,2,128]{2,1,0:T(2,128)} %copy-done.9, bf16[8,12,24,128]{3,2,1,0:T(8,128)(2,1)} %bitcast.35), custom_call_target="tpu_custom_call" | custom-call | flops 10000000 | bytes 1000000 | tf_op jit(solution)/shard_map/merge/pallas_call | solution.py:311
  (33 shorter events, 1.3 us)
Async XLA Ops:
  0.0 55.5 %copy-start = (bf16[1,6144,128]{2,1,0:T(8,128)(2,1)S(1)}, bf16[1,6144,128]{2,1,0:T(8,128)(2,1)}, u32[]{:S(2)}) copy-start(bf16[1,6144,128]{2,1,0:T(8,128)(2,1)} %param.9) | copy-start | bytes 4718596
  55.5 24.9 %collective-permute-start.4 = (bf16[6144,128]{1,0:T(8,128)(2,1)S(1)}, bf16[6144,128]{1,0:T(8,128)(2,1)S(1)}, u32[]{:S(2)}, u32[]{:S(2)}) collective-permute-start(bf16[6144,128]{1,0:T(8,128)(2,1)S(1)} %bitcast.21), channel_id=1, source_target_pairs={{0,24},{24,0},{1,25},{25,1},{2,26},{26,2},{3,27},{27,3},{4,28},{28... | collective-permute-start | bytes 4718600 | tf_op jit(solution)/shard_map/ppermute | solution.py:229
  57.4 25.6 %collective-permute-start.5 = (bf16[6144,128]{1,0:T(8,128)(2,1)}, bf16[6144,128]{1,0:T(8,128)(2,1)}, u32[]{:S(2)}, u32[]{:S(2)}) collective-permute-start(bf16[6144,128]{1,0:T(8,128)(2,1)} %bitcast.22), channel_id=1, source_target_pairs={{0,24},{24,0},{1,25},{25,1},{2,26},{26,2},{3,27},{27,3},{4,28},{28... | collective-permute-start | bytes 4718600 | tf_op jit(solution)/shard_map/ppermute | solution.py:230
  59.8 36.2 %collective-permute-start.8 = (bf16[128,6144]{1,0:T(8,128)(2,1)}, bf16[128,6144]{1,0:T(8,128)(2,1)}, u32[]{:S(2)}, u32[]{:S(2)}) collective-permute-start(bf16[128,6144]{1,0:T(8,128)(2,1)} %bitcast.31), channel_id=1, source_target_pairs={{0,24},{24,0},{1,25},{25,1},{2,26},{26,2},{3,27},{27,3},{4,28},{28... | collective-permute-start | bytes 4718600 | tf_op jit(solution)/shard_map/ppermute | solution.py:231
  61.7 12.7 %collective-permute-start.2 = (bf16[3,192,256]{2,1,0:T(8,128)(2,1)}, bf16[3,192,256]{2,1,0:T(8,128)(2,1)S(1)}, u32[]{:S(2)}, u32[]{:S(2)}) collective-permute-start(bf16[3,192,256]{2,1,0:T(8,128)(2,1)} %get-tuple-element.24.refs_2_), channel_id=1, source_target_pairs={{0,1},{1,2},{2,3},{3,0},{4,5},{5,6},{6,7},{7,4},{8,9},{9,10},{10,1... | collective-permute-start | bytes 884744 | tf_op jit(solution)/shard_map/ppermute | solution.py:200
  65.1 12.8 %collective-permute-start = (bf16[3,192,256]{2,1,0:T(8,128)(2,1)}, bf16[3,192,256]{2,1,0:T(8,128)(2,1)}, u32[]{:S(2)}, u32[]{:S(2)}) collective-permute-start(bf16[3,192,256]{2,1,0:T(8,128)(2,1)} %get-tuple-element.23.refs_1_), channel_id=1, source_target_pairs={{0,3},{1,0},{2,1},{3,2},{4,7},{5,4},{6,5},{7,6},{8,11},{9,8},{10,9... | collective-permute-start | bytes 884744 | tf_op jit(solution)/shard_map/ppermute | solution.py:203
  74.4 18.7 %copy-start.2 = (bf16[3,192,256]{2,1,0:T(8,128)(2,1)}, bf16[3,192,256]{2,1,0:T(8,128)(2,1)S(1)}, u32[]{:S(2)}) copy-start(bf16[3,192,256]{2,1,0:T(8,128)(2,1)S(1)} %collective-permute-done.2.refs_2_) | copy-start | bytes 884740
  74.5 15.8 %collective-permute-start.7 = (bf16[3,192,256]{2,1,0:T(8,128)(2,1)}, bf16[3,192,256]{2,1,0:T(8,128)(2,1)}, u32[]{:S(2)}, u32[]{:S(2)}) collective-permute-start(bf16[3,192,256]{2,1,0:T(8,128)(2,1)} %get-tuple-element.24.refs_2_), channel_id=1, source_target_pairs={{0,3},{1,0},{2,1},{3,2},{4,7},{5,4},{6,5},{7,6},{8,11},{9,8},{10,9... | collective-permute-start | bytes 884744 | tf_op jit(solution)/shard_map/ppermute | solution.py:203
  77.9 15.2 %collective-permute-start.6 = (bf16[3,192,256]{2,1,0:T(8,128)(2,1)}, bf16[3,192,256]{2,1,0:T(8,128)(2,1)}, u32[]{:S(2)}, u32[]{:S(2)}) collective-permute-start(bf16[3,192,256]{2,1,0:T(8,128)(2,1)} %get-tuple-element.23.refs_1_), channel_id=1, source_target_pairs={{0,1},{1,2},{2,3},{3,0},{4,5},{5,6},{6,7},{7,4},{8,9},{9,10},{10,1... | collective-permute-start | bytes 884744 | tf_op jit(solution)/shard_map/ppermute | solution.py:200
  80.3 7.1 %copy-start.1 = (bf16[6144,128]{1,0:T(8,128)(2,1)}, bf16[6144,128]{1,0:T(8,128)(2,1)S(1)}, u32[]{:S(2)}) copy-start(bf16[6144,128]{1,0:T(8,128)(2,1)S(1)} %collective-permute-done.4) | copy-start | bytes 4718596
  80.3 15.7 %collective-permute-start.3 = (bf16[3,192,256]{2,1,0:T(8,128)(2,1)S(1)}, bf16[3,192,256]{2,1,0:T(8,128)(2,1)S(1)}, u32[]{:S(2)}, u32[]{:S(2)}) collective-permute-start(bf16[3,192,256]{2,1,0:T(8,128)(2,1)S(1)} %collective-permute-done.2.refs_2_), channel_id=1, source_target_pairs={{0,1},{1,2},{2,3},{3,0},{4,5},{5,6},{6,7},{7,4},{8,9},{9,10},{10,1... | collective-permute-start | bytes 884744 | tf_op jit(solution)/shard_map/ppermute | solution.py:200
  83.0 13.0 %collective-permute-start.1 = (bf16[3,192,256]{2,1,0:T(8,128)(2,1)}, bf16[3,192,256]{2,1,0:T(8,128)(2,1)S(1)}, u32[]{:S(2)}, u32[]{:S(2)}) collective-permute-start(bf16[3,192,256]{2,1,0:T(8,128)(2,1)} %collective-permute-done.refs_1_), channel_id=1, source_target_pairs={{0,3},{1,0},{2,1},{3,2},{4,7},{5,4},{6,5},{7,6},{8,11},{9,8},{10,9... | collective-permute-start | bytes 884744 | tf_op jit(solution)/shard_map/ppermute | solution.py:203
  96.0 0.7 copy-start.7
  96.0 0.8 copy-start.8
  101.0 17.6 %collective-permute-start.9 = (bf16[3,192,256]{2,1,0:T(8,128)(2,1)}, bf16[3,192,256]{2,1,0:T(8,128)(2,1)S(1)}, u32[]{:S(2)}, u32[]{:S(2)}) collective-permute-start(bf16[3,192,256]{2,1,0:T(8,128)(2,1)} %get-tuple-element.32), channel_id=1, source_target_pairs={{0,1},{1,2},{2,3},{3,0},{4,5},{5,6},{6,7},{7,4},{8,9},{9,10},{10,1... | collective-permute-start | bytes 884744 | tf_op jit(solution)/shard_map/ppermute | solution.py:200
  103.0 18.6 %collective-permute-start.13 = (bf16[3,192,256]{2,1,0:T(8,128)(2,1)}, bf16[3,192,256]{2,1,0:T(8,128)(2,1)S(1)}, u32[]{:S(2)}, u32[]{:S(2)}) collective-permute-start(bf16[3,192,256]{2,1,0:T(8,128)(2,1)} %get-tuple-element.36), channel_id=1, source_target_pairs={{0,3},{1,0},{2,1},{3,2},{4,7},{5,4},{6,5},{7,6},{8,11},{9,8},{10,9... | collective-permute-start | bytes 884744 | tf_op jit(solution)/shard_map/ppermute | solution.py:203
  111.6 20.0 %collective-permute-start.11 = (bf16[3,192,256]{2,1,0:T(8,128)(2,1)}, bf16[3,192,256]{2,1,0:T(8,128)(2,1)S(1)}, u32[]{:S(2)}, u32[]{:S(2)}) collective-permute-start(bf16[3,192,256]{2,1,0:T(8,128)(2,1)} %get-tuple-element.33), channel_id=1, source_target_pairs={{0,1},{1,2},{2,3},{3,0},{4,5},{5,6},{6,7},{7,4},{8,9},{9,10},{10,1... | collective-permute-start | bytes 884744 | tf_op jit(solution)/shard_map/ppermute | solution.py:200
  113.5 18.1 %collective-permute-start.12 = (bf16[3,192,256]{2,1,0:T(8,128)(2,1)}, bf16[3,192,256]{2,1,0:T(8,128)(2,1)S(1)}, u32[]{:S(2)}, u32[]{:S(2)}) collective-permute-start(bf16[3,192,256]{2,1,0:T(8,128)(2,1)} %get-tuple-element.34), channel_id=1, source_target_pairs={{0,3},{1,0},{2,1},{3,2},{4,7},{5,4},{6,5},{7,6},{8,11},{9,8},{10,9... | collective-permute-start | bytes 884744 | tf_op jit(solution)/shard_map/ppermute | solution.py:203
  119.7 12.0 %collective-permute-start.10 = (bf16[3,192,256]{2,1,0:T(8,128)(2,1)S(1)}, bf16[3,192,256]{2,1,0:T(8,128)(2,1)S(1)}, u32[]{:S(2)}, u32[]{:S(2)}) collective-permute-start(bf16[3,192,256]{2,1,0:T(8,128)(2,1)S(1)} %add_convert_fusion.1), channel_id=1, source_target_pairs={{0,1},{1,2},{2,3},{3,0},{4,5},{5,6},{6,7},{7,4},{8,9},{9,10},{10,1... | collective-permute-start | bytes 884744 | tf_op jit(solution)/shard_map/ppermute | solution.py:200
  122.6 9.4 %collective-permute-start.14 = (bf16[3,192,256]{2,1,0:T(8,128)(2,1)S(1)}, bf16[3,192,256]{2,1,0:T(8,128)(2,1)S(1)}, u32[]{:S(2)}, u32[]{:S(2)}) collective-permute-start(bf16[3,192,256]{2,1,0:T(8,128)(2,1)S(1)} %add_convert_fusion), channel_id=1, source_target_pairs={{0,3},{1,0},{2,1},{3,2},{4,7},{5,4},{6,5},{7,6},{8,11},{9,8},{10,9... | collective-permute-start | bytes 884744 | tf_op jit(solution)/shard_map/ppermute | solution.py:203
  127.8 14.6 %all-to-all-start = ((f32[24,2,128]{2,1,0:T(2,128)}), f32[24,2,128]{2,1,0:T(2,128)S(1)}, u32[]{:S(2)}, u32[]{:S(2)}) async-start(f32[24,2,128]{2,1,0:T(2,128)} %get-tuple-element.21), calls=%async_computation | async-start | bytes 49152 | tf_op jit(solution)/shard_map/all_to_all | solution.py:215
  131.6 0.7 copy-start.3
  131.6 0.8 copy-start.4
  131.6 0.9 copy-start.5
  132.1 0.7 copy-start.6
  142.4 33.4 %copy-start.9 = (f32[24,2,128]{2,1,0:T(2,128)}, f32[24,2,128]{2,1,0:T(2,128)S(1)}, u32[]{:S(2)}) copy-start(f32[24,2,128]{2,1,0:T(2,128)S(1)} %all-to-all-done.logits_ref) | copy-start | bytes 73732
where the time goes:
time: 179 us; the launch traced here: 178 us
  blocking collectives  84.8 us (47%)
  starting transfers between devices  51.1 us (29%)
  Pallas kernels  25 us (14%)
  waiting for transfers between devices  13.3 us (7%)
  other arithmetic  2.07 us (1%)
    all_to_all x1, blocking collectives, block(): lax.all_to_all(messages.reshape(far, CHUNK, LANES), FAR, 0, 0, tiled=True)  51.4 us
    all_to_all x1, blocking collectives, block(): lax.all_to_all(leaving.reshape(far, CHUNK, LANES), FAR, 0, 0, tiled=True)  33.4 us
    ppermute x6, starting transfers between devices, behind(): return lax.ppermute(v, 'x', backward)  26.9 us
    ppermute x6, starting transfers between devices, ahead(): return lax.ppermute(v, 'x', forward)  14.2 us
    pallas_call x3, Pallas kernels, gate_up(): call(lambda *refs: gate_up_kernel(more, *refs), sums, flops, nbytes, grid...  8.55 us
    all_to_all x1, waiting for transfers between devices, block(): partial_logits = lax.all_to_all(logits, ('z', 'x'), 0, 0, tiled=True)  7.14 us
    ppermute x6, waiting for transfers between devices, ahead(): return lax.ppermute(v, 'x', forward)  5.67 us
    pallas_call x1, Pallas kernels, block(): call(lambda *refs: turn_kernel(xs, *refs), (jax.ShapeDtypeStruct((rows, 2...  4.21 us
  transfers between devices with their start and end apart: 16, of which 3 were waited for; matrix products, arithmetic and copies ran while one was open for 1% of the time, Pallas kernels for 8%

commit v1 on v0

--- a/solution.py
+++ b/solution.py
@@ -14,9 +14,10 @@
 f32, bf16 = jnp.float32, jnp.bfloat16
 
 
-def call(body, out_shape, flops, nbytes, **kw):
+def call(body, out_shape, flops, nbytes, mib=8, **kw):
     return pl.pallas_call(
         body,
+        compiler_params=pltpu.CompilerParams(vmem_limit_bytes=mib * 2**20),
         out_shape=out_shape,
         cost_estimate=pl.CostEstimate(flops=flops, bytes_accessed=nbytes, transcendentals=0),
         **kw,
@@ -102,51 +103,42 @@
             out_ref[2 * p + 1, z] = b.astype(bf16)
 
 
-def products(lo_ref, hi_ref, weights, total):
-    half = lo_ref.shape[0]
-    for z in range(2 * half):
-        rows = lo_ref[z] if z < half else hi_ref[z - half]
-        both = jnp.concatenate([w[z, 0] for w in weights], axis=1)
-        term = jnp.dot(rows, both, preferred_element_type=f32)
-        total = term if total is None else total + term
-    return total
-
-
-def gate_up_kernel(more, xi_ref, *refs):
-    lo_ref, hi_ref, *weights = refs[:6]
-    total = refs[6][...] if more else None
-    refs[-1][...] = products(lo_ref, hi_ref, weights, total)
-
-
 def down(hidden, own_ref, other_ref, column, z, xs):
     at = pl.ds(pl.multiple_of((z * xs + column) * 256, 256), 256)
     both = jnp.concatenate([own_ref[:, at], other_ref[:, at]], axis=0)
     return jnp.dot(hidden, both, preferred_element_type=f32).astype(bf16)
 
 
-def turn_kernel(xs, xi_ref, *refs):
-    lo_ref, hi_ref, *weights = refs[:6]
-    total_ref, own_ref, other_ref, hidden_ref, out_lo, out_hi = refs[6:]
-    total = products(lo_ref, hi_ref, weights, total_ref[...])
+def turn_kernel(xs, near_ref, *refs):
+    parts, weights = refs[: 2 * xs], refs[2 * xs : 2 * xs + 4]
+    own_ref, other_ref, hidden_ref, out_lo, out_hi = refs[2 * xs + 4 :]
+    half, _, share = parts[0].shape
+    total = None
+    for n in range(xs):
+        for z in range(2 * half):
+            rows = parts[2 * n + z // half][z % half]
+            at = pl.ds(pl.multiple_of((z * xs + near_ref[n]) * share, share), share)
+            both = jnp.concatenate([w[at, :] for w in weights], axis=1)
+            term = jnp.dot(rows, both, preferred_element_type=f32)
+            total = term if total is None else total + term
     units = total.shape[1] // 2
     gate, up = total[:, :units], total[:, units:]
     hidden = (jax.nn.silu(gate) * up).astype(bf16)
     hidden_ref[...] = hidden
-    half = lo_ref.shape[0]
     for z in range(2 * half):
-        value = down(hidden, own_ref, other_ref, xi_ref[0], z, xs)
+        value = down(hidden, own_ref, other_ref, near_ref[xs - 1], z, xs)
         if z < half:
             out_lo[z] = value
         else:
             out_hi[z - half] = value
 
 
-def down_kernel(xs, first_ref, second_ref, third_ref, hidden_ref, own_ref, other_ref, *outs):
+def down_kernel(xs, near_ref, hidden_ref, own_ref, other_ref, *outs):
     hidden = hidden_ref[...]
     half = outs[0].shape[0]
-    for n in range(len(outs) // 2):
+    for n, place in enumerate((1, 2, 0)):
         for z in range(2 * half):
-            value = down(hidden, own_ref, other_ref, (first_ref, second_ref, third_ref)[n][0], z, xs)
+            value = down(hidden, own_ref, other_ref, near_ref[place], z, xs)
             if z < half:
                 outs[2 * n][z] = value
             else:
@@ -192,7 +184,7 @@
     units = w_gate.shape[2]
     ids = expert_ids.T
     me = lax.axis_index("x")
-    near = [((me + k) & (xs - 1)).astype(jnp.int32).reshape(1) for k in (0, 1, 3, 2)]
+    near = ((me + jnp.array([0, 1, 3, 2], jnp.int32)) & (xs - 1)).astype(jnp.int32)
     forward = [(i, (i + 1) % xs) for i in range(xs)]
     backward = [(i, (i - 1) % xs) for i in range(xs)]
 
@@ -232,68 +224,47 @@
     far_hi = ahead(left_hi)
     far_lo = behind(right_lo)
 
-    stacked = [v.reshape(zs, xs, share, units) for v in (gate_w, gate_o, up_w, up_o)]
-    weight_spec = pl.BlockSpec((zs, 1, share, units), lambda g, xi: (0, xi[0], 0, 0))
-
-    def whole(*shape):
-        return pl.BlockSpec(shape, lambda g, *xi: (0,) * len(shape))
-
-    part = whole(half, rows, share)
-    sums = jax.ShapeDtypeStruct((rows, 4 * units), f32)
-    sums_spec = whole(rows, 4 * units)
-    flops = 2 * rows * zs * share * 4 * units
-    nbytes = zs * share * units * 8 + 2 * half * rows * share * 2
-
-    def gate_up(total, column, lo, hi):
-        more = total is not None
-        return call(
-            lambda *refs: gate_up_kernel(more, *refs),
-            sums,
-            flops,
-            nbytes,
-            grid_spec=pltpu.PrefetchScalarGridSpec(
-                num_scalar_prefetch=1,
-                grid=(1,),
-                in_specs=[part, part] + [weight_spec] * 4 + [sums_spec] * more,
-                out_specs=sums_spec,
-            ),
-            name="gate_up",
-        )(near[column], lo, hi, *stacked, *([total] if more else []))
-
-    total = gate_up(None, 0, own_lo, own_hi)
-    total = gate_up(total, 1, right_lo, right_hi)
-    total = gate_up(total, 2, left_lo, left_hi)
-    down_spec = whole(units, zs * xs * share)
-    hidden_spec = whole(rows, 2 * units)
+    smem = pl.BlockSpec(memory_space=pltpu.SMEM)
+    vmem = pl.BlockSpec(memory_space=pltpu.VMEM)
+    flops = 2 * rows * zs * xs * share * 4 * units
+    nbytes = zs * xs * share * units * 8 + 2 * xs * half * rows * share * 2
     hidden, opp_lo, opp_hi = call(
         lambda *refs: turn_kernel(xs, *refs),
         (jax.ShapeDtypeStruct((rows, 2 * units), bf16), part_shape, part_shape),
-        2 * flops,
-        2 * nbytes,
-        grid_spec=pltpu.PrefetchScalarGridSpec(
-            num_scalar_prefetch=1,
-            grid=(1,),
-            in_specs=[part, part] + [weight_spec] * 4 + [sums_spec, down_spec, down_spec],
-            out_specs=(hidden_spec, part, part),
-        ),
+        flops,
+        nbytes,
+        mib=24,
+        in_specs=[smem] + [vmem] * (2 * xs + 6),
         name="turn",
-    )(near[3], far_lo, far_hi, *stacked, total, down_w, down_o)
+    )(
+        near,
+        own_lo,
+        own_hi,
+        right_lo,
+        right_hi,
+        left_lo,
+        left_hi,
+        far_lo,
+        far_hi,
+        gate_w,
+        gate_o,
+        up_w,
+        up_o,
+        down_w,
+        down_o,
+    )
 
     from_left_lo = ahead(opp_lo)
     from_right_hi = behind(opp_hi)
     outs = call(
         lambda *refs: down_kernel(xs, *refs),
         (part_shape,) * 6,
-        2 * flops,
-        2 * nbytes,
-        grid_spec=pltpu.PrefetchScalarGridSpec(
-            num_scalar_prefetch=3,
-            grid=(1,),
-            in_specs=[hidden_spec, down_spec, down_spec],
-            out_specs=(part,) * 6,
-        ),
+        flops // 2,
+        nbytes // 2,
+        mib=12,
+        in_specs=[smem] + [vmem] * 3,
         name="down",
-    )(near[1], near[2], near[0], hidden, down_w, down_o)
+    )(near, hidden, down_w, down_o)
     next_lo, next_hi, prev_lo, prev_hi, mine_lo, mine_hi = outs
     c_hi = ahead(next_hi)
     e_lo = behind(prev_lo)

time: 179 us -> 181 us (1.011)
  Pallas kernels: 25 us -> 8.21 us
  waiting for transfers between devices: 13.3 us -> 24.4 us
  local copies, waits for them, and re-layouts: 1.53 us -> 10.8 us
  other arithmetic: 2.07 us -> 0.15 us
    pallas_call x4 -> x1, Pallas kernels: 12 us -> 1.72 us  [block(): call(lambda *refs: down_kernel(xs, *refs), (part_shape,) * 6, flops // 2,...]
    unnamed x20 -> x32, local copies, waits for them, and re-layouts: 1.53 us -> 10.8 us
    ppermute x6, waiting for transfers between devices: 5.67 us -> 12.7 us  [ahead(): return lax.ppermute(v, 'x', forward)]
    all_to_all x1, waiting for transfers between devices: 7.14 us -> 10.1 us  [block(): partial_logits = lax.all_to_all(logits, ('z', 'x'), 0, 0, tiled=True)]
    ppermute x6, starting transfers between devices: 26.9 us -> 29.5 us  [behind(): return lax.ppermute(v, 'x', backward)]
    pallas_call x1, Pallas kernels: 2.47 us -> 0.24 us  [block(): call(unspread_kernel, jax.ShapeDtypeStruct((sources, zs, CHUNK, LANES), b...]
    pallas_call x1, Pallas kernels: 2.01 us -> 0.1 us  [block(): call(spread_kernel, (part_shape, part_shape), 10 ** 6, 2 * far * CHUNK *...]
  transfers between devices with their start and end apart: 16 -> 16, of which waited for: 3 -> 6; matrix products, arithmetic and copies ran while one was open for 1% -> 0% of each run, Pallas kernels for 8% -> 1%
where the time goes in v1:
time: 181 us; the launch traced here: 180 us
  blocking collectives  83.6 us (46%)
  starting transfers between devices  52.9 us (29%)
  waiting for transfers between devices  24.4 us (13%)
  local copies, waits for them, and re-layouts  10.8 us (6%)
  Pallas kernels  8.21 us (5%)
    all_to_all x1, blocking collectives, block(): lax.all_to_all(messages.reshape(far, CHUNK, LANES), FAR, 0, 0, tiled=True)  51.1 us
    all_to_all x1, blocking collectives, block(): lax.all_to_all(leaving.reshape(far, CHUNK, LANES), FAR, 0, 0, tiled=True)  32.5 us
    ppermute x6, starting transfers between devices, behind(): return lax.ppermute(v, 'x', backward)  29.5 us
    ppermute x6, starting transfers between devices, ahead(): return lax.ppermute(v, 'x', forward)  13.4 us
    ppermute x6, waiting for transfers between devices, ahead(): return lax.ppermute(v, 'x', forward)  12.7 us
    unnamed x32, local copies, waits for them, and re-layouts  10.8 us
    all_to_all x1, waiting for transfers between devices, block(): partial_logits = lax.all_to_all(logits, ('z', 'x'), 0, 0, tiled=True)  10.1 us
    pallas_call x1, Pallas kernels, block(): call(lambda *refs: turn_kernel(xs, *refs), (jax.ShapeDtypeStruct((rows, 2...  4.04 us
  transfers between devices with their start and end apart: 16, of which 6 were waited for; matrix products, arithmetic and copies ran while one was open for 0% of the time, Pallas kernels for 1%

profile of v1, /device:TPU:8, one launch (start us, length us, event | category | flops | bytes accessed | tf_op | source)
XLA Modules:
  0.0 180.4 jit_solution(4797583582593896281)
XLA Ops:
  2.2 1.0 pack.1
  3.2 51.1 %all_to_all.15 = bf16[96,24,128]{2,1,0:T(8,128)(2,1)S(1)} all-to-all(bf16[96,24,128]{2,1,0:T(8,128)(2,1)S(1)} %bitcast.19), channel_id=1, replica_groups=mesh['zh'=2,'yq'=4,'yp'=2,'c'=2,'z'=6,'x'=4] {'zh','yq','yp','z'}, dimensions={0} | all-to-all | bytes 1179648 | tf_op jit(solution)/shard_map/all_to_all | solution.py:208
  54.4 1.9 %collective-permute-start.6 = (bf16[6144,128]{1,0:T(8,128)(2,1)}, bf16[6144,128]{1,0:T(8,128)(2,1)}, u32[]{:S(2)}, u32[]{:S(2)}) collective-permute-start(bf16[6144,128]{1,0:T(8,128)(2,1)} %bitcast.15), channel_id=1, source_target_pairs={{0,24},{24,0},{1,25},{25,1},{2,26},{26,2},{3,27},{27,3},{4,28},{28... | collective-permute-start | bytes 4718600 | tf_op jit(solution)/shard_map/ppermute | solution.py:221
  56.3 2.4 %collective-permute-start.7 = (bf16[6144,128]{1,0:T(8,128)(2,1)}, bf16[6144,128]{1,0:T(8,128)(2,1)}, u32[]{:S(2)}, u32[]{:S(2)}) collective-permute-start(bf16[6144,128]{1,0:T(8,128)(2,1)} %bitcast.17), channel_id=1, source_target_pairs={{0,24},{24,0},{1,25},{25,1},{2,26},{26,2},{3,27},{27,3},{4,28},{28... | collective-permute-start | bytes 4718600 | tf_op jit(solution)/shard_map/ppermute | solution.py:222
  58.8 1.9 %collective-permute-start.8 = (bf16[128,6144]{1,0:T(8,128)(2,1)S(1)}, bf16[128,6144]{1,0:T(8,128)(2,1)S(1)}, u32[]{:S(2)}, u32[]{:S(2)}) collective-permute-start(bf16[128,6144]{1,0:T(8,128)(2,1)S(1)} %bitcast.9), channel_id=1, source_target_pairs={{0,24},{24,0},{1,25},{25,1},{2,26},{26,2},{3,27},{27,3},{4,28},{28... | collective-permute-start | bytes 4718600 | tf_op jit(solution)/shard_map/ppermute | solution.py:223
  60.7 3.4 %collective-permute-start.3 = (bf16[3,192,256]{2,1,0:T(8,128)(2,1)S(1)}, bf16[3,192,256]{2,1,0:T(8,128)(2,1)}, u32[]{:S(2)}, u32[]{:S(2)}) collective-permute-start(bf16[3,192,256]{2,1,0:T(8,128)(2,1)S(1)} %get-tuple-element.24.refs_2_), channel_id=1, source_target_pairs={{0,1},{1,2},{2,3},{3,0},{4,5},{5,6},{6,7},{7,4},{8,9},{9,10},{10,1... | collective-permute-start | bytes 884744 | tf_op jit(solution)/shard_map/ppermute | solution.py:192
  64.1 3.7 %collective-permute-start.1 = (bf16[3,192,256]{2,1,0:T(8,128)(2,1)S(1)}, bf16[3,192,256]{2,1,0:T(8,128)(2,1)S(1)}, u32[]{:S(2)}, u32[]{:S(2)}) collective-permute-start(bf16[3,192,256]{2,1,0:T(8,128)(2,1)S(1)} %get-tuple-element.24.refs_2_), channel_id=1, source_target_pairs={{0,3},{1,0},{2,1},{3,2},{4,7},{5,4},{6,5},{7,6},{8,11},{9,8},{10,9... | collective-permute-start | bytes 884744 | tf_op jit(solution)/shard_map/ppermute | solution.py:195
  68.5 4.8 %collective-permute-done.3.refs_6_ = bf16[3,192,256]{2,1,0:T(8,128)(2,1)} collective-permute-done((bf16[3,192,256]{2,1,0:T(8,128)(2,1)S(1)}, bf16[3,192,256]{2,1,0:T(8,128)(2,1)}, u32[]{:S(2)}, u32[]{:S(2)}) %collective-permute-start.3) | collective-permute-done | bytes 294944 | tf_op jit(solution)/shard_map/ppermute | solution.py:192
  73.3 2.2 %collective-permute-start.2 = (bf16[3,192,256]{2,1,0:T(8,128)(2,1)S(1)}, bf16[3,192,256]{2,1,0:T(8,128)(2,1)S(1)}, u32[]{:S(2)}, u32[]{:S(2)}) collective-permute-start(bf16[3,192,256]{2,1,0:T(8,128)(2,1)S(1)} %get-tuple-element.23.refs_1_), channel_id=1, source_target_pairs={{0,1},{1,2},{2,3},{3,0},{4,5},{5,6},{6,7},{7,4},{8,9},{9,10},{10,1... | collective-permute-start | bytes 884744 | tf_op jit(solution)/shard_map/ppermute | solution.py:192
  76.3 4.9 %collective-permute-start = (bf16[3,192,256]{2,1,0:T(8,128)(2,1)S(1)}, bf16[3,192,256]{2,1,0:T(8,128)(2,1)}, u32[]{:S(2)}, u32[]{:S(2)}) collective-permute-start(bf16[3,192,256]{2,1,0:T(8,128)(2,1)S(1)} %get-tuple-element.23.refs_1_), channel_id=1, source_target_pairs={{0,3},{1,0},{2,1},{3,2},{4,7},{5,4},{6,5},{7,6},{8,11},{9,8},{10,9... | collective-permute-start | bytes 884744 | tf_op jit(solution)/shard_map/ppermute | solution.py:195
  81.1 3.8 %collective-permute-done.2.refs_5_ = bf16[3,192,256]{2,1,0:T(8,128)(2,1)S(1)} collective-permute-done((bf16[3,192,256]{2,1,0:T(8,128)(2,1)S(1)}, bf16[3,192,256]{2,1,0:T(8,128)(2,1)S(1)}, u32[]{:S(2)}, u32[]{:S(2)}) %collective-permute-start.2) | collective-permute-done | bytes 294944 | tf_op jit(solution)/shard_map/ppermute | solution.py:192
  85.7 1.9 %collective-permute-start.5 = (bf16[3,192,256]{2,1,0:T(8,128)(2,1)}, bf16[3,192,256]{2,1,0:T(8,128)(2,1)}, u32[]{:S(2)}, u32[]{:S(2)}) collective-permute-start(bf16[3,192,256]{2,1,0:T(8,128)(2,1)} %collective-permute-done.3.refs_6_), channel_id=1, source_target_pairs={{0,1},{1,2},{2,3},{3,0},{4,5},{5,6},{6,7},{7,4},{8,9},{9,10},{10,1... | collective-permute-start | bytes 884744 | tf_op jit(solution)/shard_map/ppermute | solution.py:192
  87.6 5.1 %collective-permute-start.4 = (bf16[3,192,256]{2,1,0:T(8,128)(2,1)}, bf16[3,192,256]{2,1,0:T(8,128)(2,1)}, u32[]{:S(2)}, u32[]{:S(2)}) collective-permute-start(bf16[3,192,256]{2,1,0:T(8,128)(2,1)} %collective-permute-done.refs_3_), channel_id=1, source_target_pairs={{0,3},{1,0},{2,1},{3,2},{4,7},{5,4},{6,5},{7,6},{8,11},{9,8},{10,9... | collective-permute-start | bytes 884744 | tf_op jit(solution)/shard_map/ppermute | solution.py:195
  92.8 4.0 %collective-permute-done.5.refs_8_ = bf16[3,192,256]{2,1,0:T(8,128)(2,1)} collective-permute-done((bf16[3,192,256]{2,1,0:T(8,128)(2,1)}, bf16[3,192,256]{2,1,0:T(8,128)(2,1)}, u32[]{:S(2)}, u32[]{:S(2)}) %collective-permute-start.5) | collective-permute-done | bytes 294944 | tf_op jit(solution)/shard_map/ppermute | solution.py:192
  96.8 1.2 collective-permute-done.4.refs_7_
  98.0 1.4 copy-done.1
  99.4 1.4 copy-done.2
  100.8 1.0 copy-done.4
  101.8 1.0 copy-done.6
  102.8 1.0 copy-done.10
  103.7 4.0 %turn.1 = (bf16[192,256]{1,0:T(8,128)(2,1)S(1)}, bf16[3,192,256]{2,1,0:T(8,128)(2,1)S(1)}, bf16[3,192,256]{2,1,0:T(8,128)(2,1)S(1)}) custom-call(s32[4]{0:T(128)S(1)} %add_and_fusion.refs_0_, bf16[3,192,256]{2,1,0:T(8,128)(2,1)S(1)} %get-tuple-element.23.refs_1_, bf16[3,192,256]{2,1,0:T(8,128)(2,1)S(1)} %copy-done.4, ...), custom_call_target="tpu_custom_call" | custom-call | flops 1207959552 | bytes 8650752 | tf_op jit(solution)/shard_map/turn/pallas_call | solution.py:231
  107.8 1.9 %collective-permute-start.9 = (bf16[3,192,256]{2,1,0:T(8,128)(2,1)S(1)}, bf16[3,192,256]{2,1,0:T(8,128)(2,1)S(1)}, u32[]{:S(2)}, u32[]{:S(2)}) collective-permute-start(bf16[3,192,256]{2,1,0:T(8,128)(2,1)S(1)} %get-tuple-element.32), channel_id=1, source_target_pairs={{0,1},{1,2},{2,3},{3,0},{4,5},{5,6},{6,7},{7,4},{8,9},{9,10},{10,1... | collective-permute-start | bytes 884744 | tf_op jit(solution)/shard_map/ppermute | solution.py:192
  109.7 5.6 %collective-permute-start.13 = (bf16[3,192,256]{2,1,0:T(8,128)(2,1)S(1)}, bf16[3,192,256]{2,1,0:T(8,128)(2,1)S(1)}, u32[]{:S(2)}, u32[]{:S(2)}) collective-permute-start(bf16[3,192,256]{2,1,0:T(8,128)(2,1)S(1)} %get-tuple-element.36), channel_id=1, source_target_pairs={{0,3},{1,0},{2,1},{3,2},{4,7},{5,4},{6,5},{7,6},{8,11},{9,8},{10,9... | collective-permute-start | bytes 884744 | tf_op jit(solution)/shard_map/ppermute | solution.py:195
  115.3 1.7 down.1
  117.8 2.0 %collective-permute-start.11 = (bf16[3,192,256]{2,1,0:T(8,128)(2,1)}, bf16[3,192,256]{2,1,0:T(8,128)(2,1)S(1)}, u32[]{:S(2)}, u32[]{:S(2)}) collective-permute-start(bf16[3,192,256]{2,1,0:T(8,128)(2,1)} %get-tuple-element.33), channel_id=1, source_target_pairs={{0,1},{1,2},{2,3},{3,0},{4,5},{5,6},{6,7},{7,4},{8,9},{9,10},{10,1... | collective-permute-start | bytes 884744 | tf_op jit(solution)/shard_map/ppermute | solution.py:192
  119.8 5.1 %collective-permute-start.12 = (bf16[3,192,256]{2,1,0:T(8,128)(2,1)}, bf16[3,192,256]{2,1,0:T(8,128)(2,1)S(1)}, u32[]{:S(2)}, u32[]{:S(2)}) collective-permute-start(bf16[3,192,256]{2,1,0:T(8,128)(2,1)} %get-tuple-element.34), channel_id=1, source_target_pairs={{0,3},{1,0},{2,1},{3,2},{4,7},{5,4},{6,5},{7,6},{8,11},{9,8},{10,9... | collective-permute-start | bytes 884744 | tf_op jit(solution)/shard_map/ppermute | solution.py:195
  125.0 1.9 %collective-permute-start.10 = (bf16[3,192,256]{2,1,0:T(8,128)(2,1)S(1)}, bf16[3,192,256]{2,1,0:T(8,128)(2,1)S(1)}, u32[]{:S(2)}, u32[]{:S(2)}) collective-permute-start(bf16[3,192,256]{2,1,0:T(8,128)(2,1)S(1)} %add_convert_fusion.1), channel_id=1, source_target_pairs={{0,1},{1,2},{2,3},{3,0},{4,5},{5,6},{6,7},{7,4},{8,9},{9,10},{10,1... | collective-permute-start | bytes 884744 | tf_op jit(solution)/shard_map/ppermute | solution.py:192
  127.0 5.1 %collective-permute-start.14 = (bf16[3,192,256]{2,1,0:T(8,128)(2,1)S(1)}, bf16[3,192,256]{2,1,0:T(8,128)(2,1)S(1)}, u32[]{:S(2)}, u32[]{:S(2)}) collective-permute-start(bf16[3,192,256]{2,1,0:T(8,128)(2,1)S(1)} %add_convert_fusion), channel_id=1, source_target_pairs={{0,3},{1,0},{2,1},{3,2},{4,7},{5,4},{6,5},{7,6},{8,11},{9,8},{10,9... | collective-permute-start | bytes 884744 | tf_op jit(solution)/shard_map/ppermute | solution.py:195
  132.2 3.8 %all-to-all-start = ((f32[24,2,128]{2,1,0:T(2,128)}), f32[24,2,128]{2,1,0:T(2,128)S(1)}, u32[]{:S(2)}, u32[]{:S(2)}) async-start(f32[24,2,128]{2,1,0:T(2,128)} %get-tuple-element.21), calls=%async_computation | async-start | bytes 49152 | tf_op jit(solution)/shard_map/all_to_all | solution.py:207
  136.8 10.1 %all-to-all-done.logits_ref = f32[24,2,128]{2,1,0:T(2,128)S(1)} async-done(((f32[24,2,128]{2,1,0:T(2,128)}), f32[24,2,128]{2,1,0:T(2,128)S(1)}, u32[]{:S(2)}, u32[]{:S(2)}) %all-to-all-start) | async-done | bytes 24608 | tf_op jit(solution)/shard_map/all_to_all | solution.py:207
  146.8 32.5 %all_to_all.16 = bf16[96,24,128]{2,1,0:T(8,128)(2,1)S(1)} all-to-all(bf16[96,24,128]{2,1,0:T(8,128)(2,1)S(1)} %bitcast.14), channel_id=1, replica_groups=mesh['zh'=2,'yq'=4,'yp'=2,'c'=2,'z'=6,'x'=4] {'zh','yq','yp','z'}, dimensions={0} | all-to-all | bytes 1179648 | tf_op jit(solution)/shard_map/all_to_all | solution.py:281
  179.3 1.1 merge.1
  (43 shorter events, 6.1 us)
Async XLA Ops:
  0.0 58.8 %copy-start = (bf16[1,128,6144]{2,1,0:T(8,128)(2,1)S(1)}, bf16[1,128,6144]{2,1,0:T(8,128)(2,1)}, u32[]{:S(2)}) copy-start(bf16[1,128,6144]{2,1,0:T(8,128)(2,1)} %param.12) | copy-start | bytes 4718596
  0.0 0.8 copy-start.11
  0.8 0.7 copy-start.13
  1.5 0.7 copy-start.14
  2.2 90.6 %copy-start.15 = (s32[4]{0:T(128)S(1)}, s32[4]{0:T(128)}, u32[]{:S(2)}) copy-start(s32[4]{0:T(128)} %constant.8.clone) | copy-start | bytes 52
  54.4 43.6 %collective-permute-start.6 = (bf16[6144,128]{1,0:T(8,128)(2,1)}, bf16[6144,128]{1,0:T(8,128)(2,1)}, u32[]{:S(2)}, u32[]{:S(2)}) collective-permute-start(bf16[6144,128]{1,0:T(8,128)(2,1)} %bitcast.15), channel_id=1, source_target_pairs={{0,24},{24,0},{1,25},{25,1},{2,26},{26,2},{3,27},{27,3},{4,28},{28... | collective-permute-start | bytes 4718600 | tf_op jit(solution)/shard_map/ppermute | solution.py:221
  56.3 41.7 %collective-permute-start.7 = (bf16[6144,128]{1,0:T(8,128)(2,1)}, bf16[6144,128]{1,0:T(8,128)(2,1)}, u32[]{:S(2)}, u32[]{:S(2)}) collective-permute-start(bf16[6144,128]{1,0:T(8,128)(2,1)} %bitcast.17), channel_id=1, source_target_pairs={{0,24},{24,0},{1,25},{25,1},{2,26},{26,2},{3,27},{27,3},{4,28},{28... | collective-permute-start | bytes 4718600 | tf_op jit(solution)/shard_map/ppermute | solution.py:222
  58.8 39.2 %collective-permute-start.8 = (bf16[128,6144]{1,0:T(8,128)(2,1)S(1)}, bf16[128,6144]{1,0:T(8,128)(2,1)S(1)}, u32[]{:S(2)}, u32[]{:S(2)}) collective-permute-start(bf16[128,6144]{1,0:T(8,128)(2,1)S(1)} %bitcast.9), channel_id=1, source_target_pairs={{0,24},{24,0},{1,25},{25,1},{2,26},{26,2},{3,27},{27,3},{4,28},{28... | collective-permute-start | bytes 4718600 | tf_op jit(solution)/shard_map/ppermute | solution.py:223
  60.7 12.6 %collective-permute-start.3 = (bf16[3,192,256]{2,1,0:T(8,128)(2,1)S(1)}, bf16[3,192,256]{2,1,0:T(8,128)(2,1)}, u32[]{:S(2)}, u32[]{:S(2)}) collective-permute-start(bf16[3,192,256]{2,1,0:T(8,128)(2,1)S(1)} %get-tuple-element.24.refs_2_), channel_id=1, source_target_pairs={{0,1},{1,2},{2,3},{3,0},{4,5},{5,6},{6,7},{7,4},{8,9},{9,10},{10,1... | collective-permute-start | bytes 884744 | tf_op jit(solution)/shard_map/ppermute | solution.py:192
  64.1 11.4 %collective-permute-start.1 = (bf16[3,192,256]{2,1,0:T(8,128)(2,1)S(1)}, bf16[3,192,256]{2,1,0:T(8,128)(2,1)S(1)}, u32[]{:S(2)}, u32[]{:S(2)}) collective-permute-start(bf16[3,192,256]{2,1,0:T(8,128)(2,1)S(1)} %get-tuple-element.24.refs_2_), channel_id=1, source_target_pairs={{0,3},{1,0},{2,1},{3,2},{4,7},{5,4},{6,5},{7,6},{8,11},{9,8},{10,9... | collective-permute-start | bytes 884744 | tf_op jit(solution)/shard_map/ppermute | solution.py:195
  67.8 0.7 copy-start.3
  73.3 11.6 %collective-permute-start.2 = (bf16[3,192,256]{2,1,0:T(8,128)(2,1)S(1)}, bf16[3,192,256]{2,1,0:T(8,128)(2,1)S(1)}, u32[]{:S(2)}, u32[]{:S(2)}) collective-permute-start(bf16[3,192,256]{2,1,0:T(8,128)(2,1)S(1)} %get-tuple-element.23.refs_1_), channel_id=1, source_target_pairs={{0,1},{1,2},{2,3},{3,0},{4,5},{5,6},{6,7},{7,4},{8,9},{9,10},{10,1... | collective-permute-start | bytes 884744 | tf_op jit(solution)/shard_map/ppermute | solution.py:192
  75.5 0.7 copy-start.5
  76.3 11.4 %collective-permute-start = (bf16[3,192,256]{2,1,0:T(8,128)(2,1)S(1)}, bf16[3,192,256]{2,1,0:T(8,128)(2,1)}, u32[]{:S(2)}, u32[]{:S(2)}) collective-permute-start(bf16[3,192,256]{2,1,0:T(8,128)(2,1)S(1)} %get-tuple-element.23.refs_1_), channel_id=1, source_target_pairs={{0,3},{1,0},{2,1},{3,2},{4,7},{5,4},{6,5},{7,6},{8,11},{9,8},{10,9... | collective-permute-start | bytes 884744 | tf_op jit(solution)/shard_map/ppermute | solution.py:195
  85.0 0.7 copy-start.9
  85.7 11.1 %collective-permute-start.5 = (bf16[3,192,256]{2,1,0:T(8,128)(2,1)}, bf16[3,192,256]{2,1,0:T(8,128)(2,1)}, u32[]{:S(2)}, u32[]{:S(2)}) collective-permute-start(bf16[3,192,256]{2,1,0:T(8,128)(2,1)} %collective-permute-done.3.refs_6_), channel_id=1, source_target_pairs={{0,1},{1,2},{2,3},{3,0},{4,5},{5,6},{6,7},{7,4},{8,9},{9,10},{10,1... | collective-permute-start | bytes 884744 | tf_op jit(solution)/shard_map/ppermute | solution.py:192
  87.6 10.4 %collective-permute-start.4 = (bf16[3,192,256]{2,1,0:T(8,128)(2,1)}, bf16[3,192,256]{2,1,0:T(8,128)(2,1)}, u32[]{:S(2)}, u32[]{:S(2)}) collective-permute-start(bf16[3,192,256]{2,1,0:T(8,128)(2,1)} %collective-permute-done.refs_3_), channel_id=1, source_target_pairs={{0,3},{1,0},{2,1},{3,2},{4,7},{5,4},{6,5},{7,6},{8,11},{9,8},{10,9... | collective-permute-start | bytes 884744 | tf_op jit(solution)/shard_map/ppermute | solution.py:195
  98.0 1.4 copy-start.1
  99.4 1.4 copy-start.2
  100.8 1.0 copy-start.4
  101.8 1.0 copy-start.6
  102.8 1.0 copy-start.10
  107.8 17.2 %collective-permute-start.9 = (bf16[3,192,256]{2,1,0:T(8,128)(2,1)S(1)}, bf16[3,192,256]{2,1,0:T(8,128)(2,1)S(1)}, u32[]{:S(2)}, u32[]{:S(2)}) collective-permute-start(bf16[3,192,256]{2,1,0:T(8,128)(2,1)S(1)} %get-tuple-element.32), channel_id=1, source_target_pairs={{0,1},{1,2},{2,3},{3,0},{4,5},{5,6},{6,7},{7,4},{8,9},{9,10},{10,1... | collective-permute-start | bytes 884744 | tf_op jit(solution)/shard_map/ppermute | solution.py:192
  109.7 17.3 %collective-permute-start.13 = (bf16[3,192,256]{2,1,0:T(8,128)(2,1)S(1)}, bf16[3,192,256]{2,1,0:T(8,128)(2,1)S(1)}, u32[]{:S(2)}, u32[]{:S(2)}) collective-permute-start(bf16[3,192,256]{2,1,0:T(8,128)(2,1)S(1)} %get-tuple-element.36), channel_id=1, source_target_pairs={{0,3},{1,0},{2,1},{3,2},{4,7},{5,4},{6,5},{7,6},{8,11},{9,8},{10,9... | collective-permute-start | bytes 884744 | tf_op jit(solution)/shard_map/ppermute | solution.py:195
  117.0 0.7 copy-start.7
  117.8 18.8 %copy-start.8 = (bf16[3,192,256]{2,1,0:T(8,128)(2,1)S(1)}, bf16[3,192,256]{2,1,0:T(8,128)(2,1)}, u32[]{:S(2)}) copy-start(bf16[3,192,256]{2,1,0:T(8,128)(2,1)} %copy-done.7) | copy-start | bytes 884740
  117.8 18.3 %collective-permute-start.11 = (bf16[3,192,256]{2,1,0:T(8,128)(2,1)}, bf16[3,192,256]{2,1,0:T(8,128)(2,1)S(1)}, u32[]{:S(2)}, u32[]{:S(2)}) collective-permute-start(bf16[3,192,256]{2,1,0:T(8,128)(2,1)} %get-tuple-element.33), channel_id=1, source_target_pairs={{0,1},{1,2},{2,3},{3,0},{4,5},{5,6},{6,7},{7,4},{8,9},{9,10},{10,1... | collective-permute-start | bytes 884744 | tf_op jit(solution)/shard_map/ppermute | solution.py:192
  119.8 16.2 %collective-permute-start.12 = (bf16[3,192,256]{2,1,0:T(8,128)(2,1)}, bf16[3,192,256]{2,1,0:T(8,128)(2,1)S(1)}, u32[]{:S(2)}, u32[]{:S(2)}) collective-permute-start(bf16[3,192,256]{2,1,0:T(8,128)(2,1)} %get-tuple-element.34), channel_id=1, source_target_pairs={{0,3},{1,0},{2,1},{3,2},{4,7},{5,4},{6,5},{7,6},{8,11},{9,8},{10,9... | collective-permute-start | bytes 884744 | tf_op jit(solution)/shard_map/ppermute | solution.py:195
  125.0 11.0 %collective-permute-start.10 = (bf16[3,192,256]{2,1,0:T(8,128)(2,1)S(1)}, bf16[3,192,256]{2,1,0:T(8,128)(2,1)S(1)}, u32[]{:S(2)}, u32[]{:S(2)}) collective-permute-start(bf16[3,192,256]{2,1,0:T(8,128)(2,1)S(1)} %add_convert_fusion.1), channel_id=1, source_target_pairs={{0,1},{1,2},{2,3},{3,0},{4,5},{5,6},{6,7},{7,4},{8,9},{9,10},{10,1... | collective-permute-start | bytes 884744 | tf_op jit(solution)/shard_map/ppermute | solution.py:192
  127.0 9.5 %collective-permute-start.14 = (bf16[3,192,256]{2,1,0:T(8,128)(2,1)S(1)}, bf16[3,192,256]{2,1,0:T(8,128)(2,1)S(1)}, u32[]{:S(2)}, u32[]{:S(2)}) collective-permute-start(bf16[3,192,256]{2,1,0:T(8,128)(2,1)S(1)} %add_convert_fusion), channel_id=1, source_target_pairs={{0,3},{1,0},{2,1},{3,2},{4,7},{5,4},{6,5},{7,6},{8,11},{9,8},{10,9... | collective-permute-start | bytes 884744 | tf_op jit(solution)/shard_map/ppermute | solution.py:195
  132.2 14.7 %all-to-all-start = ((f32[24,2,128]{2,1,0:T(2,128)}), f32[24,2,128]{2,1,0:T(2,128)S(1)}, u32[]{:S(2)}, u32[]{:S(2)}) async-start(f32[24,2,128]{2,1,0:T(2,128)} %get-tuple-element.21), calls=%async_computation | async-start | bytes 49152 | tf_op jit(solution)/shard_map/all_to_all | solution.py:207
  136.5 42.8 %copy-start.12 = (s32[32,2]{0,1:T(2,128)S(1)}, s32[32,2]{0,1:T(2,128)}, u32[]{:S(2)}) copy-start(s32[32,2]{0,1:T(2,128)} %param.9) | copy-start | bytes 772

commit v2 on v1

--- a/solution.py
+++ b/solution.py
@@ -69,19 +69,18 @@
         logits_ref[n] = lines
 
 
-def spread_kernel(in_ref, lo_ref, hi_ref):
+def spread_kernel(in_ref, out_ref):
     sources, zs = in_ref.shape[0], in_ref.shape[1]
     top = lax.broadcasted_iota(jnp.int32, (8, LANES), 0) < 4
     for z in range(zs):
-        ref, at = (lo_ref, z) if z < zs // 2 else (hi_ref, z - zs // 2)
         for p in range(sources // 2):
             a = in_ref[2 * p, z].astype(f32)
             b = in_ref[2 * p + 1, z].astype(f32)
             ac, bc = a[8:16], b[8:16]
             left = jnp.concatenate([a[0:8], jnp.where(top, ac, pltpu.roll(bc, 4, 0)), b[0:8]], axis=0)
             right = jnp.concatenate([a[16:24], jnp.where(top, pltpu.roll(ac, 4, 0), bc), b[16:24]], axis=0)
-            ref[at, CHUNK * p : CHUNK * (p + 1), :LANES] = left.astype(bf16)
-            ref[at, CHUNK * p : CHUNK * (p + 1), LANES:] = right.astype(bf16)
+            out_ref[z, CHUNK * p : CHUNK * (p + 1), :LANES] = left.astype(bf16)
+            out_ref[z, CHUNK * p : CHUNK * (p + 1), LANES:] = right.astype(bf16)
 
 
 def unspread_kernel(*refs):
@@ -89,11 +88,10 @@
     sources, zs = out_ref.shape[0], out_ref.shape[1]
     top = lax.broadcasted_iota(jnp.int32, (8, LANES), 0) < 4
     for z in range(zs):
-        half, at = (0, z) if z < zs // 2 else (1, z - zs // 2)
         for p in range(sources // 2):
             total = None
-            for n in range(len(ins) // 2):
-                term = ins[2 * n + half][at, CHUNK * p : CHUNK * (p + 1), :].astype(f32)
+            for ref in ins:
+                term = ref[z, CHUNK * p : CHUNK * (p + 1), :].astype(f32)
                 total = term if total is None else total + term
             y, w = total[:, :LANES], total[:, LANES:]
             yc, wc = y[8:16], w[8:16]
@@ -103,24 +101,36 @@
             out_ref[2 * p + 1, z] = b.astype(bf16)
 
 
+def products(blocks, columns, weights, total):
+    xs = 4
+    for block, column in zip(blocks, columns):
+        for z, rows in enumerate(block):
+            share = rows.shape[1]
+            at = pl.ds(pl.multiple_of((z * xs + column) * share, share), share)
+            both = jnp.concatenate([w[at, :] for w in weights], axis=1)
+            term = jnp.dot(rows, both, preferred_element_type=f32)
+            total = term if total is None else total + term
+    return total
+
+
+def gate_up_kernel(places, near_ref, *refs):
+    parts, weights, more = refs[: len(places)], refs[len(places) : len(places) + 4], refs[len(places) + 4 : -1]
+    blocks = [[p[z] for z in range(p.shape[0])] for p in parts]
+    refs[-1][...] = products(blocks, [near_ref[n] for n in places], weights, more[0][...] if more else None)
+
+
 def down(hidden, own_ref, other_ref, column, z, xs):
     at = pl.ds(pl.multiple_of((z * xs + column) * 256, 256), 256)
     both = jnp.concatenate([own_ref[:, at], other_ref[:, at]], axis=0)
     return jnp.dot(hidden, both, preferred_element_type=f32).astype(bf16)
 
 
-def turn_kernel(xs, near_ref, *refs):
-    parts, weights = refs[: 2 * xs], refs[2 * xs : 2 * xs + 4]
-    own_ref, other_ref, hidden_ref, out_lo, out_hi = refs[2 * xs + 4 :]
-    half, _, share = parts[0].shape
-    total = None
-    for n in range(xs):
-        for z in range(2 * half):
-            rows = parts[2 * n + z // half][z % half]
-            at = pl.ds(pl.multiple_of((z * xs + near_ref[n]) * share, share), share)
-            both = jnp.concatenate([w[at, :] for w in weights], axis=1)
-            term = jnp.dot(rows, both, preferred_element_type=f32)
-            total = term if total is None else total + term
+def turn_kernel(xs, near_ref, lo_ref, hi_ref, *refs):
+    weights, total_ref = refs[:4], refs[4]
+    own_ref, other_ref, hidden_ref, out_lo, out_hi = refs[5:]
+    half = lo_ref.shape[0]
+    far = [lo_ref[z] for z in range(half)] + [hi_ref[z] for z in range(half)]
+    total = products([far], [near_ref[xs - 1]], weights, total_ref[...])
     units = total.shape[1] // 2
     gate, up = total[:, :units], total[:, units:]
     hidden = (jax.nn.silu(gate) * up).astype(bf16)
@@ -135,14 +145,9 @@
 
 def down_kernel(xs, near_ref, hidden_ref, own_ref, other_ref, *outs):
     hidden = hidden_ref[...]
-    half = outs[0].shape[0]
-    for n, place in enumerate((1, 2, 0)):
-        for z in range(2 * half):
-            value = down(hidden, own_ref, other_ref, near_ref[place], z, xs)
-            if z < half:
-                outs[2 * n][z] = value
-            else:
-                outs[2 * n + 1][z - half] = value
+    for out, place in zip(outs, (1, 2, 0)):
+        for z in range(out.shape[0]):
+            out[z] = down(hidden, own_ref, other_ref, near_ref[place], z, xs)
 
 
 def merge_kernel(ids_ref, logits_ref, in_ref, out_ref):
@@ -202,74 +207,77 @@
         ),
         10**7,
         10**6,
+        mib=60,
         name="pack",
     )(ids, tokens, router_weight.T)
     partial_logits = lax.all_to_all(logits, ("z", "x"), 0, 0, tiled=True)
     arrived = lax.all_to_all(messages.reshape(far, CHUNK, LANES), FAR, 0, 0, tiled=True)
 
-    part_shape = jax.ShapeDtypeStruct((half, rows, share), bf16)
-    own_lo, own_hi = call(spread_kernel, (part_shape, part_shape), 10**6, 2 * far * CHUNK * LANES * 2, name="spread")(
+    part = jax.ShapeDtypeStruct((half, rows, share), bf16)
+    full = jax.ShapeDtypeStruct((zs, rows, share), bf16)
+    own = call(spread_kernel, full, 10**6, 2 * far * CHUNK * LANES * 2, name="spread")(
         arrived.reshape(sources, zs, CHUNK, LANES)
     )
 
-    left_hi = ahead(own_hi)
-    right_lo = behind(own_lo)
-    left_lo = ahead(own_lo)
-    right_hi = behind(own_hi)
+    left = ahead(own)
+    right = behind(own)
     swap = [(0, 1), (1, 0)]
-    gate_w, up_w, down_w, _ = lax.optimization_barrier((w_gate[0], w_up[0], w_down[0], own_lo))
+    gate_w, up_w, down_w, _ = lax.optimization_barrier((w_gate[0], w_up[0], w_down[0], own))
     gate_o = lax.ppermute(gate_w, "c", swap)
     up_o = lax.ppermute(up_w, "c", swap)
     down_o = lax.ppermute(down_w, "c", swap)
-    far_hi = ahead(left_hi)
-    far_lo = behind(right_lo)
+    far_hi = ahead(left[half:])
+    far_lo = behind(right[:half])
 
     smem = pl.BlockSpec(memory_space=pltpu.SMEM)
     vmem = pl.BlockSpec(memory_space=pltpu.VMEM)
-    flops = 2 * rows * zs * xs * share * 4 * units
-    nbytes = zs * xs * share * units * 8 + 2 * xs * half * rows * share * 2
+    weights = (gate_w, gate_o, up_w, up_o)
+    sums = jax.ShapeDtypeStruct((rows, 4 * units), f32)
+    flops = 2 * rows * zs * share * 4 * units
+    nbytes = zs * share * units * 8 + 2 * half * rows * share * 2
+
+    def gate_up(places, blocks, total):
+        more = () if total is None else (total,)
+        return call(
+            lambda *refs: gate_up_kernel(places, *refs),
+            sums,
+            flops * len(places),
+            nbytes * len(places),
+            mib=16,
+            in_specs=[smem] + [vmem] * (len(places) + 4 + len(more)),
+            name="gate_up",
+        )(near, *blocks, *weights, *more)
+
+    total = gate_up((0,), (own,), None)
+    total = gate_up((1, 2), (right, left), total)
     hidden, opp_lo, opp_hi = call(
         lambda *refs: turn_kernel(xs, *refs),
-        (jax.ShapeDtypeStruct((rows, 2 * units), bf16), part_shape, part_shape),
-        flops,
-        nbytes,
-        mib=24,
-        in_specs=[smem] + [vmem] * (2 * xs + 6),
+        (jax.ShapeDtypeStruct((rows, 2 * units), bf16), part, part),
+        2 * flops,
+        2 * nbytes,
+        mib=20,
+        in_specs=[smem] + [vmem] * 9,
         name="turn",
-    )(
-        near,
-        own_lo,
-        own_hi,
-        right_lo,
-        right_hi,
-        left_lo,
-        left_hi,
-        far_lo,
-        far_hi,
-        gate_w,
-        gate_o,
-        up_w,
-        up_o,
-        down_w,
-        down_o,
-    )
-
-    from_left_lo = ahead(opp_lo)
-    from_right_hi = behind(opp_hi)
-    outs = call(
+    )(near, far_lo, far_hi, *weights, total, down_w, down_o)
+
+    from_left = ahead(opp_lo)
+    from_right = behind(opp_hi)
+    to_next, to_prev, mine = call(
         lambda *refs: down_kernel(xs, *refs),
-        (part_shape,) * 6,
-        flops // 2,
-        nbytes // 2,
+        (full,) * 3,
+        2 * flops,
+        2 * nbytes,
         mib=12,
         in_specs=[smem] + [vmem] * 3,
         name="down",
     )(near, hidden, down_w, down_o)
-    next_lo, next_hi, prev_lo, prev_hi, mine_lo, mine_hi = outs
-    c_hi = ahead(next_hi)
-    e_lo = behind(prev_lo)
-    c_lo = ahead((next_lo.astype(f32) + from_left_lo.astype(f32)).astype(bf16))
-    e_hi = behind((prev_hi.astype(f32) + from_right_hi.astype(f32)).astype(bf16))
+
+    def add(whole, at, term):
+        value = (whole[at].astype(f32) + term.astype(f32)).astype(bf16)
+        return whole.at[at].set(value)
+
+    from_prev = ahead(add(to_next, slice(0, half), from_left))
+    from_next = behind(add(to_prev, slice(half, zs), from_right))
 
     leaving = call(
         unspread_kernel,
@@ -277,7 +285,7 @@
         10**7,
         4 * far * CHUNK * LANES * 2,
         name="unspread",
-    )(mine_lo, mine_hi, c_lo, c_hi, e_lo, e_hi)
+    )(mine, from_prev, from_next)
     back = lax.all_to_all(leaving.reshape(far, CHUNK, LANES), FAR, 0, 0, tiled=True)
     return call(
         merge_kernel,

time: 181 us -> 169 us (0.934)
  starting transfers between devices: 52.9 us -> 38.3 us
  local copies, waits for them, and re-layouts: 10.8 us -> 1.98 us
  Pallas kernels: 8.21 us -> 15.2 us
  waiting for transfers between devices: 24.4 us -> 27.2 us
    ppermute x6 -> x4, waiting for transfers between devices: 1.66 us -> 13.1 us  [behind(): return lax.ppermute(v, 'x', backward)]
    unnamed x32 -> x10, local copies, waits for them, and re-layouts: 10.8 us -> 0.02 us
    ppermute x6 -> x4, starting transfers between devices: 29.5 us -> 20.5 us  [behind(): return lax.ppermute(v, 'x', backward)]
    pallas_call x2 -> x4, Pallas kernels: 1.82 us -> 8.72 us  [the longest x2 5.7 us: gate_up(): call(lambda *refs: gate_up_kernel(places, *refs), sums, flops * len(place...]
    all_to_all x1, waiting for transfers between devices: 10.1 us -> 4.05 us  [block(): partial_logits = lax.all_to_all(logits, ('z', 'x'), 0, 0, tiled=True)]
    ppermute x6 -> x4, starting transfers between devices: 13.4 us -> 7.68 us  [ahead(): return lax.ppermute(v, 'x', forward)]
    ppermute x6 -> x4, waiting for transfers between devices: 12.7 us -> 10.1 us  [ahead(): return lax.ppermute(v, 'x', forward)]
    slice x0 -> x2, local copies, waits for them, and re-layouts: none -> 1.96 us  [the longest x1 0.98 us: block(): far_hi = ahead(left[half:])]
  transfers between devices with their start and end apart: 16 -> 12, of which waited for: 6 -> 6; matrix products, arithmetic and copies ran while one was open for 0% -> 1% of each run, Pallas kernels for 1% -> 5%
where the time goes in v2:
time: 169 us; the launch traced here: 168 us
  blocking collectives  84.8 us (50%)
  starting transfers between devices  38.3 us (23%)
  waiting for transfers between devices  27.2 us (16%)
  Pallas kernels  15.2 us (9%)
  local copies, waits for them, and re-layouts  1.98 us (1%)
    all_to_all x1, blocking collectives, block(): lax.all_to_all(messages.reshape(far, CHUNK, LANES), FAR, 0, 0, tiled=True)  51.5 us
    all_to_all x1, blocking collectives, block(): lax.all_to_all(leaving.reshape(far, CHUNK, LANES), FAR, 0, 0, tiled=True)  33.3 us
    ppermute x4, starting transfers between devices, behind(): return lax.ppermute(v, 'x', backward)  20.5 us
    ppermute x4, waiting for transfers between devices, behind(): return lax.ppermute(v, 'x', backward)  13.1 us
    ppermute x4, waiting for transfers between devices, ahead(): return lax.ppermute(v, 'x', forward)  10.1 us
    ppermute x4, starting transfers between devices, ahead(): return lax.ppermute(v, 'x', forward)  7.68 us
    pallas_call x2, Pallas kernels, gate_up(): call(lambda *refs: gate_up_kernel(places, *refs), sums, flops * len(place...  5.7 us
    all_to_all x1, waiting for transfers between devices, block(): partial_logits = lax.all_to_all(logits, ('z', 'x'), 0, 0, tiled=True)  4.05 us
  transfers between devices with their start and end apart: 12, of which 6 were waited for; matrix products, arithmetic and copies ran while one was open for 1% of the time, Pallas kernels for 5%

profile of v2, /device:TPU:8, one launch (start us, length us, event | category | flops | bytes accessed | tf_op | source)
XLA Modules:
  0.0 168.0 jit_solution(9141743855514613137)
XLA Ops:
  0.0 2.0 %pack.1 = (bf16[8,12,24,128]{3,2,1,0:T(8,128)(2,1)}, f32[24,2,128]{2,1,0:T(2,128)}) custom-call(s32[2,32]{1,0:T(2,128)} %bitcast.23, bf16[32,256]{1,0:T(8,128)(2,1)} %tokens_ref.1, bf16[8,256]{1,0:T(8,128)(2,1)} %bitcast.26), custom_call_target="tpu_custom_call" | custom-call | flops 10000000 | bytes 1000000 | tf_op jit(solution)/shard_map/pack/pallas_call | solution.py:202
  2.0 51.5 %all_to_all.15 = bf16[96,24,128]{2,1,0:T(8,128)(2,1)S(1)} all-to-all(bf16[96,24,128]{2,1,0:T(8,128)(2,1)} %bitcast.25), channel_id=1, replica_groups=mesh['zh'=2,'yq'=4,'yp'=2,'c'=2,'z'=6,'x'=4] {'zh','yq','yp','z'}, dimensions={0} | all-to-all | bytes 1179648 | tf_op jit(solution)/shard_map/all_to_all | solution.py:214
  53.5 0.9 spread.1.refs_1_
  54.4 1.9 %collective-permute-start.4 = (bf16[6144,128]{1,0:T(8,128)(2,1)S(1)}, bf16[6144,128]{1,0:T(8,128)(2,1)}, u32[]{:S(2)}, u32[]{:S(2)}) collective-permute-start(bf16[6144,128]{1,0:T(8,128)(2,1)S(1)} %bitcast.9), channel_id=1, source_target_pairs={{0,24},{24,0},{1,25},{25,1},{2,26},{26,2},{3,27},{27,3},{4,28},{28... | collective-permute-start | bytes 4718600 | tf_op jit(solution)/shard_map/ppermute | solution.py:226
  56.3 2.4 %collective-permute-start.5 = (bf16[6144,128]{1,0:T(8,128)(2,1)}, bf16[6144,128]{1,0:T(8,128)(2,1)}, u32[]{:S(2)}, u32[]{:S(2)}) collective-permute-start(bf16[6144,128]{1,0:T(8,128)(2,1)} %bitcast.13), channel_id=1, source_target_pairs={{0,24},{24,0},{1,25},{25,1},{2,26},{26,2},{3,27},{27,3},{4,28},{28... | collective-permute-start | bytes 4718600 | tf_op jit(solution)/shard_map/ppermute | solution.py:227
  58.8 1.9 %collective-permute-start.6 = (bf16[128,6144]{1,0:T(8,128)(2,1)}, bf16[128,6144]{1,0:T(8,128)(2,1)}, u32[]{:S(2)}, u32[]{:S(2)}) collective-permute-start(bf16[128,6144]{1,0:T(8,128)(2,1)} %bitcast.17), channel_id=1, source_target_pairs={{0,24},{24,0},{1,25},{25,1},{2,26},{26,2},{3,27},{27,3},{4,28},{28... | collective-permute-start | bytes 4718600 | tf_op jit(solution)/shard_map/ppermute | solution.py:228
  60.7 4.7 %collective-permute-start = (bf16[6,192,256]{2,1,0:T(8,128)(2,1)}, bf16[6,192,256]{2,1,0:T(8,128)(2,1)}, u32[]{:S(2)}, u32[]{:S(2)}) collective-permute-start(bf16[6,192,256]{2,1,0:T(8,128)(2,1)} %spread.1.refs_1_), channel_id=1, source_target_pairs={{0,3},{1,0},{2,1},{3,2},{4,7},{5,4},{6,5},{7,6},{8,11},{9,8},{10,9... | collective-permute-start | bytes 1769480 | tf_op jit(solution)/shard_map/ppermute | solution.py:200
  65.4 1.9 %collective-permute-start.2 = (bf16[6,192,256]{2,1,0:T(8,128)(2,1)}, bf16[6,192,256]{2,1,0:T(8,128)(2,1)}, u32[]{:S(2)}, u32[]{:S(2)}) collective-permute-start(bf16[6,192,256]{2,1,0:T(8,128)(2,1)} %spread.1.refs_1_), channel_id=1, source_target_pairs={{0,1},{1,2},{2,3},{3,0},{4,5},{5,6},{6,7},{7,4},{8,9},{9,10},{10,1... | collective-permute-start | bytes 1769480 | tf_op jit(solution)/shard_map/ppermute | solution.py:197
  67.3 11.6 %collective-permute-done.refs_1_ = bf16[6,192,256]{2,1,0:T(8,128)(2,1)} collective-permute-done((bf16[6,192,256]{2,1,0:T(8,128)(2,1)}, bf16[6,192,256]{2,1,0:T(8,128)(2,1)}, u32[]{:S(2)}, u32[]{:S(2)}) %collective-permute-start) | collective-permute-done | bytes 589856 | tf_op jit(solution)/shard_map/ppermute | solution.py:200
  78.9 1.0 slice.60
  79.9 5.6 %collective-permute-start.1 = (bf16[3,192,256]{2,1,0:T(8,128)(2,1)S(1)}, bf16[3,192,256]{2,1,0:T(8,128)(2,1)S(1)}, u32[]{:S(2)}, u32[]{:S(2)}) collective-permute-start(bf16[3,192,256]{2,1,0:T(8,128)(2,1)S(1)} %slice.60), channel_id=1, source_target_pairs={{0,3},{1,0},{2,1},{3,2},{4,7},{5,4},{6,5},{7,6},{8,11},{9,8},{10,9... | collective-permute-start | bytes 884744 | tf_op jit(solution)/shard_map/ppermute | solution.py:200
  85.5 1.0 slice.61
  86.5 1.9 %collective-permute-start.3 = (bf16[3,192,256]{2,1,0:T(8,128)(2,1)S(1)}, bf16[3,192,256]{2,1,0:T(8,128)(2,1)S(1)}, u32[]{:S(2)}, u32[]{:S(2)}) collective-permute-start(bf16[3,192,256]{2,1,0:T(8,128)(2,1)S(1)} %slice.61), channel_id=1, source_target_pairs={{0,1},{1,2},{2,3},{3,0},{4,5},{5,6},{6,7},{7,4},{8,9},{9,10},{10,1... | collective-permute-start | bytes 884744 | tf_op jit(solution)/shard_map/ppermute | solution.py:197
  88.5 2.5 %gate_up.2.refs_7_ = f32[192,512]{1,0:T(8,128)S(1)} custom-call(s32[4]{0:T(128)S(1)} %add_and_fusion.refs_0_, bf16[6,192,256]{2,1,0:T(8,128)(2,1)} %spread.1.refs_1_, bf16[6144,128]{1,0:T(8,128)(2,1)S(1)} %bitcast.10, bf16[6144,128]{1,0:T(8,128)(2,1)} %collective-permute-done.4.refs_3_.refs_4_, bf16[6144,128]{1,0:T(8,128)(2,1)S(1)} %bitcast.14, ...), custom_call_target="tpu_custom_call" | custom-call | flops 301989888 | bytes 2162688 | tf_op jit(solution)/shard_map/gate_up/pallas_call | solution.py:241
  91.1 3.2 %gate_up.3.refs_7_ = f32[192,512]{1,0:T(8,128)S(1)} custom-call(s32[4]{0:T(128)S(1)} %add_and_fusion.refs_0_, bf16[6,192,256]{2,1,0:T(8,128)(2,1)} %collective-permute-done.refs_1_, bf16[6,192,256]{2,1,0:T(8,128)(2,1)} %collective-permute-done.2.refs_2_, bf16[6144,128]{1,0:T(8,128)(2,1)S(1)} %bitcast.11, ...), custom_call_target="tpu_custom_call" | custom-call | flops 603979776 | bytes 4325376 | tf_op jit(solution)/shard_map/gate_up/pallas_call | solution.py:241
  94.2 3.7 %collective-permute-done.3.refs_2_ = bf16[3,192,256]{2,1,0:T(8,128)(2,1)S(1)} collective-permute-done((bf16[3,192,256]{2,1,0:T(8,128)(2,1)S(1)}, bf16[3,192,256]{2,1,0:T(8,128)(2,1)S(1)}, u32[]{:S(2)}, u32[]{:S(2)}) %collective-permute-start.3) | collective-permute-done | bytes 294944 | tf_op jit(solution)/shard_map/ppermute | solution.py:197
  97.9 3.1 %turn.1 = (bf16[192,256]{1,0:T(8,128)(2,1)S(1)}, bf16[3,192,256]{2,1,0:T(8,128)(2,1)S(1)}, bf16[3,192,256]{2,1,0:T(8,128)(2,1)S(1)}) custom-call(s32[4]{0:T(128)S(1)} %add_and_fusion.refs_0_, bf16[3,192,256]{2,1,0:T(8,128)(2,1)S(1)} %collective-permute-done.1.refs_1_, bf16[3,192,256]{2,1,0:T(8,128)(2,1)S(1)} %collective-permute-done.3.refs_2_, ...), custom_call_target="tpu_custom_call" | custom-call | flops 603979776 | bytes 4325376 | tf_op jit(solution)/shard_map/turn/pallas_call | solution.py:253
  101.0 1.9 %collective-permute-start.7 = (bf16[3,192,256]{2,1,0:T(8,128)(2,1)S(1)}, bf16[3,192,256]{2,1,0:T(8,128)(2,1)S(1)}, u32[]{:S(2)}, u32[]{:S(2)}) collective-permute-start(bf16[3,192,256]{2,1,0:T(8,128)(2,1)S(1)} %get-tuple-element.48), channel_id=1, source_target_pairs={{0,1},{1,2},{2,3},{3,0},{4,5},{5,6},{6,7},{7,4},{8,9},{9,10},{10,1... | collective-permute-start | bytes 884744 | tf_op jit(solution)/shard_map/ppermute | solution.py:197
  102.9 5.1 %collective-permute-start.9 = (bf16[3,192,256]{2,1,0:T(8,128)(2,1)S(1)}, bf16[3,192,256]{2,1,0:T(8,128)(2,1)S(1)}, u32[]{:S(2)}, u32[]{:S(2)}) collective-permute-start(bf16[3,192,256]{2,1,0:T(8,128)(2,1)S(1)} %get-tuple-element.50), channel_id=1, source_target_pairs={{0,3},{1,0},{2,1},{3,2},{4,7},{5,4},{6,5},{7,6},{8,11},{9,8},{10,9... | collective-permute-start | bytes 884744 | tf_op jit(solution)/shard_map/ppermute | solution.py:200
  108.1 2.1 %down.1 = (bf16[6,192,256]{2,1,0:T(8,128)(2,1)S(1)}, bf16[6,192,256]{2,1,0:T(8,128)(2,1)S(1)}, bf16[6,192,256]{2,1,0:T(8,128)(2,1)S(1)}) custom-call(s32[4]{0:T(128)S(1)} %add_and_fusion.refs_0_, bf16[192,256]{1,0:T(8,128)(2,1)S(1)} %get-tuple-element.45.refs_1_, bf16[128,6144]{1,0:T(8,128)(2,1)S(1)} %bitcast.19, ...), custom_call_target="tpu_custom_call" | custom-call | flops 603979776 | bytes 4325376 | tf_op jit(solution)/shard_map/down/pallas_call | solution.py:265
  110.2 1.4 collective-permute-done.7
  111.5 0.1 fusion
  111.7 1.9 %collective-permute-start.8 = (bf16[6,192,256]{2,1,0:T(8,128)(2,1)S(1)}, bf16[6,192,256]{2,1,0:T(8,128)(2,1)S(1)}, u32[]{:S(2)}, u32[]{:S(2)}) collective-permute-start(bf16[6,192,256]{2,1,0:T(8,128)(2,1)S(1)} %fusion), channel_id=1, source_target_pairs={{0,1},{1,2},{2,3},{3,0},{4,5},{5,6},{6,7},{7,4},{8,9},{9,10},{10,1... | collective-permute-start | bytes 1769480 | tf_op jit(solution)/shard_map/ppermute | solution.py:197
  113.6 0.1 fusion.1
  113.7 5.1 %collective-permute-start.10 = (bf16[6,192,256]{2,1,0:T(8,128)(2,1)S(1)}, bf16[6,192,256]{2,1,0:T(8,128)(2,1)S(1)}, u32[]{:S(2)}, u32[]{:S(2)}) collective-permute-start(bf16[6,192,256]{2,1,0:T(8,128)(2,1)S(1)} %fusion.1), channel_id=1, source_target_pairs={{0,3},{1,0},{2,1},{3,2},{4,7},{5,4},{6,5},{7,6},{8,11},{9,8},{10,9... | collective-permute-start | bytes 1769480 | tf_op jit(solution)/shard_map/ppermute | solution.py:200
  118.9 3.8 %all-to-all-start = ((f32[24,2,128]{2,1,0:T(2,128)}), f32[24,2,128]{2,1,0:T(2,128)S(1)}, u32[]{:S(2)}, u32[]{:S(2)}) async-start(f32[24,2,128]{2,1,0:T(2,128)} %get-tuple-element.40), calls=%async_computation | async-start | bytes 49152 | tf_op jit(solution)/shard_map/all_to_all | solution.py:213
  122.7 5.0 %collective-permute-done.8.refs_1_ = bf16[6,192,256]{2,1,0:T(8,128)(2,1)S(1)} collective-permute-done((bf16[6,192,256]{2,1,0:T(8,128)(2,1)S(1)}, bf16[6,192,256]{2,1,0:T(8,128)(2,1)S(1)}, u32[]{:S(2)}, u32[]{:S(2)}) %collective-permute-start.8) | collective-permute-done | bytes 589856 | tf_op jit(solution)/shard_map/ppermute | solution.py:197
  127.8 1.5 collective-permute-done.10.refs_2_
  129.2 0.2 unspread.1
  129.5 4.1 %all-to-all-done.logits_ref = f32[24,2,128]{2,1,0:T(2,128)S(1)} async-done(((f32[24,2,128]{2,1,0:T(2,128)}), f32[24,2,128]{2,1,0:T(2,128)S(1)}, u32[]{:S(2)}, u32[]{:S(2)}) %all-to-all-start) | async-done | bytes 24608 | tf_op jit(solution)/shard_map/all_to_all | solution.py:213
  133.5 33.3 %all_to_all.16 = bf16[96,24,128]{2,1,0:T(8,128)(2,1)S(1)} all-to-all(bf16[96,24,128]{2,1,0:T(8,128)(2,1)S(1)} %bitcast.22), channel_id=1, replica_groups=mesh['zh'=2,'yq'=4,'yp'=2,'c'=2,'z'=6,'x'=4] {'zh','yq','yp','z'}, dimensions={0} | all-to-all | bytes 1179648 | tf_op jit(solution)/shard_map/all_to_all | solution.py:289
  166.9 1.1 merge.1
  (17 shorter events, 0.0 us)
Async XLA Ops:
  0.0 54.4 %copy-start = (bf16[1,6144,128]{2,1,0:T(8,128)(2,1)S(1)}, bf16[1,6144,128]{2,1,0:T(8,128)(2,1)}, u32[]{:S(2)}) copy-start(bf16[1,6144,128]{2,1,0:T(8,128)(2,1)} %param.14) | copy-start | bytes 4718596
  2.0 86.4 %copy-start.4 = (s32[4]{0:T(128)S(1)}, s32[4]{0:T(128)}, u32[]{:S(2)}) copy-start(s32[4]{0:T(128)} %constant.62.clone) | copy-start | bytes 52
  2.0 86.5 %copy-start.1 = (bf16[1,6144,128]{2,1,0:T(8,128)(2,1)S(1)}, bf16[1,6144,128]{2,1,0:T(8,128)(2,1)}, u32[]{:S(2)}) copy-start(bf16[1,6144,128]{2,1,0:T(8,128)(2,1)} %param.15) | copy-start | bytes 4718596
  54.4 34.0 %collective-permute-start.4 = (bf16[6144,128]{1,0:T(8,128)(2,1)S(1)}, bf16[6144,128]{1,0:T(8,128)(2,1)}, u32[]{:S(2)}, u32[]{:S(2)}) collective-permute-start(bf16[6144,128]{1,0:T(8,128)(2,1)S(1)} %bitcast.9), channel_id=1, source_target_pairs={{0,24},{24,0},{1,25},{25,1},{2,26},{26,2},{3,27},{27,3},{4,28},{28... | collective-permute-start | bytes 4718600 | tf_op jit(solution)/shard_map/ppermute | solution.py:226
  56.3 32.1 %collective-permute-start.5 = (bf16[6144,128]{1,0:T(8,128)(2,1)}, bf16[6144,128]{1,0:T(8,128)(2,1)}, u32[]{:S(2)}, u32[]{:S(2)}) collective-permute-start(bf16[6144,128]{1,0:T(8,128)(2,1)} %bitcast.13), channel_id=1, source_target_pairs={{0,24},{24,0},{1,25},{25,1},{2,26},{26,2},{3,27},{27,3},{4,28},{28... | collective-permute-start | bytes 4718600 | tf_op jit(solution)/shard_map/ppermute | solution.py:227
  58.8 39.1 %collective-permute-start.6 = (bf16[128,6144]{1,0:T(8,128)(2,1)}, bf16[128,6144]{1,0:T(8,128)(2,1)}, u32[]{:S(2)}, u32[]{:S(2)}) collective-permute-start(bf16[128,6144]{1,0:T(8,128)(2,1)} %bitcast.17), channel_id=1, source_target_pairs={{0,24},{24,0},{1,25},{25,1},{2,26},{26,2},{3,27},{27,3},{4,28},{28... | collective-permute-start | bytes 4718600 | tf_op jit(solution)/shard_map/ppermute | solution.py:228
  60.7 18.2 %collective-permute-start = (bf16[6,192,256]{2,1,0:T(8,128)(2,1)}, bf16[6,192,256]{2,1,0:T(8,128)(2,1)}, u32[]{:S(2)}, u32[]{:S(2)}) collective-permute-start(bf16[6,192,256]{2,1,0:T(8,128)(2,1)} %spread.1.refs_1_), channel_id=1, source_target_pairs={{0,3},{1,0},{2,1},{3,2},{4,7},{5,4},{6,5},{7,6},{8,11},{9,8},{10,9... | collective-permute-start | bytes 1769480 | tf_op jit(solution)/shard_map/ppermute | solution.py:200
  65.4 20.1 %collective-permute-start.2 = (bf16[6,192,256]{2,1,0:T(8,128)(2,1)}, bf16[6,192,256]{2,1,0:T(8,128)(2,1)}, u32[]{:S(2)}, u32[]{:S(2)}) collective-permute-start(bf16[6,192,256]{2,1,0:T(8,128)(2,1)} %spread.1.refs_1_), channel_id=1, source_target_pairs={{0,1},{1,2},{2,3},{3,0},{4,5},{5,6},{6,7},{7,4},{8,9},{9,10},{10,1... | collective-permute-start | bytes 1769480 | tf_op jit(solution)/shard_map/ppermute | solution.py:197
  79.9 14.3 %collective-permute-start.1 = (bf16[3,192,256]{2,1,0:T(8,128)(2,1)S(1)}, bf16[3,192,256]{2,1,0:T(8,128)(2,1)S(1)}, u32[]{:S(2)}, u32[]{:S(2)}) collective-permute-start(bf16[3,192,256]{2,1,0:T(8,128)(2,1)S(1)} %slice.60), channel_id=1, source_target_pairs={{0,3},{1,0},{2,1},{3,2},{4,7},{5,4},{6,5},{7,6},{8,11},{9,8},{10,9... | collective-permute-start | bytes 884744 | tf_op jit(solution)/shard_map/ppermute | solution.py:200
  86.5 11.4 %collective-permute-start.3 = (bf16[3,192,256]{2,1,0:T(8,128)(2,1)S(1)}, bf16[3,192,256]{2,1,0:T(8,128)(2,1)S(1)}, u32[]{:S(2)}, u32[]{:S(2)}) collective-permute-start(bf16[3,192,256]{2,1,0:T(8,128)(2,1)S(1)} %slice.61), channel_id=1, source_target_pairs={{0,1},{1,2},{2,3},{3,0},{4,5},{5,6},{6,7},{7,4},{8,9},{9,10},{10,1... | collective-permute-start | bytes 884744 | tf_op jit(solution)/shard_map/ppermute | solution.py:197
  91.0 6.8 %copy-start.2 = (bf16[1,128,6144]{2,1,0:T(8,128)(2,1)S(1)}, bf16[1,128,6144]{2,1,0:T(8,128)(2,1)}, u32[]{:S(2)}) copy-start(bf16[1,128,6144]{2,1,0:T(8,128)(2,1)} %param.16) | copy-start | bytes 4718596
  101.0 10.5 %collective-permute-start.7 = (bf16[3,192,256]{2,1,0:T(8,128)(2,1)S(1)}, bf16[3,192,256]{2,1,0:T(8,128)(2,1)S(1)}, u32[]{:S(2)}, u32[]{:S(2)}) collective-permute-start(bf16[3,192,256]{2,1,0:T(8,128)(2,1)S(1)} %get-tuple-element.48), channel_id=1, source_target_pairs={{0,1},{1,2},{2,3},{3,0},{4,5},{5,6},{6,7},{7,4},{8,9},{9,10},{10,1... | collective-permute-start | bytes 884744 | tf_op jit(solution)/shard_map/ppermute | solution.py:197
  102.9 10.7 %collective-permute-start.9 = (bf16[3,192,256]{2,1,0:T(8,128)(2,1)S(1)}, bf16[3,192,256]{2,1,0:T(8,128)(2,1)S(1)}, u32[]{:S(2)}, u32[]{:S(2)}) collective-permute-start(bf16[3,192,256]{2,1,0:T(8,128)(2,1)S(1)} %get-tuple-element.50), channel_id=1, source_target_pairs={{0,3},{1,0},{2,1},{3,2},{4,7},{5,4},{6,5},{7,6},{8,11},{9,8},{10,9... | collective-permute-start | bytes 884744 | tf_op jit(solution)/shard_map/ppermute | solution.py:200
  111.7 16.1 %collective-permute-start.8 = (bf16[6,192,256]{2,1,0:T(8,128)(2,1)S(1)}, bf16[6,192,256]{2,1,0:T(8,128)(2,1)S(1)}, u32[]{:S(2)}, u32[]{:S(2)}) collective-permute-start(bf16[6,192,256]{2,1,0:T(8,128)(2,1)S(1)} %fusion), channel_id=1, source_target_pairs={{0,1},{1,2},{2,3},{3,0},{4,5},{5,6},{6,7},{7,4},{8,9},{9,10},{10,1... | collective-permute-start | bytes 1769480 | tf_op jit(solution)/shard_map/ppermute | solution.py:197
  113.7 15.5 %collective-permute-start.10 = (bf16[6,192,256]{2,1,0:T(8,128)(2,1)S(1)}, bf16[6,192,256]{2,1,0:T(8,128)(2,1)S(1)}, u32[]{:S(2)}, u32[]{:S(2)}) collective-permute-start(bf16[6,192,256]{2,1,0:T(8,128)(2,1)S(1)} %fusion.1), channel_id=1, source_target_pairs={{0,3},{1,0},{2,1},{3,2},{4,7},{5,4},{6,5},{7,6},{8,11},{9,8},{10,9... | collective-permute-start | bytes 1769480 | tf_op jit(solution)/shard_map/ppermute | solution.py:200
  118.9 14.6 %all-to-all-start = ((f32[24,2,128]{2,1,0:T(2,128)}), f32[24,2,128]{2,1,0:T(2,128)S(1)}, u32[]{:S(2)}, u32[]{:S(2)}) async-start(f32[24,2,128]{2,1,0:T(2,128)} %get-tuple-element.40), calls=%async_computation | async-start | bytes 49152 | tf_op jit(solution)/shard_map/all_to_all | solution.py:213
  129.2 37.6 %copy-start.3 = (s32[32,2]{0,1:T(2,128)S(1)}, s32[32,2]{0,1:T(2,128)}, u32[]{:S(2)}) copy-start(s32[32,2]{0,1:T(2,128)} %param.13) | copy-start | bytes 772

commit v3 on v2

--- a/solution.py
+++ b/solution.py
@@ -125,29 +125,17 @@
     return jnp.dot(hidden, both, preferred_element_type=f32).astype(bf16)
 
 
-def turn_kernel(xs, near_ref, lo_ref, hi_ref, *refs):
+def turn_kernel(xs, near_ref, far_ref, *refs):
     weights, total_ref = refs[:4], refs[4]
-    own_ref, other_ref, hidden_ref, out_lo, out_hi = refs[5:]
-    half = lo_ref.shape[0]
-    far = [lo_ref[z] for z in range(half)] + [hi_ref[z] for z in range(half)]
+    own_ref, other_ref, *outs = refs[5:]
+    far = [far_ref[z] for z in range(far_ref.shape[0])]
     total = products([far], [near_ref[xs - 1]], weights, total_ref[...])
     units = total.shape[1] // 2
     gate, up = total[:, :units], total[:, units:]
     hidden = (jax.nn.silu(gate) * up).astype(bf16)
-    hidden_ref[...] = hidden
-    for z in range(2 * half):
-        value = down(hidden, own_ref, other_ref, near_ref[xs - 1], z, xs)
-        if z < half:
-            out_lo[z] = value
-        else:
-            out_hi[z - half] = value
-
-
-def down_kernel(xs, near_ref, hidden_ref, own_ref, other_ref, *outs):
-    hidden = hidden_ref[...]
-    for out, place in zip(outs, (1, 2, 0)):
+    for n, out in enumerate(outs):
         for z in range(out.shape[0]):
-            out[z] = down(hidden, own_ref, other_ref, near_ref[place], z, xs)
+            out[z] = down(hidden, own_ref, other_ref, near_ref[n], z, xs)
 
 
 def merge_kernel(ids_ref, logits_ref, in_ref, out_ref):
@@ -184,8 +172,7 @@
     sources = experts * 2
     far = sources * zs
     rows = sources * CAP
-    half = zs // 2
-    assert xs == 4 and share == 256 and zs % 2 == 0
+    assert xs == 4 and share == 256
     units = w_gate.shape[2]
     ids = expert_ids.T
     me = lax.axis_index("x")
@@ -195,6 +182,9 @@
 
     def ahead(v):
         return lax.ppermute(v, "x", forward)
+
+    def across(v):
+        return lax.ppermute(v, "x", [(i, (i + 2) % xs) for i in range(xs)])
 
     def behind(v):
         return lax.ppermute(v, "x", backward)
@@ -213,7 +203,6 @@
     partial_logits = lax.all_to_all(logits, ("z", "x"), 0, 0, tiled=True)
     arrived = lax.all_to_all(messages.reshape(far, CHUNK, LANES), FAR, 0, 0, tiled=True)
 
-    part = jax.ShapeDtypeStruct((half, rows, share), bf16)
     full = jax.ShapeDtypeStruct((zs, rows, share), bf16)
     own = call(spread_kernel, full, 10**6, 2 * far * CHUNK * LANES * 2, name="spread")(
         arrived.reshape(sources, zs, CHUNK, LANES)
@@ -221,20 +210,19 @@
 
     left = ahead(own)
     right = behind(own)
+    opposite = across(own)
     swap = [(0, 1), (1, 0)]
     gate_w, up_w, down_w, _ = lax.optimization_barrier((w_gate[0], w_up[0], w_down[0], own))
     gate_o = lax.ppermute(gate_w, "c", swap)
     up_o = lax.ppermute(up_w, "c", swap)
     down_o = lax.ppermute(down_w, "c", swap)
-    far_hi = ahead(left[half:])
-    far_lo = behind(right[:half])
 
     smem = pl.BlockSpec(memory_space=pltpu.SMEM)
     vmem = pl.BlockSpec(memory_space=pltpu.VMEM)
     weights = (gate_w, gate_o, up_w, up_o)
     sums = jax.ShapeDtypeStruct((rows, 4 * units), f32)
     flops = 2 * rows * zs * share * 4 * units
-    nbytes = zs * share * units * 8 + 2 * half * rows * share * 2
+    nbytes = zs * share * units * 8 + zs * rows * share * 2
 
     def gate_up(places, blocks, total):
         more = () if total is None else (total,)
@@ -250,34 +238,19 @@
 
     total = gate_up((0,), (own,), None)
     total = gate_up((1, 2), (right, left), total)
-    hidden, opp_lo, opp_hi = call(
+    mine, to_next, to_prev, to_far = call(
         lambda *refs: turn_kernel(xs, *refs),
-        (jax.ShapeDtypeStruct((rows, 2 * units), bf16), part, part),
-        2 * flops,
-        2 * nbytes,
-        mib=20,
-        in_specs=[smem] + [vmem] * 9,
+        (full,) * xs,
+        3 * flops,
+        3 * nbytes,
+        mib=24,
+        in_specs=[smem] + [vmem] * 8,
         name="turn",
-    )(near, far_lo, far_hi, *weights, total, down_w, down_o)
-
-    from_left = ahead(opp_lo)
-    from_right = behind(opp_hi)
-    to_next, to_prev, mine = call(
-        lambda *refs: down_kernel(xs, *refs),
-        (full,) * 3,
-        2 * flops,
-        2 * nbytes,
-        mib=12,
-        in_specs=[smem] + [vmem] * 3,
-        name="down",
-    )(near, hidden, down_w, down_o)
-
-    def add(whole, at, term):
-        value = (whole[at].astype(f32) + term.astype(f32)).astype(bf16)
-        return whole.at[at].set(value)
-
-    from_prev = ahead(add(to_next, slice(0, half), from_left))
-    from_next = behind(add(to_prev, slice(half, zs), from_right))
+    )(near, opposite, *weights, total, down_w, down_o)
+
+    from_far = across(to_far)
+    from_prev = ahead(to_next)
+    from_next = behind(to_prev)
 
     leaving = call(
         unspread_kernel,
@@ -285,7 +258,7 @@
         10**7,
         4 * far * CHUNK * LANES * 2,
         name="unspread",
-    )(mine, from_prev, from_next)
+    )(mine, from_prev, from_next, from_far)
     back = lax.all_to_all(leaving.reshape(far, CHUNK, LANES), FAR, 0, 0, tiled=True)
     return call(
         merge_kernel,

time: 169 us -> 170 us (level)
  the two profiles are of different devices: /device:TPU:8 before, /device:TPU:6 now
where the time goes in v3:
time: 170 us; the launch traced here: 169 us
  blocking collectives  85.7 us (50%)
  waiting for transfers between devices  36.1 us (21%)
  starting transfers between devices  30.7 us (18%)
  Pallas kernels  13.4 us (8%)
  local copies, waits for them, and re-layouts  3.32 us (2%)
    all_to_all x1, blocking collectives, block(): lax.all_to_all(messages.reshape(far, CHUNK, LANES), FAR, 0, 0, tiled=True)  52.1 us
    all_to_all x1, blocking collectives, block(): lax.all_to_all(leaving.reshape(far, CHUNK, LANES), FAR, 0, 0, tiled=True)  33.6 us
    ppermute x2, waiting for transfers between devices, behind(): return lax.ppermute(v, 'x', backward)  17 us
    ppermute x2, waiting for transfers between devices, across(): return lax.ppermute(v, 'x', [(i, (i + 2) % xs) for i in range(xs)])  10.5 us
    ppermute x2, waiting for transfers between devices, ahead(): return lax.ppermute(v, 'x', forward)  8.61 us
    all_to_all x1, starting transfers between devices, block(): partial_logits = lax.all_to_all(logits, ('z', 'x'), 0, 0, tiled=True)  7.53 us
    ppermute x2, starting transfers between devices, behind(): return lax.ppermute(v, 'x', backward)  7.38 us
    ppermute x2, starting transfers between devices, across(): return lax.ppermute(v, 'x', [(i, (i + 2) % xs) for i in range(xs)])  5.23 us
  transfers between devices with their start and end apart: 10, of which 5 were waited for; matrix products, arithmetic and copies ran while one was open for 0% of the time, Pallas kernels for 3%

profile of v3, /device:TPU:6, one launch (start us, length us, event | category | flops | bytes accessed | tf_op | source)
XLA Modules:
  0.0 169.4 jit_solution(8686355044701861533)
XLA Ops:
  0.0 2.0 %pack.1 = (bf16[8,12,24,128]{3,2,1,0:T(8,128)(2,1)}, f32[24,2,128]{2,1,0:T(2,128)}) custom-call(s32[2,32]{1,0:T(2,128)} %bitcast.22, bf16[32,256]{1,0:T(8,128)(2,1)} %tokens_ref.1, bf16[8,256]{1,0:T(8,128)(2,1)} %bitcast.25), custom_call_target="tpu_custom_call" | custom-call | flops 10000000 | bytes 1000000 | tf_op jit(solution)/shard_map/pack/pallas_call | solution.py:192
  2.0 52.1 %all_to_all.15 = bf16[96,24,128]{2,1,0:T(8,128)(2,1)S(1)} all-to-all(bf16[96,24,128]{2,1,0:T(8,128)(2,1)} %bitcast.24), channel_id=1, replica_groups=mesh['zh'=2,'yq'=4,'yp'=2,'c'=2,'z'=6,'x'=4] {'zh','yq','yp','z'}, dimensions={0} | all-to-all | bytes 1179648 | tf_op jit(solution)/shard_map/all_to_all | solution.py:204
  54.1 0.9 spread.1.refs_1_
  55.0 1.9 %collective-permute-start.1 = (bf16[6144,128]{1,0:T(8,128)(2,1)S(1)}, bf16[6144,128]{1,0:T(8,128)(2,1)S(1)}, u32[]{:S(2)}, u32[]{:S(2)}) collective-permute-start(bf16[6144,128]{1,0:T(8,128)(2,1)S(1)} %bitcast.9), channel_id=1, source_target_pairs={{0,24},{24,0},{1,25},{25,1},{2,26},{26,2},{3,27},{27,3},{4,28},{28... | collective-permute-start | bytes 4718600 | tf_op jit(solution)/shard_map/ppermute | solution.py:216
  56.9 2.4 %collective-permute-start.2 = (bf16[6144,128]{1,0:T(8,128)(2,1)}, bf16[6144,128]{1,0:T(8,128)(2,1)}, u32[]{:S(2)}, u32[]{:S(2)}) collective-permute-start(bf16[6144,128]{1,0:T(8,128)(2,1)} %bitcast.13), channel_id=1, source_target_pairs={{0,24},{24,0},{1,25},{25,1},{2,26},{26,2},{3,27},{27,3},{4,28},{28... | collective-permute-start | bytes 4718600 | tf_op jit(solution)/shard_map/ppermute | solution.py:217
  59.3 1.9 %collective-permute-start.5 = (bf16[128,6144]{1,0:T(8,128)(2,1)}, bf16[128,6144]{1,0:T(8,128)(2,1)}, u32[]{:S(2)}, u32[]{:S(2)}) collective-permute-start(bf16[128,6144]{1,0:T(8,128)(2,1)} %bitcast.20), channel_id=1, source_target_pairs={{0,24},{24,0},{1,25},{25,1},{2,26},{26,2},{3,27},{27,3},{4,28},{28... | collective-permute-start | bytes 4718600 | tf_op jit(solution)/shard_map/ppermute | solution.py:218
  61.3 2.4 %collective-permute-start.4 = (bf16[6,192,256]{2,1,0:T(8,128)(2,1)}, bf16[6,192,256]{2,1,0:T(8,128)(2,1)}, u32[]{:S(2)}, u32[]{:S(2)}) collective-permute-start(bf16[6,192,256]{2,1,0:T(8,128)(2,1)} %spread.1.refs_1_), channel_id=1, source_target_pairs={{0,1},{1,2},{2,3},{3,0},{4,5},{5,6},{6,7},{7,4},{8,9},{9,10},{10,1... | collective-permute-start | bytes 1769480 | tf_op jit(solution)/shard_map/ppermute | solution.py:184
  63.7 3.5 %collective-permute-start.3 = (bf16[6,192,256]{2,1,0:T(8,128)(2,1)}, bf16[6,192,256]{2,1,0:T(8,128)(2,1)}, u32[]{:S(2)}, u32[]{:S(2)}) collective-permute-start(bf16[6,192,256]{2,1,0:T(8,128)(2,1)} %spread.1.refs_1_), channel_id=1, source_target_pairs={{0,3},{1,0},{2,1},{3,2},{4,7},{5,4},{6,5},{7,6},{8,11},{9,8},{10,9... | collective-permute-start | bytes 1769480 | tf_op jit(solution)/shard_map/ppermute | solution.py:190
  67.1 0.0 collective-permute-done.1.refs_3_.refs_4_
  67.2 3.3 %collective-permute-start = (bf16[6,192,256]{2,1,0:T(8,128)(2,1)}, bf16[6,192,256]{2,1,0:T(8,128)(2,1)}, u32[]{:S(2)}, u32[]{:S(2)}) collective-permute-start(bf16[6,192,256]{2,1,0:T(8,128)(2,1)} %spread.1.refs_1_), channel_id=1, source_target_pairs={{0,2},{1,3},{2,0},{3,1},{4,6},{5,7},{6,4},{7,5},{8,10},{9,11},{10,... | collective-permute-start | bytes 1769480 | tf_op jit(solution)/shard_map/ppermute | solution.py:187
  70.5 0.0 collective-permute-done.2.refs_5_.refs_6_
  70.5 0.0 copy-start.1
  70.5 1.4 copy-done.1
  71.9 2.2 %gate_up.2.refs_7_ = f32[192,512]{1,0:T(8,128)S(1)} custom-call(s32[4]{0:T(128)S(1)} %add_and_fusion.refs_0_, bf16[6,192,256]{2,1,0:T(8,128)(2,1)} %spread.1.refs_1_, bf16[6144,128]{1,0:T(8,128)(2,1)S(1)} %bitcast.10, bf16[6144,128]{1,0:T(8,128)(2,1)S(1)} %collective-permute-done.1.refs_3_.refs_4_, bf16[6144,128]{1,0:T(8,128)(2,1)S(1)} %bitcast.14, ...), custom_call_target="tpu_custom_call" | custom-call | flops 301989888 | bytes 2162688 | tf_op jit(solution)/shard_map/gate_up/pallas_call | solution.py:229
  74.1 0.0 copy-start.3
  74.2 5.5 %collective-permute-done.4.refs_2_ = bf16[6,192,256]{2,1,0:T(8,128)(2,1)} collective-permute-done((bf16[6,192,256]{2,1,0:T(8,128)(2,1)}, bf16[6,192,256]{2,1,0:T(8,128)(2,1)}, u32[]{:S(2)}, u32[]{:S(2)}) %collective-permute-start.4) | collective-permute-done | bytes 589856 | tf_op jit(solution)/shard_map/ppermute | solution.py:184
  79.7 15.5 %collective-permute-done.3.refs_1_ = bf16[6,192,256]{2,1,0:T(8,128)(2,1)} collective-permute-done((bf16[6,192,256]{2,1,0:T(8,128)(2,1)}, bf16[6,192,256]{2,1,0:T(8,128)(2,1)}, u32[]{:S(2)}, u32[]{:S(2)}) %collective-permute-start.3) | collective-permute-done | bytes 589856 | tf_op jit(solution)/shard_map/ppermute | solution.py:190
  95.2 2.6 %gate_up.3.refs_6_ = f32[192,512]{1,0:T(8,128)S(1)} custom-call(s32[4]{0:T(128)S(1)} %add_and_fusion.refs_0_, bf16[6,192,256]{2,1,0:T(8,128)(2,1)} %collective-permute-done.3.refs_1_, bf16[6,192,256]{2,1,0:T(8,128)(2,1)} %collective-permute-done.4.refs_2_, bf16[6144,128]{1,0:T(8,128)(2,1)S(1)} %bitcast.11, ...), custom_call_target="tpu_custom_call" | custom-call | flops 603979776 | bytes 4325376 | tf_op jit(solution)/shard_map/gate_up/pallas_call | solution.py:229
  97.8 0.0 collective-permute-done.refs_1_
  97.8 4.3 %turn.1 = (bf16[6,192,256]{2,1,0:T(8,128)(2,1)S(1)}, bf16[6,192,256]{2,1,0:T(8,128)(2,1)}, bf16[6,192,256]{2,1,0:T(8,128)(2,1)}, bf16[6,192,256]{2,1,0:T(8,128)(2,1)}) custom-call(s32[4]{0:T(128)S(1)} %add_and_fusion.refs_0_, bf16[6,192,256]{2,1,0:T(8,128)(2,1)} %collective-permute-done.refs_1_, bf16[6144,128]{1,0:T(8,128)(2,1)S(1)} %bitcast.12, ...), custom_call_target="tpu_custom_call" | custom-call | flops 905969664 | bytes 6488064 | tf_op jit(solution)/shard_map/turn/pallas_call | solution.py:241
  102.1 0.8 copy-done.4
  102.9 1.9 %collective-permute-start.6 = (bf16[6,192,256]{2,1,0:T(8,128)(2,1)}, bf16[6,192,256]{2,1,0:T(8,128)(2,1)S(1)}, u32[]{:S(2)}, u32[]{:S(2)}) collective-permute-start(bf16[6,192,256]{2,1,0:T(8,128)(2,1)} %get-tuple-element.20), channel_id=1, source_target_pairs={{0,1},{1,2},{2,3},{3,0},{4,5},{5,6},{6,7},{7,4},{8,9},{9,10},{10,1... | collective-permute-start | bytes 1769480 | tf_op jit(solution)/shard_map/ppermute | solution.py:184
  104.8 3.9 %collective-permute-start.7 = (bf16[6,192,256]{2,1,0:T(8,128)(2,1)}, bf16[6,192,256]{2,1,0:T(8,128)(2,1)S(1)}, u32[]{:S(2)}, u32[]{:S(2)}) collective-permute-start(bf16[6,192,256]{2,1,0:T(8,128)(2,1)} %get-tuple-element.21), channel_id=1, source_target_pairs={{0,3},{1,0},{2,1},{3,2},{4,7},{5,4},{6,5},{7,6},{8,11},{9,8},{10,9... | collective-permute-start | bytes 1769480 | tf_op jit(solution)/shard_map/ppermute | solution.py:190
  108.8 1.9 %collective-permute-start.8 = (bf16[6,192,256]{2,1,0:T(8,128)(2,1)}, bf16[6,192,256]{2,1,0:T(8,128)(2,1)S(1)}, u32[]{:S(2)}, u32[]{:S(2)}) collective-permute-start(bf16[6,192,256]{2,1,0:T(8,128)(2,1)} %get-tuple-element.22), channel_id=1, source_target_pairs={{0,2},{1,3},{2,0},{3,1},{4,6},{5,7},{6,4},{7,5},{8,10},{9,11},{10,... | collective-permute-start | bytes 1769480 | tf_op jit(solution)/shard_map/ppermute | solution.py:187
  110.7 7.5 %all-to-all-start = ((f32[24,2,128]{2,1,0:T(2,128)}), f32[24,2,128]{2,1,0:T(2,128)S(1)}, u32[]{:S(2)}, u32[]{:S(2)}) async-start(f32[24,2,128]{2,1,0:T(2,128)} %get-tuple-element.14), calls=%async_computation | async-start | bytes 49152 | tf_op jit(solution)/shard_map/all_to_all | solution.py:203
  118.2 3.1 %collective-permute-done.6.refs_1_ = bf16[6,192,256]{2,1,0:T(8,128)(2,1)S(1)} collective-permute-done((bf16[6,192,256]{2,1,0:T(8,128)(2,1)}, bf16[6,192,256]{2,1,0:T(8,128)(2,1)S(1)}, u32[]{:S(2)}, u32[]{:S(2)}) %collective-permute-start.6) | collective-permute-done | bytes 589856 | tf_op jit(solution)/shard_map/ppermute | solution.py:184
  121.3 1.5 collective-permute-done.7.refs_2_
  122.8 10.5 %collective-permute-done.8.refs_3_ = bf16[6,192,256]{2,1,0:T(8,128)(2,1)S(1)} collective-permute-done((bf16[6,192,256]{2,1,0:T(8,128)(2,1)}, bf16[6,192,256]{2,1,0:T(8,128)(2,1)S(1)}, u32[]{:S(2)}, u32[]{:S(2)}) %collective-permute-start.8) | collective-permute-done | bytes 589856 | tf_op jit(solution)/shard_map/ppermute | solution.py:187
  133.3 1.1 copy-done.5
  134.4 0.3 unspread.1
  134.7 33.6 %all_to_all.16 = bf16[96,24,128]{2,1,0:T(8,128)(2,1)S(1)} all-to-all(bf16[96,24,128]{2,1,0:T(8,128)(2,1)S(1)} %bitcast.19), channel_id=1, replica_groups=mesh['zh'=2,'yq'=4,'yp'=2,'c'=2,'z'=6,'x'=4] {'zh','yq','yp','z'}, dimensions={0} | all-to-all | bytes 1179648 | tf_op jit(solution)/shard_map/all_to_all | solution.py:262
  168.3 1.1 merge.1
  (14 shorter events, 0.0 us)
Async XLA Ops:
  0.0 70.5 %copy-start.7 = (s32[4]{0:T(128)S(1)}, s32[4]{0:T(128)}, u32[]{:S(2)}) copy-start(s32[4]{0:T(128)} %constant.8.clone) | copy-start | bytes 52
  0.0 55.0 %copy-start = (bf16[1,6144,128]{2,1,0:T(8,128)(2,1)S(1)}, bf16[1,6144,128]{2,1,0:T(8,128)(2,1)}, u32[]{:S(2)}) copy-start(bf16[1,6144,128]{2,1,0:T(8,128)(2,1)} %param.10) | copy-start | bytes 4718596
  55.0 12.1 %collective-permute-start.1 = (bf16[6144,128]{1,0:T(8,128)(2,1)S(1)}, bf16[6144,128]{1,0:T(8,128)(2,1)S(1)}, u32[]{:S(2)}, u32[]{:S(2)}) collective-permute-start(bf16[6144,128]{1,0:T(8,128)(2,1)S(1)} %bitcast.9), channel_id=1, source_target_pairs={{0,24},{24,0},{1,25},{25,1},{2,26},{26,2},{3,27},{27,3},{4,28},{28... | collective-permute-start | bytes 4718600 | tf_op jit(solution)/shard_map/ppermute | solution.py:216
  56.9 13.6 %collective-permute-start.2 = (bf16[6144,128]{1,0:T(8,128)(2,1)}, bf16[6144,128]{1,0:T(8,128)(2,1)}, u32[]{:S(2)}, u32[]{:S(2)}) collective-permute-start(bf16[6144,128]{1,0:T(8,128)(2,1)} %bitcast.13), channel_id=1, source_target_pairs={{0,24},{24,0},{1,25},{25,1},{2,26},{26,2},{3,27},{27,3},{4,28},{28... | collective-permute-start | bytes 4718600 | tf_op jit(solution)/shard_map/ppermute | solution.py:217
  59.3 38.5 %collective-permute-start.5 = (bf16[128,6144]{1,0:T(8,128)(2,1)}, bf16[128,6144]{1,0:T(8,128)(2,1)}, u32[]{:S(2)}, u32[]{:S(2)}) collective-permute-start(bf16[128,6144]{1,0:T(8,128)(2,1)} %bitcast.20), channel_id=1, source_target_pairs={{0,24},{24,0},{1,25},{25,1},{2,26},{26,2},{3,27},{27,3},{4,28},{28... | collective-permute-start | bytes 4718600 | tf_op jit(solution)/shard_map/ppermute | solution.py:218
  61.3 18.4 %collective-permute-start.4 = (bf16[6,192,256]{2,1,0:T(8,128)(2,1)}, bf16[6,192,256]{2,1,0:T(8,128)(2,1)}, u32[]{:S(2)}, u32[]{:S(2)}) collective-permute-start(bf16[6,192,256]{2,1,0:T(8,128)(2,1)} %spread.1.refs_1_), channel_id=1, source_target_pairs={{0,1},{1,2},{2,3},{3,0},{4,5},{5,6},{6,7},{7,4},{8,9},{9,10},{10,1... | collective-permute-start | bytes 1769480 | tf_op jit(solution)/shard_map/ppermute | solution.py:184
  63.7 31.5 %collective-permute-start.3 = (bf16[6,192,256]{2,1,0:T(8,128)(2,1)}, bf16[6,192,256]{2,1,0:T(8,128)(2,1)}, u32[]{:S(2)}, u32[]{:S(2)}) collective-permute-start(bf16[6,192,256]{2,1,0:T(8,128)(2,1)} %spread.1.refs_1_), channel_id=1, source_target_pairs={{0,3},{1,0},{2,1},{3,2},{4,7},{5,4},{6,5},{7,6},{8,11},{9,8},{10,9... | collective-permute-start | bytes 1769480 | tf_op jit(solution)/shard_map/ppermute | solution.py:190
  67.2 30.7 %collective-permute-start = (bf16[6,192,256]{2,1,0:T(8,128)(2,1)}, bf16[6,192,256]{2,1,0:T(8,128)(2,1)}, u32[]{:S(2)}, u32[]{:S(2)}) collective-permute-start(bf16[6,192,256]{2,1,0:T(8,128)(2,1)} %spread.1.refs_1_), channel_id=1, source_target_pairs={{0,2},{1,3},{2,0},{3,1},{4,6},{5,7},{6,4},{7,5},{8,10},{9,11},{10,... | collective-permute-start | bytes 1769480 | tf_op jit(solution)/shard_map/ppermute | solution.py:187
  70.5 1.4 copy-start.1
  71.9 23.3 %copy-start.2 = (bf16[1,6144,128]{2,1,0:T(8,128)(2,1)S(1)}, bf16[1,6144,128]{2,1,0:T(8,128)(2,1)}, u32[]{:S(2)}) copy-start(bf16[1,6144,128]{2,1,0:T(8,128)(2,1)} %param.11) | copy-start | bytes 4718596
  74.1 23.7 %copy-start.3 = (bf16[1,128,6144]{2,1,0:T(8,128)(2,1)S(1)}, bf16[1,128,6144]{2,1,0:T(8,128)(2,1)}, u32[]{:S(2)}) copy-start(bf16[1,128,6144]{2,1,0:T(8,128)(2,1)} %param.12) | copy-start | bytes 4718596
  102.1 0.8 copy-start.4
  102.9 18.4 %collective-permute-start.6 = (bf16[6,192,256]{2,1,0:T(8,128)(2,1)}, bf16[6,192,256]{2,1,0:T(8,128)(2,1)S(1)}, u32[]{:S(2)}, u32[]{:S(2)}) collective-permute-start(bf16[6,192,256]{2,1,0:T(8,128)(2,1)} %get-tuple-element.20), channel_id=1, source_target_pairs={{0,1},{1,2},{2,3},{3,0},{4,5},{5,6},{6,7},{7,4},{8,9},{9,10},{10,1... | collective-permute-start | bytes 1769480 | tf_op jit(solution)/shard_map/ppermute | solution.py:184
  104.8 18.0 %collective-permute-start.7 = (bf16[6,192,256]{2,1,0:T(8,128)(2,1)}, bf16[6,192,256]{2,1,0:T(8,128)(2,1)S(1)}, u32[]{:S(2)}, u32[]{:S(2)}) collective-permute-start(bf16[6,192,256]{2,1,0:T(8,128)(2,1)} %get-tuple-element.21), channel_id=1, source_target_pairs={{0,3},{1,0},{2,1},{3,2},{4,7},{5,4},{6,5},{7,6},{8,11},{9,8},{10,9... | collective-permute-start | bytes 1769480 | tf_op jit(solution)/shard_map/ppermute | solution.py:190
  108.8 24.5 %collective-permute-start.8 = (bf16[6,192,256]{2,1,0:T(8,128)(2,1)}, bf16[6,192,256]{2,1,0:T(8,128)(2,1)S(1)}, u32[]{:S(2)}, u32[]{:S(2)}) collective-permute-start(bf16[6,192,256]{2,1,0:T(8,128)(2,1)} %get-tuple-element.22), channel_id=1, source_target_pairs={{0,2},{1,3},{2,0},{3,1},{4,6},{5,7},{6,4},{7,5},{8,10},{9,11},{10,... | collective-permute-start | bytes 1769480 | tf_op jit(solution)/shard_map/ppermute | solution.py:187
  110.7 24.0 %all-to-all-start = ((f32[24,2,128]{2,1,0:T(2,128)}), f32[24,2,128]{2,1,0:T(2,128)S(1)}, u32[]{:S(2)}, u32[]{:S(2)}) async-start(f32[24,2,128]{2,1,0:T(2,128)} %get-tuple-element.14), calls=%async_computation | async-start | bytes 49152 | tf_op jit(solution)/shard_map/all_to_all | solution.py:203
  133.3 1.1 copy-start.5
  134.4 33.9 %copy-start.6 = (s32[32,2]{0,1:T(2,128)S(1)}, s32[32,2]{0,1:T(2,128)}, u32[]{:S(2)}) copy-start(s32[32,2]{0,1:T(2,128)} %param.9) | copy-start | bytes 772

commit v4 on v3

--- a/solution.py
+++ b/solution.py
@@ -8,6 +8,7 @@
 
 
 CAP = 12
+MIB_GATE, MIB_TURN, MIB_DOWN = 16, 24, 8
 LANES = 128
 CHUNK = 2 * CAP
 FAR = ("zh", "yq", "yp", "z")
@@ -127,15 +128,22 @@
 
 def turn_kernel(xs, near_ref, far_ref, *refs):
     weights, total_ref = refs[:4], refs[4]
-    own_ref, other_ref, *outs = refs[5:]
+    own_ref, other_ref, hidden_ref, *outs = refs[5:]
     far = [far_ref[z] for z in range(far_ref.shape[0])]
     total = products([far], [near_ref[xs - 1]], weights, total_ref[...])
     units = total.shape[1] // 2
     gate, up = total[:, :units], total[:, units:]
     hidden = (jax.nn.silu(gate) * up).astype(bf16)
+    hidden_ref[...] = hidden
     for n, out in enumerate(outs):
         for z in range(out.shape[0]):
-            out[z] = down(hidden, own_ref, other_ref, near_ref[n], z, xs)
+            out[z] = down(hidden, own_ref, other_ref, near_ref[n + 1], z, xs)
+
+
+def down_kernel(xs, near_ref, hidden_ref, own_ref, other_ref, out_ref):
+    hidden = hidden_ref[...]
+    for z in range(out_ref.shape[0]):
+        out_ref[z] = down(hidden, own_ref, other_ref, near_ref[0], z, xs)
 
 
 def merge_kernel(ids_ref, logits_ref, in_ref, out_ref):
@@ -231,19 +239,19 @@
             sums,
             flops * len(places),
             nbytes * len(places),
-            mib=16,
+            mib=MIB_GATE,
             in_specs=[smem] + [vmem] * (len(places) + 4 + len(more)),
             name="gate_up",
         )(near, *blocks, *weights, *more)
 
     total = gate_up((0,), (own,), None)
     total = gate_up((1, 2), (right, left), total)
-    mine, to_next, to_prev, to_far = call(
+    hidden, to_next, to_prev, to_far = call(
         lambda *refs: turn_kernel(xs, *refs),
-        (full,) * xs,
+        (jax.ShapeDtypeStruct((rows, 2 * units), bf16),) + (full,) * (xs - 1),
         3 * flops,
         3 * nbytes,
-        mib=24,
+        mib=MIB_TURN,
         in_specs=[smem] + [vmem] * 8,
         name="turn",
     )(near, opposite, *weights, total, down_w, down_o)
@@ -251,6 +259,15 @@
     from_far = across(to_far)
     from_prev = ahead(to_next)
     from_next = behind(to_prev)
+    mine = call(
+        lambda *refs: down_kernel(xs, *refs),
+        full,
+        flops // 2,
+        nbytes // 2,
+        mib=MIB_DOWN,
+        in_specs=[smem] + [vmem] * 3,
+        name="down",
+    )(near, hidden, down_w, down_o)
 
     leaving = call(
         unspread_kernel,

time: 170 us -> 168 us (0.988)
  waiting for transfers between devices: 36.1 us -> 33 us
    ppermute x2, waiting for transfers between devices: 8.61 us -> 5.55 us  [ahead(): return lax.ppermute(v, 'x', forward)]
    pallas_call x1 -> x2, Pallas kernels: 4.26 us -> 5.87 us  [the longest x1 4.13 us: block(): call(lambda *refs: turn_kernel(xs, *refs), (jax.ShapeDtypeStruct((rows, 2...]
  transfers between devices with their start and end apart: 10 -> 10, of which waited for: 5 -> 4; matrix products, arithmetic and copies ran while one was open for 0% -> 0% of each run, Pallas kernels for 3% -> 4%
where the time goes in v4:
time: 168 us; the launch traced here: 167 us
  blocking collectives  85.7 us (51%)
  waiting for transfers between devices  33 us (20%)
  starting transfers between devices  30.7 us (18%)
  Pallas kernels  15 us (9%)
  local copies, waits for them, and re-layouts  2.83 us (2%)
    all_to_all x1, blocking collectives, block(): lax.all_to_all(messages.reshape(far, CHUNK, LANES), FAR, 0, 0, tiled=True)  52.1 us
    all_to_all x1, blocking collectives, block(): lax.all_to_all(leaving.reshape(far, CHUNK, LANES), FAR, 0, 0, tiled=True)  33.6 us
    ppermute x2, waiting for transfers between devices, behind(): return lax.ppermute(v, 'x', backward)  16.9 us
    ppermute x2, waiting for transfers between devices, across(): return lax.ppermute(v, 'x', [(i, (i + 2) % xs) for i in range(xs)])  10.5 us
    all_to_all x1, starting transfers between devices, block(): partial_logits = lax.all_to_all(logits, ('z', 'x'), 0, 0, tiled=True)  7.54 us
    ppermute x2, starting transfers between devices, behind(): return lax.ppermute(v, 'x', backward)  7.38 us
    ppermute x2, waiting for transfers between devices, ahead(): return lax.ppermute(v, 'x', forward)  5.55 us
    ppermute x2, starting transfers between devices, across(): return lax.ppermute(v, 'x', [(i, (i + 2) % xs) for i in range(xs)])  5.23 us
  transfers between devices with their start and end apart: 10, of which 4 were waited for; matrix products, arithmetic and copies ran while one was open for 0% of the time, Pallas kernels for 4%

profile of v4, /device:TPU:6, one launch (start us, length us, event | category | flops | bytes accessed | tf_op | source)
XLA Modules:
  0.0 167.4 jit_solution(12219489374984454015)
XLA Ops:
  0.0 2.0 %pack.1 = (bf16[8,12,24,128]{3,2,1,0:T(8,128)(2,1)}, f32[24,2,128]{2,1,0:T(2,128)}) custom-call(s32[2,32]{1,0:T(2,128)} %bitcast.23, bf16[32,256]{1,0:T(8,128)(2,1)} %tokens_ref.1, bf16[8,256]{1,0:T(8,128)(2,1)} %bitcast.26), custom_call_target="tpu_custom_call" | custom-call | flops 10000000 | bytes 1000000 | tf_op jit(solution)/shard_map/pack/pallas_call | solution.py:200
  2.0 52.1 %all_to_all.15 = bf16[96,24,128]{2,1,0:T(8,128)(2,1)S(1)} all-to-all(bf16[96,24,128]{2,1,0:T(8,128)(2,1)} %bitcast.25), channel_id=1, replica_groups=mesh['zh'=2,'yq'=4,'yp'=2,'c'=2,'z'=6,'x'=4] {'zh','yq','yp','z'}, dimensions={0} | all-to-all | bytes 1179648 | tf_op jit(solution)/shard_map/all_to_all | solution.py:212
  54.1 0.9 spread.1.refs_1_
  55.0 1.9 %collective-permute-start.1 = (bf16[6144,128]{1,0:T(8,128)(2,1)S(1)}, bf16[6144,128]{1,0:T(8,128)(2,1)S(1)}, u32[]{:S(2)}, u32[]{:S(2)}) collective-permute-start(bf16[6144,128]{1,0:T(8,128)(2,1)S(1)} %bitcast.9), channel_id=1, source_target_pairs={{0,24},{24,0},{1,25},{25,1},{2,26},{26,2},{3,27},{27,3},{4,28},{28... | collective-permute-start | bytes 4718600 | tf_op jit(solution)/shard_map/ppermute | solution.py:224
  56.9 2.4 %collective-permute-start.2 = (bf16[6144,128]{1,0:T(8,128)(2,1)}, bf16[6144,128]{1,0:T(8,128)(2,1)}, u32[]{:S(2)}, u32[]{:S(2)}) collective-permute-start(bf16[6144,128]{1,0:T(8,128)(2,1)} %bitcast.13), channel_id=1, source_target_pairs={{0,24},{24,0},{1,25},{25,1},{2,26},{26,2},{3,27},{27,3},{4,28},{28... | collective-permute-start | bytes 4718600 | tf_op jit(solution)/shard_map/ppermute | solution.py:225
  59.3 1.9 %collective-permute-start.5 = (bf16[128,6144]{1,0:T(8,128)(2,1)}, bf16[128,6144]{1,0:T(8,128)(2,1)}, u32[]{:S(2)}, u32[]{:S(2)}) collective-permute-start(bf16[128,6144]{1,0:T(8,128)(2,1)} %bitcast.17), channel_id=1, source_target_pairs={{0,24},{24,0},{1,25},{25,1},{2,26},{26,2},{3,27},{27,3},{4,28},{28... | collective-permute-start | bytes 4718600 | tf_op jit(solution)/shard_map/ppermute | solution.py:226
  61.3 2.4 %collective-permute-start.4 = (bf16[6,192,256]{2,1,0:T(8,128)(2,1)}, bf16[6,192,256]{2,1,0:T(8,128)(2,1)}, u32[]{:S(2)}, u32[]{:S(2)}) collective-permute-start(bf16[6,192,256]{2,1,0:T(8,128)(2,1)} %spread.1.refs_1_), channel_id=1, source_target_pairs={{0,1},{1,2},{2,3},{3,0},{4,5},{5,6},{6,7},{7,4},{8,9},{9,10},{10,1... | collective-permute-start | bytes 1769480 | tf_op jit(solution)/shard_map/ppermute | solution.py:192
  63.7 3.5 %collective-permute-start.3 = (bf16[6,192,256]{2,1,0:T(8,128)(2,1)}, bf16[6,192,256]{2,1,0:T(8,128)(2,1)}, u32[]{:S(2)}, u32[]{:S(2)}) collective-permute-start(bf16[6,192,256]{2,1,0:T(8,128)(2,1)} %spread.1.refs_1_), channel_id=1, source_target_pairs={{0,3},{1,0},{2,1},{3,2},{4,7},{5,4},{6,5},{7,6},{8,11},{9,8},{10,9... | collective-permute-start | bytes 1769480 | tf_op jit(solution)/shard_map/ppermute | solution.py:198
  67.1 0.0 collective-permute-done.1.refs_3_.refs_4_
  67.1 3.3 %collective-permute-start = (bf16[6,192,256]{2,1,0:T(8,128)(2,1)}, bf16[6,192,256]{2,1,0:T(8,128)(2,1)}, u32[]{:S(2)}, u32[]{:S(2)}) collective-permute-start(bf16[6,192,256]{2,1,0:T(8,128)(2,1)} %spread.1.refs_1_), channel_id=1, source_target_pairs={{0,2},{1,3},{2,0},{3,1},{4,6},{5,7},{6,4},{7,5},{8,10},{9,11},{10,... | collective-permute-start | bytes 1769480 | tf_op jit(solution)/shard_map/ppermute | solution.py:195
  70.5 0.0 collective-permute-done.2.refs_5_.refs_6_
  70.5 0.0 copy-start.1
  70.5 1.4 copy-done.1
  71.9 2.2 %gate_up.2.refs_7_ = f32[192,512]{1,0:T(8,128)S(1)} custom-call(s32[4]{0:T(128)S(1)} %add_and_fusion.refs_0_, bf16[6,192,256]{2,1,0:T(8,128)(2,1)} %spread.1.refs_1_, bf16[6144,128]{1,0:T(8,128)(2,1)S(1)} %bitcast.10, bf16[6144,128]{1,0:T(8,128)(2,1)S(1)} %collective-permute-done.1.refs_3_.refs_4_, bf16[6144,128]{1,0:T(8,128)(2,1)S(1)} %bitcast.14, ...), custom_call_target="tpu_custom_call" | custom-call | flops 301989888 | bytes 2162688 | tf_op jit(solution)/shard_map/gate_up/pallas_call | solution.py:237
  74.1 0.0 copy-start.3
  74.1 5.5 %collective-permute-done.4.refs_2_ = bf16[6,192,256]{2,1,0:T(8,128)(2,1)} collective-permute-done((bf16[6,192,256]{2,1,0:T(8,128)(2,1)}, bf16[6,192,256]{2,1,0:T(8,128)(2,1)}, u32[]{:S(2)}, u32[]{:S(2)}) %collective-permute-start.4) | collective-permute-done | bytes 589856 | tf_op jit(solution)/shard_map/ppermute | solution.py:192
  79.7 15.5 %collective-permute-done.3.refs_1_ = bf16[6,192,256]{2,1,0:T(8,128)(2,1)} collective-permute-done((bf16[6,192,256]{2,1,0:T(8,128)(2,1)}, bf16[6,192,256]{2,1,0:T(8,128)(2,1)}, u32[]{:S(2)}, u32[]{:S(2)}) %collective-permute-start.3) | collective-permute-done | bytes 589856 | tf_op jit(solution)/shard_map/ppermute | solution.py:198
  95.2 2.6 %gate_up.3.refs_6_ = f32[192,512]{1,0:T(8,128)S(1)} custom-call(s32[4]{0:T(128)S(1)} %add_and_fusion.refs_0_, bf16[6,192,256]{2,1,0:T(8,128)(2,1)} %collective-permute-done.3.refs_1_, bf16[6,192,256]{2,1,0:T(8,128)(2,1)} %collective-permute-done.4.refs_2_, bf16[6144,128]{1,0:T(8,128)(2,1)S(1)} %bitcast.11, ...), custom_call_target="tpu_custom_call" | custom-call | flops 603979776 | bytes 4325376 | tf_op jit(solution)/shard_map/gate_up/pallas_call | solution.py:237
  97.8 4.1 %turn.1 = (bf16[192,256]{1,0:T(8,128)(2,1)S(1)}, bf16[6,192,256]{2,1,0:T(8,128)(2,1)}, bf16[6,192,256]{2,1,0:T(8,128)(2,1)}, bf16[6,192,256]{2,1,0:T(8,128)(2,1)}) custom-call(s32[4]{0:T(128)S(1)} %add_and_fusion.refs_0_, bf16[6,192,256]{2,1,0:T(8,128)(2,1)} %collective-permute-done.refs_1_, bf16[6144,128]{1,0:T(8,128)(2,1)S(1)} %bitcast.12, ...), custom_call_target="tpu_custom_call" | custom-call | flops 905969664 | bytes 6488064 | tf_op jit(solution)/shard_map/turn/pallas_call | solution.py:249
  101.9 1.9 %collective-permute-start.6 = (bf16[6,192,256]{2,1,0:T(8,128)(2,1)}, bf16[6,192,256]{2,1,0:T(8,128)(2,1)S(1)}, u32[]{:S(2)}, u32[]{:S(2)}) collective-permute-start(bf16[6,192,256]{2,1,0:T(8,128)(2,1)} %get-tuple-element.20), channel_id=1, source_target_pairs={{0,1},{1,2},{2,3},{3,0},{4,5},{5,6},{6,7},{7,4},{8,9},{9,10},{10,1... | collective-permute-start | bytes 1769480 | tf_op jit(solution)/shard_map/ppermute | solution.py:192
  103.9 3.9 %collective-permute-start.7 = (bf16[6,192,256]{2,1,0:T(8,128)(2,1)}, bf16[6,192,256]{2,1,0:T(8,128)(2,1)S(1)}, u32[]{:S(2)}, u32[]{:S(2)}) collective-permute-start(bf16[6,192,256]{2,1,0:T(8,128)(2,1)} %get-tuple-element.21), channel_id=1, source_target_pairs={{0,3},{1,0},{2,1},{3,2},{4,7},{5,4},{6,5},{7,6},{8,11},{9,8},{10,9... | collective-permute-start | bytes 1769480 | tf_op jit(solution)/shard_map/ppermute | solution.py:198
  107.8 1.9 %collective-permute-start.8 = (bf16[6,192,256]{2,1,0:T(8,128)(2,1)}, bf16[6,192,256]{2,1,0:T(8,128)(2,1)S(1)}, u32[]{:S(2)}, u32[]{:S(2)}) collective-permute-start(bf16[6,192,256]{2,1,0:T(8,128)(2,1)} %get-tuple-element.22), channel_id=1, source_target_pairs={{0,2},{1,3},{2,0},{3,1},{4,6},{5,7},{6,4},{7,5},{8,10},{9,11},{10,... | collective-permute-start | bytes 1769480 | tf_op jit(solution)/shard_map/ppermute | solution.py:195
  109.7 7.5 %all-to-all-start = ((f32[24,2,128]{2,1,0:T(2,128)}), f32[24,2,128]{2,1,0:T(2,128)S(1)}, u32[]{:S(2)}, u32[]{:S(2)}) async-start(f32[24,2,128]{2,1,0:T(2,128)} %get-tuple-element.14), calls=%async_computation | async-start | bytes 49152 | tf_op jit(solution)/shard_map/all_to_all | solution.py:211
  117.3 0.0 copy-start.4
  117.3 1.4 copy-done.4
  118.7 1.7 %down.1.refs_0_ = bf16[6,192,256]{2,1,0:T(8,128)(2,1)S(1)} custom-call(s32[4]{0:T(128)S(1)} %add_and_fusion.refs_0_, bf16[192,256]{1,0:T(8,128)(2,1)S(1)} %get-tuple-element.19.refs_1_, bf16[128,6144]{1,0:T(8,128)(2,1)S(1)} %bitcast.19, bf16[128,6144]{1,0:T(8,128)(2,1)} %collective-permute-done.5.refs_8_.refs_3_), custom_call_target="tpu_custom_call" | custom-call | flops 150994944 | bytes 1081344 | tf_op jit(solution)/shard_map/down/pallas_call | solution.py:262
  120.4 0.0 copy-start.5
  120.5 1.4 collective-permute-done.7.refs_2_
  121.8 10.5 %collective-permute-done.8.refs_3_ = bf16[6,192,256]{2,1,0:T(8,128)(2,1)S(1)} collective-permute-done((bf16[6,192,256]{2,1,0:T(8,128)(2,1)}, bf16[6,192,256]{2,1,0:T(8,128)(2,1)S(1)}, u32[]{:S(2)}, u32[]{:S(2)}) %collective-permute-start.8) | collective-permute-done | bytes 589856 | tf_op jit(solution)/shard_map/ppermute | solution.py:195
  132.3 0.3 unspread.1
  132.7 33.6 %all_to_all.16 = bf16[96,24,128]{2,1,0:T(8,128)(2,1)S(1)} all-to-all(bf16[96,24,128]{2,1,0:T(8,128)(2,1)S(1)} %bitcast.22), channel_id=1, replica_groups=mesh['zh'=2,'yq'=4,'yp'=2,'c'=2,'z'=6,'x'=4] {'zh','yq','yp','z'}, dimensions={0} | all-to-all | bytes 1179648 | tf_op jit(solution)/shard_map/all_to_all | solution.py:279
  166.3 1.1 merge.1
  (13 shorter events, 0.0 us)
Async XLA Ops:
  0.0 70.5 %copy-start.6 = (s32[4]{0:T(128)S(1)}, s32[4]{0:T(128)}, u32[]{:S(2)}) copy-start(s32[4]{0:T(128)} %constant.8.clone) | copy-start | bytes 52
  0.0 55.0 %copy-start = (bf16[1,6144,128]{2,1,0:T(8,128)(2,1)S(1)}, bf16[1,6144,128]{2,1,0:T(8,128)(2,1)}, u32[]{:S(2)}) copy-start(bf16[1,6144,128]{2,1,0:T(8,128)(2,1)} %param.10) | copy-start | bytes 4718596
  55.0 12.1 %collective-permute-start.1 = (bf16[6144,128]{1,0:T(8,128)(2,1)S(1)}, bf16[6144,128]{1,0:T(8,128)(2,1)S(1)}, u32[]{:S(2)}, u32[]{:S(2)}) collective-permute-start(bf16[6144,128]{1,0:T(8,128)(2,1)S(1)} %bitcast.9), channel_id=1, source_target_pairs={{0,24},{24,0},{1,25},{25,1},{2,26},{26,2},{3,27},{27,3},{4,28},{28... | collective-permute-start | bytes 4718600 | tf_op jit(solution)/shard_map/ppermute | solution.py:224
  56.9 13.6 %collective-permute-start.2 = (bf16[6144,128]{1,0:T(8,128)(2,1)}, bf16[6144,128]{1,0:T(8,128)(2,1)}, u32[]{:S(2)}, u32[]{:S(2)}) collective-permute-start(bf16[6144,128]{1,0:T(8,128)(2,1)} %bitcast.13), channel_id=1, source_target_pairs={{0,24},{24,0},{1,25},{25,1},{2,26},{26,2},{3,27},{27,3},{4,28},{28... | collective-permute-start | bytes 4718600 | tf_op jit(solution)/shard_map/ppermute | solution.py:225
  59.3 38.5 %collective-permute-start.5 = (bf16[128,6144]{1,0:T(8,128)(2,1)}, bf16[128,6144]{1,0:T(8,128)(2,1)}, u32[]{:S(2)}, u32[]{:S(2)}) collective-permute-start(bf16[128,6144]{1,0:T(8,128)(2,1)} %bitcast.17), channel_id=1, source_target_pairs={{0,24},{24,0},{1,25},{25,1},{2,26},{26,2},{3,27},{27,3},{4,28},{28... | collective-permute-start | bytes 4718600 | tf_op jit(solution)/shard_map/ppermute | solution.py:226
  61.3 18.4 %collective-permute-start.4 = (bf16[6,192,256]{2,1,0:T(8,128)(2,1)}, bf16[6,192,256]{2,1,0:T(8,128)(2,1)}, u32[]{:S(2)}, u32[]{:S(2)}) collective-permute-start(bf16[6,192,256]{2,1,0:T(8,128)(2,1)} %spread.1.refs_1_), channel_id=1, source_target_pairs={{0,1},{1,2},{2,3},{3,0},{4,5},{5,6},{6,7},{7,4},{8,9},{9,10},{10,1... | collective-permute-start | bytes 1769480 | tf_op jit(solution)/shard_map/ppermute | solution.py:192
  63.7 31.5 %collective-permute-start.3 = (bf16[6,192,256]{2,1,0:T(8,128)(2,1)}, bf16[6,192,256]{2,1,0:T(8,128)(2,1)}, u32[]{:S(2)}, u32[]{:S(2)}) collective-permute-start(bf16[6,192,256]{2,1,0:T(8,128)(2,1)} %spread.1.refs_1_), channel_id=1, source_target_pairs={{0,3},{1,0},{2,1},{3,2},{4,7},{5,4},{6,5},{7,6},{8,11},{9,8},{10,9... | collective-permute-start | bytes 1769480 | tf_op jit(solution)/shard_map/ppermute | solution.py:198
  67.1 30.7 %collective-permute-start = (bf16[6,192,256]{2,1,0:T(8,128)(2,1)}, bf16[6,192,256]{2,1,0:T(8,128)(2,1)}, u32[]{:S(2)}, u32[]{:S(2)}) collective-permute-start(bf16[6,192,256]{2,1,0:T(8,128)(2,1)} %spread.1.refs_1_), channel_id=1, source_target_pairs={{0,2},{1,3},{2,0},{3,1},{4,6},{5,7},{6,4},{7,5},{8,10},{9,11},{10,... | collective-permute-start | bytes 1769480 | tf_op jit(solution)/shard_map/ppermute | solution.py:195
  70.5 1.4 copy-start.1
  71.9 23.3 %copy-start.2 = (bf16[1,6144,128]{2,1,0:T(8,128)(2,1)S(1)}, bf16[1,6144,128]{2,1,0:T(8,128)(2,1)}, u32[]{:S(2)}) copy-start(bf16[1,6144,128]{2,1,0:T(8,128)(2,1)} %param.11) | copy-start | bytes 4718596
  74.1 23.7 %copy-start.3 = (bf16[1,128,6144]{2,1,0:T(8,128)(2,1)S(1)}, bf16[1,128,6144]{2,1,0:T(8,128)(2,1)}, u32[]{:S(2)}) copy-start(bf16[1,128,6144]{2,1,0:T(8,128)(2,1)} %param.12) | copy-start | bytes 4718596
  101.9 18.5 %collective-permute-start.6 = (bf16[6,192,256]{2,1,0:T(8,128)(2,1)}, bf16[6,192,256]{2,1,0:T(8,128)(2,1)S(1)}, u32[]{:S(2)}, u32[]{:S(2)}) collective-permute-start(bf16[6,192,256]{2,1,0:T(8,128)(2,1)} %get-tuple-element.20), channel_id=1, source_target_pairs={{0,1},{1,2},{2,3},{3,0},{4,5},{5,6},{6,7},{7,4},{8,9},{9,10},{10,1... | collective-permute-start | bytes 1769480 | tf_op jit(solution)/shard_map/ppermute | solution.py:192
  103.9 18.0 %collective-permute-start.7 = (bf16[6,192,256]{2,1,0:T(8,128)(2,1)}, bf16[6,192,256]{2,1,0:T(8,128)(2,1)S(1)}, u32[]{:S(2)}, u32[]{:S(2)}) collective-permute-start(bf16[6,192,256]{2,1,0:T(8,128)(2,1)} %get-tuple-element.21), channel_id=1, source_target_pairs={{0,3},{1,0},{2,1},{3,2},{4,7},{5,4},{6,5},{7,6},{8,11},{9,8},{10,9... | collective-permute-start | bytes 1769480 | tf_op jit(solution)/shard_map/ppermute | solution.py:198
  107.8 24.6 %collective-permute-start.8 = (bf16[6,192,256]{2,1,0:T(8,128)(2,1)}, bf16[6,192,256]{2,1,0:T(8,128)(2,1)S(1)}, u32[]{:S(2)}, u32[]{:S(2)}) collective-permute-start(bf16[6,192,256]{2,1,0:T(8,128)(2,1)} %get-tuple-element.22), channel_id=1, source_target_pairs={{0,2},{1,3},{2,0},{3,1},{4,6},{5,7},{6,4},{7,5},{8,10},{9,11},{10,... | collective-permute-start | bytes 1769480 | tf_op jit(solution)/shard_map/ppermute | solution.py:195
  109.7 23.0 %all-to-all-start = ((f32[24,2,128]{2,1,0:T(2,128)}), f32[24,2,128]{2,1,0:T(2,128)S(1)}, u32[]{:S(2)}, u32[]{:S(2)}) async-start(f32[24,2,128]{2,1,0:T(2,128)} %get-tuple-element.14), calls=%async_computation | async-start | bytes 49152 | tf_op jit(solution)/shard_map/all_to_all | solution.py:211
  117.3 1.4 copy-start.4
  120.4 45.9 %copy-start.5 = (s32[32,2]{0,1:T(2,128)S(1)}, s32[32,2]{0,1:T(2,128)}, u32[]{:S(2)}) copy-start(s32[32,2]{0,1:T(2,128)} %param.9) | copy-start | bytes 772

commit v5 on v4

--- a/solution.py
+++ b/solution.py
@@ -126,10 +126,10 @@
     return jnp.dot(hidden, both, preferred_element_type=f32).astype(bf16)
 
 
-def turn_kernel(xs, near_ref, far_ref, *refs):
+def turn_kernel(xs, near_ref, lo_ref, hi_ref, *refs):
     weights, total_ref = refs[:4], refs[4]
     own_ref, other_ref, hidden_ref, *outs = refs[5:]
-    far = [far_ref[z] for z in range(far_ref.shape[0])]
+    far = [ref[z] for ref in (lo_ref, hi_ref) for z in range(ref.shape[0])]
     total = products([far], [near_ref[xs - 1]], weights, total_ref[...])
     units = total.shape[1] // 2
     gate, up = total[:, :units], total[:, units:]
@@ -218,12 +218,13 @@
 
     left = ahead(own)
     right = behind(own)
-    opposite = across(own)
+    opposite_lo = across(own[: zs // 2])
     swap = [(0, 1), (1, 0)]
     gate_w, up_w, down_w, _ = lax.optimization_barrier((w_gate[0], w_up[0], w_down[0], own))
     gate_o = lax.ppermute(gate_w, "c", swap)
     up_o = lax.ppermute(up_w, "c", swap)
     down_o = lax.ppermute(down_w, "c", swap)
+    opposite_hi = ahead(left[zs // 2 :])
 
     smem = pl.BlockSpec(memory_space=pltpu.SMEM)
     vmem = pl.BlockSpec(memory_space=pltpu.VMEM)
@@ -252,9 +253,9 @@
         3 * flops,
         3 * nbytes,
         mib=MIB_TURN,
-        in_specs=[smem] + [vmem] * 8,
+        in_specs=[smem] + [vmem] * 9,
         name="turn",
-    )(near, opposite, *weights, total, down_w, down_o)
+    )(near, opposite_lo, opposite_hi, *weights, total, down_w, down_o)
 
     from_far = across(to_far)
     from_prev = ahead(to_next)

time: 168 us -> 172 us (1.024)
  the two profiles are of different devices: /device:TPU:6 before, /device:TPU:2 now
where the time goes in v5:
time: 172 us
  blocking collectives  86.8 us (50%)
  starting transfers between devices  36 us (21%)
  waiting for transfers between devices  29 us (17%)
  Pallas kernels  16.2 us (9%)
  local copies, waits for them, and re-layouts  3.4 us (2%)
    all_to_all x1, blocking collectives, block(): lax.all_to_all(messages.reshape(far, CHUNK, LANES), FAR, 0, 0, tiled=True)  52.2 us
    all_to_all x1, blocking collectives, block(): lax.all_to_all(leaving.reshape(far, CHUNK, LANES), FAR, 0, 0, tiled=True)  34.6 us
    ppermute x3, waiting for transfers between devices, ahead(): return lax.ppermute(v, 'x', forward)  24.8 us
    ppermute x3, starting transfers between devices, ahead(): return lax.ppermute(v, 'x', forward)  9.71 us
    ppermute x2, starting transfers between devices, across(): return lax.ppermute(v, 'x', [(i, (i + 2) % xs) for i in range(xs)])  7.66 us
    all_to_all x1, starting transfers between devices, block(): partial_logits = lax.all_to_all(logits, ('z', 'x'), 0, 0, tiled=True)  7.48 us
    pallas_call x2, Pallas kernels, gate_up(): call(lambda *refs: gate_up_kernel(places, *refs), sums, flops * len(place...  5.69 us
    ppermute x2, starting transfers between devices, behind(): return lax.ppermute(v, 'x', backward)  4.96 us
  transfers between devices with their start and end apart: 11, of which 4 were waited for; matrix products, arithmetic and copies ran while one was open for 1% of the time, Pallas kernels for 5%

profile of v5, /device:TPU:2, one launch (start us, length us, event | category | flops | bytes accessed | tf_op | source)
XLA Modules:
  0.0 171.7 jit_solution(7435237072272881208)
XLA Ops:
  0.0 2.0 %pack.1 = (bf16[8,12,24,128]{3,2,1,0:T(8,128)(2,1)}, f32[24,2,128]{2,1,0:T(2,128)}) custom-call(s32[2,32]{1,0:T(2,128)} %bitcast.23, bf16[32,256]{1,0:T(8,128)(2,1)} %tokens_ref.1, bf16[8,256]{1,0:T(8,128)(2,1)} %bitcast.26), custom_call_target="tpu_custom_call" | custom-call | flops 10000000 | bytes 1000000 | tf_op jit(solution)/shard_map/pack/pallas_call | solution.py:200
  2.0 52.2 %all_to_all.15 = bf16[96,24,128]{2,1,0:T(8,128)(2,1)S(1)} all-to-all(bf16[96,24,128]{2,1,0:T(8,128)(2,1)} %bitcast.25), channel_id=1, replica_groups=mesh['zh'=2,'yq'=4,'yp'=2,'c'=2,'z'=6,'x'=4] {'zh','yq','yp','z'}, dimensions={0} | all-to-all | bytes 1179648 | tf_op jit(solution)/shard_map/all_to_all | solution.py:212
  54.2 0.9 spread.1.refs_1_
  55.1 1.9 %collective-permute-start.3 = (bf16[6144,128]{1,0:T(8,128)(2,1)S(1)}, bf16[6144,128]{1,0:T(8,128)(2,1)}, u32[]{:S(2)}, u32[]{:S(2)}) collective-permute-start(bf16[6144,128]{1,0:T(8,128)(2,1)S(1)} %bitcast.9), channel_id=1, source_target_pairs={{0,24},{24,0},{1,25},{25,1},{2,26},{26,2},{3,27},{27,3},{4,28},{28... | collective-permute-start | bytes 4718600 | tf_op jit(solution)/shard_map/ppermute | solution.py:224
  57.1 2.4 %collective-permute-start.4 = (bf16[6144,128]{1,0:T(8,128)(2,1)}, bf16[6144,128]{1,0:T(8,128)(2,1)}, u32[]{:S(2)}, u32[]{:S(2)}) collective-permute-start(bf16[6144,128]{1,0:T(8,128)(2,1)} %bitcast.13), channel_id=1, source_target_pairs={{0,24},{24,0},{1,25},{25,1},{2,26},{26,2},{3,27},{27,3},{4,28},{28... | collective-permute-start | bytes 4718600 | tf_op jit(solution)/shard_map/ppermute | solution.py:225
  59.5 1.9 %collective-permute-start.6 = (bf16[128,6144]{1,0:T(8,128)(2,1)}, bf16[128,6144]{1,0:T(8,128)(2,1)}, u32[]{:S(2)}, u32[]{:S(2)}) collective-permute-start(bf16[128,6144]{1,0:T(8,128)(2,1)} %bitcast.17), channel_id=1, source_target_pairs={{0,24},{24,0},{1,25},{25,1},{2,26},{26,2},{3,27},{27,3},{4,28},{28... | collective-permute-start | bytes 4718600 | tf_op jit(solution)/shard_map/ppermute | solution.py:226
  61.4 3.4 %collective-permute-start.1 = (bf16[6,192,256]{2,1,0:T(8,128)(2,1)}, bf16[6,192,256]{2,1,0:T(8,128)(2,1)}, u32[]{:S(2)}, u32[]{:S(2)}) collective-permute-start(bf16[6,192,256]{2,1,0:T(8,128)(2,1)} %spread.1.refs_1_), channel_id=1, source_target_pairs={{0,1},{1,2},{2,3},{3,0},{4,5},{5,6},{6,7},{7,4},{8,9},{9,10},{10,1... | collective-permute-start | bytes 1769480 | tf_op jit(solution)/shard_map/ppermute | solution.py:192
  64.8 2.4 %collective-permute-start.5 = (bf16[6,192,256]{2,1,0:T(8,128)(2,1)}, bf16[6,192,256]{2,1,0:T(8,128)(2,1)}, u32[]{:S(2)}, u32[]{:S(2)}) collective-permute-start(bf16[6,192,256]{2,1,0:T(8,128)(2,1)} %spread.1.refs_1_), channel_id=1, source_target_pairs={{0,3},{1,0},{2,1},{3,2},{4,7},{5,4},{6,5},{7,6},{8,11},{9,8},{10,9... | collective-permute-start | bytes 1769480 | tf_op jit(solution)/shard_map/ppermute | solution.py:198
  67.3 1.0 slice.8
  68.3 11.1 %collective-permute-done.1.refs_2_ = bf16[6,192,256]{2,1,0:T(8,128)(2,1)} collective-permute-done((bf16[6,192,256]{2,1,0:T(8,128)(2,1)}, bf16[6,192,256]{2,1,0:T(8,128)(2,1)}, u32[]{:S(2)}, u32[]{:S(2)}) %collective-permute-start.1) | collective-permute-done | bytes 589856 | tf_op jit(solution)/shard_map/ppermute | solution.py:192
  79.3 4.0 %collective-permute-start = (bf16[3,192,256]{2,1,0:T(8,128)(2,1)S(1)}, bf16[3,192,256]{2,1,0:T(8,128)(2,1)S(1)}, u32[]{:S(2)}, u32[]{:S(2)}) collective-permute-start(bf16[3,192,256]{2,1,0:T(8,128)(2,1)S(1)} %slice.8), channel_id=1, source_target_pairs={{0,2},{1,3},{2,0},{3,1},{4,6},{5,7},{6,4},{7,5},{8,10},{9,11},{10,... | collective-permute-start | bytes 884744 | tf_op jit(solution)/shard_map/ppermute | solution.py:195
  83.4 1.0 slice.9
  84.4 3.0 %collective-permute-start.2 = (bf16[3,192,256]{2,1,0:T(8,128)(2,1)S(1)}, bf16[3,192,256]{2,1,0:T(8,128)(2,1)S(1)}, u32[]{:S(2)}, u32[]{:S(2)}) collective-permute-start(bf16[3,192,256]{2,1,0:T(8,128)(2,1)S(1)} %slice.9), channel_id=1, source_target_pairs={{0,1},{1,2},{2,3},{3,0},{4,5},{5,6},{6,7},{7,4},{8,9},{9,10},{10,1... | collective-permute-start | bytes 884744 | tf_op jit(solution)/shard_map/ppermute | solution.py:192
  87.4 2.5 %gate_up.2.refs_7_ = f32[192,512]{1,0:T(8,128)S(1)} custom-call(s32[4]{0:T(128)S(1)} %add_and_fusion.refs_0_, bf16[6,192,256]{2,1,0:T(8,128)(2,1)} %spread.1.refs_1_, bf16[6144,128]{1,0:T(8,128)(2,1)S(1)} %bitcast.10, bf16[6144,128]{1,0:T(8,128)(2,1)} %collective-permute-done.3.refs_3_.refs_4_, bf16[6144,128]{1,0:T(8,128)(2,1)S(1)} %bitcast.14, ...), custom_call_target="tpu_custom_call" | custom-call | flops 301989888 | bytes 2162688 | tf_op jit(solution)/shard_map/gate_up/pallas_call | solution.py:238
  90.0 0.0 copy-start.2
  90.0 0.0 collective-permute-done.5.refs_1_
  90.0 3.1 %gate_up.3.refs_7_ = f32[192,512]{1,0:T(8,128)S(1)} custom-call(s32[4]{0:T(128)S(1)} %add_and_fusion.refs_0_, bf16[6,192,256]{2,1,0:T(8,128)(2,1)} %collective-permute-done.5.refs_1_, bf16[6,192,256]{2,1,0:T(8,128)(2,1)} %collective-permute-done.1.refs_2_, bf16[6144,128]{1,0:T(8,128)(2,1)S(1)} %bitcast.11, ...), custom_call_target="tpu_custom_call" | custom-call | flops 603979776 | bytes 4325376 | tf_op jit(solution)/shard_map/gate_up/pallas_call | solution.py:238
  93.2 4.5 %collective-permute-done.2.refs_2_ = bf16[3,192,256]{2,1,0:T(8,128)(2,1)S(1)} collective-permute-done((bf16[3,192,256]{2,1,0:T(8,128)(2,1)S(1)}, bf16[3,192,256]{2,1,0:T(8,128)(2,1)S(1)}, u32[]{:S(2)}, u32[]{:S(2)}) %collective-permute-start.2) | collective-permute-done | bytes 294944 | tf_op jit(solution)/shard_map/ppermute | solution.py:192
  97.7 4.4 %turn.1 = (bf16[192,256]{1,0:T(8,128)(2,1)S(1)}, bf16[6,192,256]{2,1,0:T(8,128)(2,1)}, bf16[6,192,256]{2,1,0:T(8,128)(2,1)}, bf16[6,192,256]{2,1,0:T(8,128)(2,1)}) custom-call(s32[4]{0:T(128)S(1)} %add_and_fusion.refs_0_, bf16[3,192,256]{2,1,0:T(8,128)(2,1)S(1)} %collective-permute-done.refs_1_, bf16[3,192,256]{2,1,0:T(8,128)(2,1)S(1)} %collective-permute-done.2.refs_2_, ...), custom_call_target="tpu_custom_call" | custom-call | flops 905969664 | bytes 6488064 | tf_op jit(solution)/shard_map/turn/pallas_call | solution.py:250
  102.1 3.3 %collective-permute-start.7 = (bf16[6,192,256]{2,1,0:T(8,128)(2,1)}, bf16[6,192,256]{2,1,0:T(8,128)(2,1)S(1)}, u32[]{:S(2)}, u32[]{:S(2)}) collective-permute-start(bf16[6,192,256]{2,1,0:T(8,128)(2,1)} %get-tuple-element.20), channel_id=1, source_target_pairs={{0,1},{1,2},{2,3},{3,0},{4,5},{5,6},{6,7},{7,4},{8,9},{9,10},{10,1... | collective-permute-start | bytes 1769480 | tf_op jit(solution)/shard_map/ppermute | solution.py:192
  105.4 2.5 %collective-permute-start.8 = (bf16[6,192,256]{2,1,0:T(8,128)(2,1)}, bf16[6,192,256]{2,1,0:T(8,128)(2,1)S(1)}, u32[]{:S(2)}, u32[]{:S(2)}) collective-permute-start(bf16[6,192,256]{2,1,0:T(8,128)(2,1)} %get-tuple-element.21), channel_id=1, source_target_pairs={{0,3},{1,0},{2,1},{3,2},{4,7},{5,4},{6,5},{7,6},{8,11},{9,8},{10,9... | collective-permute-start | bytes 1769480 | tf_op jit(solution)/shard_map/ppermute | solution.py:198
  107.9 3.6 %collective-permute-start.9 = (bf16[6,192,256]{2,1,0:T(8,128)(2,1)}, bf16[6,192,256]{2,1,0:T(8,128)(2,1)S(1)}, u32[]{:S(2)}, u32[]{:S(2)}) collective-permute-start(bf16[6,192,256]{2,1,0:T(8,128)(2,1)} %get-tuple-element.22), channel_id=1, source_target_pairs={{0,2},{1,3},{2,0},{3,1},{4,6},{5,7},{6,4},{7,5},{8,10},{9,11},{10,... | collective-permute-start | bytes 1769480 | tf_op jit(solution)/shard_map/ppermute | solution.py:195
  111.6 7.5 %all-to-all-start = ((f32[24,2,128]{2,1,0:T(2,128)}), f32[24,2,128]{2,1,0:T(2,128)S(1)}, u32[]{:S(2)}, u32[]{:S(2)}) async-start(f32[24,2,128]{2,1,0:T(2,128)} %get-tuple-element.14), calls=%async_computation | async-start | bytes 49152 | tf_op jit(solution)/shard_map/all_to_all | solution.py:211
  119.1 0.0 copy-start.3
  119.1 1.4 copy-done.3
  120.5 1.8 %down.1.refs_0_ = bf16[6,192,256]{2,1,0:T(8,128)(2,1)S(1)} custom-call(s32[4]{0:T(128)S(1)} %add_and_fusion.refs_0_, bf16[192,256]{1,0:T(8,128)(2,1)S(1)} %get-tuple-element.19.refs_1_, bf16[128,6144]{1,0:T(8,128)(2,1)S(1)} %bitcast.19, bf16[128,6144]{1,0:T(8,128)(2,1)} %collective-permute-done.6.refs_9_.refs_3_), custom_call_target="tpu_custom_call" | custom-call | flops 150994944 | bytes 1081344 | tf_op jit(solution)/shard_map/down/pallas_call | solution.py:263
  122.2 0.0 copy-start.4
  122.3 9.2 %collective-permute-done.7.refs_1_ = bf16[6,192,256]{2,1,0:T(8,128)(2,1)S(1)} collective-permute-done((bf16[6,192,256]{2,1,0:T(8,128)(2,1)}, bf16[6,192,256]{2,1,0:T(8,128)(2,1)S(1)}, u32[]{:S(2)}, u32[]{:S(2)}) %collective-permute-start.7) | collective-permute-done | bytes 589856 | tf_op jit(solution)/shard_map/ppermute | solution.py:192
  131.4 4.3 %collective-permute-done.9.refs_3_ = bf16[6,192,256]{2,1,0:T(8,128)(2,1)S(1)} collective-permute-done((bf16[6,192,256]{2,1,0:T(8,128)(2,1)}, bf16[6,192,256]{2,1,0:T(8,128)(2,1)S(1)}, u32[]{:S(2)}, u32[]{:S(2)}) %collective-permute-start.9) | collective-permute-done | bytes 589856 | tf_op jit(solution)/shard_map/ppermute | solution.py:195
  135.7 0.3 unspread.1
  136.0 34.6 %all_to_all.16 = bf16[96,24,128]{2,1,0:T(8,128)(2,1)S(1)} all-to-all(bf16[96,24,128]{2,1,0:T(8,128)(2,1)S(1)} %bitcast.22), channel_id=1, replica_groups=mesh['zh'=2,'yq'=4,'yp'=2,'c'=2,'z'=6,'x'=4] {'zh','yq','yp','z'}, dimensions={0} | all-to-all | bytes 1179648 | tf_op jit(solution)/shard_map/all_to_all | solution.py:280
  170.6 1.1 merge.1
  (15 shorter events, 0.0 us)
Async XLA Ops:
  0.0 55.1 %copy-start = (bf16[1,6144,128]{2,1,0:T(8,128)(2,1)S(1)}, bf16[1,6144,128]{2,1,0:T(8,128)(2,1)}, u32[]{:S(2)}) copy-start(bf16[1,6144,128]{2,1,0:T(8,128)(2,1)} %param.10) | copy-start | bytes 4718596
  2.0 85.4 %copy-start.5 = (s32[4]{0:T(128)S(1)}, s32[4]{0:T(128)}, u32[]{:S(2)}) copy-start(s32[4]{0:T(128)} %constant.8.clone) | copy-start | bytes 52
  2.0 85.4 %copy-start.1 = (bf16[1,6144,128]{2,1,0:T(8,128)(2,1)S(1)}, bf16[1,6144,128]{2,1,0:T(8,128)(2,1)}, u32[]{:S(2)}) copy-start(bf16[1,6144,128]{2,1,0:T(8,128)(2,1)} %param.11) | copy-start | bytes 4718596
  55.1 29.2 %collective-permute-start.3 = (bf16[6144,128]{1,0:T(8,128)(2,1)S(1)}, bf16[6144,128]{1,0:T(8,128)(2,1)}, u32[]{:S(2)}, u32[]{:S(2)}) collective-permute-start(bf16[6144,128]{1,0:T(8,128)(2,1)S(1)} %bitcast.9), channel_id=1, source_target_pairs={{0,24},{24,0},{1,25},{25,1},{2,26},{26,2},{3,27},{27,3},{4,28},{28... | collective-permute-start | bytes 4718600 | tf_op jit(solution)/shard_map/ppermute | solution.py:224
  57.1 30.3 %collective-permute-start.4 = (bf16[6144,128]{1,0:T(8,128)(2,1)}, bf16[6144,128]{1,0:T(8,128)(2,1)}, u32[]{:S(2)}, u32[]{:S(2)}) collective-permute-start(bf16[6144,128]{1,0:T(8,128)(2,1)} %bitcast.13), channel_id=1, source_target_pairs={{0,24},{24,0},{1,25},{25,1},{2,26},{26,2},{3,27},{27,3},{4,28},{28... | collective-permute-start | bytes 4718600 | tf_op jit(solution)/shard_map/ppermute | solution.py:225
  59.5 38.2 %collective-permute-start.6 = (bf16[128,6144]{1,0:T(8,128)(2,1)}, bf16[128,6144]{1,0:T(8,128)(2,1)}, u32[]{:S(2)}, u32[]{:S(2)}) collective-permute-start(bf16[128,6144]{1,0:T(8,128)(2,1)} %bitcast.17), channel_id=1, source_target_pairs={{0,24},{24,0},{1,25},{25,1},{2,26},{26,2},{3,27},{27,3},{4,28},{28... | collective-permute-start | bytes 4718600 | tf_op jit(solution)/shard_map/ppermute | solution.py:226
  61.4 17.9 %collective-permute-start.1 = (bf16[6,192,256]{2,1,0:T(8,128)(2,1)}, bf16[6,192,256]{2,1,0:T(8,128)(2,1)}, u32[]{:S(2)}, u32[]{:S(2)}) collective-permute-start(bf16[6,192,256]{2,1,0:T(8,128)(2,1)} %spread.1.refs_1_), channel_id=1, source_target_pairs={{0,1},{1,2},{2,3},{3,0},{4,5},{5,6},{6,7},{7,4},{8,9},{9,10},{10,1... | collective-permute-start | bytes 1769480 | tf_op jit(solution)/shard_map/ppermute | solution.py:192
  64.8 25.2 %collective-permute-start.5 = (bf16[6,192,256]{2,1,0:T(8,128)(2,1)}, bf16[6,192,256]{2,1,0:T(8,128)(2,1)}, u32[]{:S(2)}, u32[]{:S(2)}) collective-permute-start(bf16[6,192,256]{2,1,0:T(8,128)(2,1)} %spread.1.refs_1_), channel_id=1, source_target_pairs={{0,3},{1,0},{2,1},{3,2},{4,7},{5,4},{6,5},{7,6},{8,11},{9,8},{10,9... | collective-permute-start | bytes 1769480 | tf_op jit(solution)/shard_map/ppermute | solution.py:198
  79.3 13.8 %collective-permute-start = (bf16[3,192,256]{2,1,0:T(8,128)(2,1)S(1)}, bf16[3,192,256]{2,1,0:T(8,128)(2,1)S(1)}, u32[]{:S(2)}, u32[]{:S(2)}) collective-permute-start(bf16[3,192,256]{2,1,0:T(8,128)(2,1)S(1)} %slice.8), channel_id=1, source_target_pairs={{0,2},{1,3},{2,0},{3,1},{4,6},{5,7},{6,4},{7,5},{8,10},{9,11},{10,... | collective-permute-start | bytes 884744 | tf_op jit(solution)/shard_map/ppermute | solution.py:195
  84.4 13.3 %collective-permute-start.2 = (bf16[3,192,256]{2,1,0:T(8,128)(2,1)S(1)}, bf16[3,192,256]{2,1,0:T(8,128)(2,1)S(1)}, u32[]{:S(2)}, u32[]{:S(2)}) collective-permute-start(bf16[3,192,256]{2,1,0:T(8,128)(2,1)S(1)} %slice.9), channel_id=1, source_target_pairs={{0,1},{1,2},{2,3},{3,0},{4,5},{5,6},{6,7},{7,4},{8,9},{9,10},{10,1... | collective-permute-start | bytes 884744 | tf_op jit(solution)/shard_map/ppermute | solution.py:192
  90.0 7.7 %copy-start.2 = (bf16[1,128,6144]{2,1,0:T(8,128)(2,1)S(1)}, bf16[1,128,6144]{2,1,0:T(8,128)(2,1)}, u32[]{:S(2)}) copy-start(bf16[1,128,6144]{2,1,0:T(8,128)(2,1)} %param.12) | copy-start | bytes 4718596
  102.1 29.3 %collective-permute-start.7 = (bf16[6,192,256]{2,1,0:T(8,128)(2,1)}, bf16[6,192,256]{2,1,0:T(8,128)(2,1)S(1)}, u32[]{:S(2)}, u32[]{:S(2)}) collective-permute-start(bf16[6,192,256]{2,1,0:T(8,128)(2,1)} %get-tuple-element.20), channel_id=1, source_target_pairs={{0,1},{1,2},{2,3},{3,0},{4,5},{5,6},{6,7},{7,4},{8,9},{9,10},{10,1... | collective-permute-start | bytes 1769480 | tf_op jit(solution)/shard_map/ppermute | solution.py:192
  105.4 26.0 %collective-permute-start.8 = (bf16[6,192,256]{2,1,0:T(8,128)(2,1)}, bf16[6,192,256]{2,1,0:T(8,128)(2,1)S(1)}, u32[]{:S(2)}, u32[]{:S(2)}) collective-permute-start(bf16[6,192,256]{2,1,0:T(8,128)(2,1)} %get-tuple-element.21), channel_id=1, source_target_pairs={{0,3},{1,0},{2,1},{3,2},{4,7},{5,4},{6,5},{7,6},{8,11},{9,8},{10,9... | collective-permute-start | bytes 1769480 | tf_op jit(solution)/shard_map/ppermute | solution.py:198
  107.9 27.7 %collective-permute-start.9 = (bf16[6,192,256]{2,1,0:T(8,128)(2,1)}, bf16[6,192,256]{2,1,0:T(8,128)(2,1)S(1)}, u32[]{:S(2)}, u32[]{:S(2)}) collective-permute-start(bf16[6,192,256]{2,1,0:T(8,128)(2,1)} %get-tuple-element.22), channel_id=1, source_target_pairs={{0,2},{1,3},{2,0},{3,1},{4,6},{5,7},{6,4},{7,5},{8,10},{9,11},{10,... | collective-permute-start | bytes 1769480 | tf_op jit(solution)/shard_map/ppermute | solution.py:195
  111.6 24.4 %all-to-all-start = ((f32[24,2,128]{2,1,0:T(2,128)}), f32[24,2,128]{2,1,0:T(2,128)S(1)}, u32[]{:S(2)}, u32[]{:S(2)}) async-start(f32[24,2,128]{2,1,0:T(2,128)} %get-tuple-element.14), calls=%async_computation | async-start | bytes 49152 | tf_op jit(solution)/shard_map/all_to_all | solution.py:211
  119.1 1.4 copy-start.3
  122.2 48.3 %copy-start.4 = (s32[32,2]{0,1:T(2,128)S(1)}, s32[32,2]{0,1:T(2,128)}, u32[]{:S(2)}) copy-start(s32[32,2]{0,1:T(2,128)} %param.9) | copy-start | bytes 772
